TPU v7x, 256 devices: a whole 4x4x8 slice. The times are simulated.
256 devices in a mesh: seq: 16 (over y_hi, z), head: 16 (over y_lo, x, core).
Axes of the slice: x: 4, y: 4 (y_hi: 2, y_lo: 2; y = y_hi * 2 + y_lo), z: 8, core: 2. Of those that a mesh axis runs over, the one named last changes fastest.
Arguments:
- queries: bfloat16 [16384, 4096], P(('seq', 'head')), may hold values from -9 to 9, as said below
- keys: bfloat16 [16384, 512], P(('seq', 'head')), may hold values from -9 to 9, as said below
- values: bfloat16 [16384, 512], P(('seq', 'head')), may hold values from -6 to 6
Outputs:
- attended: bfloat16 [16384, 4096], P(('seq', 'head'))
Inputs may be any that keep to these rules, and one draw needn't show every extreme that they name: `queries`: query entries are of order one except on a few rows. `keys`: key entries are of order one except on a few rows.
All inputs are finite; a program needn't handle non-finite values.
Results may differ from a plain program's by a relative error of at most 0.005.
Values may be sent and summed in bfloat16 or wider, within the bound.
No kernel may reach another device: no remote copies, remote signals or barrier semaphores. Data moves between devices by JAX's collectives and lax.ppermute only.
A program may use at most 64 MiB of HBM per device.

v0:
```python
import functools
import math

import jax
import jax.numpy as jnp
from jax import lax
from jax.experimental import pallas as pl
from jax.experimental.pallas import tpu as pltpu
from jax.sharding import Mesh, PartitionSpec as P


H = 32
KV = 4
DH = 128
STRIP = 64
C2 = math.log2(math.e) / math.sqrt(DH)
NEG = -1e30
ROW_M, ROW_L, ROW_Q, ROW_W = (slice(DH + i, DH + i + 1) for i in range(4))
HALF = 1040
AXES = ("yh", "z", "yl", "x", "c")
VMEM = pl.BlockSpec(memory_space=pltpu.VMEM)
SMEM = pl.BlockSpec(memory_space=pltpu.SMEM)


def prep_kernel(kv_ref, out_ref):
    for half in range(2):
        base = half * HALF
        norm = jnp.zeros((1, 1), jnp.float32)
        for s in range(8):
            k = kv_ref[half * 8 + s, :64, :]
            out_ref[base + s * 64 : base + (s + 1) * 64, :] = k
            kf = k.astype(jnp.float32)
            norm = jnp.maximum(norm, jnp.max(jnp.sum(kf * kf, axis=1, keepdims=True), axis=0, keepdims=True))
        for b in range(4):
            src = half * 8 + 2 * b
            block = jnp.concatenate([kv_ref[src, 64:, :], kv_ref[src + 1, 64:, :]], axis=0)
            at = base + 512 + b * 128
            out_ref[at : at + 128, :] = block.astype(jnp.float32).T.astype(jnp.bfloat16)
        bound = jnp.broadcast_to(jnp.sqrt(norm) * 1.01, (16, DH)).astype(jnp.bfloat16)
        out_ref[base + 1024 : base + HALF, :] = bound


def prep(kv):
    return pl.pallas_call(
        prep_kernel,
        out_shape=jax.ShapeDtypeStruct((2 * HALF, DH), jnp.bfloat16),
        in_specs=[VMEM],
        out_specs=VMEM,
        name="prep",
        compiler_params=pltpu.CompilerParams(vmem_limit_bytes=8 * 1024 * 1024),
        cost_estimate=pl.CostEstimate(flops=1000000, bytes_accessed=1000000, transcendentals=0),
    )(kv)


def rows_of(q_ref, y, t, hq):
    x = q_ref[jnp.bitwise_and(y - t + 4, 3), :, pl.ds(pl.multiple_of(hq * 4 * DH, DH), 4 * DH)]
    return jnp.concatenate([x[:, i * DH : (i + 1) * DH] for i in range(4)], axis=0)


def qk(k_blk, rows):
    return lax.dot_general(k_blk, rows, (((1,), (1,)), ((), ())), preferred_element_type=jnp.float32)


def finish_piece(st_ref, t, hq, vt_blk, s, m_new, mask):
    m_old = st_ref[t, hq, ROW_M, :]
    l_old = st_ref[t, hq, ROW_L, :]
    p = jnp.exp2(s * C2 - m_new)
    if mask is not None:
        p = jnp.where(mask, p, 0.0)
    alpha = jnp.exp2(m_old - m_new)
    pv = lax.dot_general(
        vt_blk, p.astype(jnp.bfloat16), (((1,), (0,)), ((), ())), preferred_element_type=jnp.float32
    )
    st_ref[t, hq, ROW_M, :] = m_new
    st_ref[t, hq, ROW_L, :] = alpha * l_old + jnp.sum(p, axis=0, keepdims=True)
    st_ref[t, hq, 0:DH, :] = alpha * st_ref[t, hq, 0:DH, :] + pv


def unit(refs, ch_ref, half, tp, fast, masks=None):
    q_refs, st_refs, y = refs
    base = pl.multiple_of(half * HALF, 16)
    k_blk = ch_ref[pl.ds(base, 512), :]
    vt_blk = jnp.concatenate([ch_ref[pl.ds(base + 512 + b * 128, 128), :] for b in range(4)], axis=1)
    kn = ch_ref[pl.ds(base + 1024, 16), :].astype(jnp.float32)[0:1, :]
    kn = jnp.concatenate([kn, kn], axis=1)

    def mask_of(w, i):
        return (None, None) if masks is None else masks(w, i)

    if fast:
        todo = [(w, i, hq) for i in range(2) for w in range(2) for hq in range(2)]
        ahead = 2
        scores = [qk(k_blk, rows_of(q_refs[w], y, 2 * tp + i, hq)) for w, i, hq in todo[:ahead]]
        for n, (w, i, hq) in enumerate(todo):
            if n + ahead < len(todo):
                w2, i2, hq2 = todo[n + ahead]
                scores.append(qk(k_blk, rows_of(q_refs[w2], y, 2 * tp + i2, hq2)))
            t = 2 * tp + i
            mask, some = mask_of(w, i)
            bound = st_refs[w][t, hq, ROW_Q, :] * kn
            if some is not None:
                bound = jnp.where(some, bound, NEG)
            m_new = jnp.maximum(st_refs[w][t, hq, ROW_M, :], bound)
            finish_piece(st_refs[w], t, hq, vt_blk, scores[n], m_new, mask)
        return
    for w in range(2):

        def body(n, carry, w=w):
            i, hq = n // 2, n % 2
            t = 2 * tp + i
            mask, _ = mask_of(w, i)
            s = qk(k_blk, rows_of(q_refs[w], y, t, hq))
            if mask is not None:
                s = jnp.where(mask, s, NEG)
            top = jnp.maximum(jnp.max(s, axis=0, keepdims=True) * C2, NEG)
            m_new = jnp.maximum(st_refs[w][t, hq, ROW_M, :], top)
            finish_piece(st_refs[w], t, hq, vt_blk, s, m_new, mask)
            return carry

        lax.fori_loop(0, 4, body, 0)


def both_ways(fast, run):
    @pl.when(fast)
    def _():
        run(True)

    @pl.when(jnp.logical_not(fast))
    def _():
        run(False)


def is_fast(st_ref, chunks):
    kn = functools.reduce(
        jnp.maximum,
        [ch[h * HALF + 1024 : h * HALF + 1040, :].astype(jnp.float32) for ch, halves in chunks for h in range(halves)],
    )
    return jnp.max(kn[0:1, :] * st_ref[0, 0, ROW_W, 0:DH]) <= 60.0


def own_kernel(sc_ref, q0, q1, ch_ref, st0, st1):
    y, x, c = sc_ref[0], sc_ref[1], sc_ref[2]
    refs = ((q0, q1), (st0, st1), y)
    ones = jnp.ones((16, DH), jnp.bfloat16)
    widest = jnp.zeros((1, 256), jnp.float32)
    for q_ref, st_ref in ((q0, st0), (q1, st1)):
        st_ref[:, :, :DH, :] = jnp.zeros((4, 2, DH, 256), jnp.float32)
        for t in range(4):
            for hq in range(2):
                r = rows_of(q_ref, y, t, hq).astype(jnp.float32)
                n2 = qk(ones, (r * r).astype(jnp.bfloat16))[0:1, :]
                qn = jnp.sqrt(n2) * (1.02 * C2)
                widest = jnp.maximum(widest, qn)
                st_ref[t, hq, ROW_M, :] = jnp.full((1, 256), NEG, jnp.float32)
                st_ref[t, hq, ROW_L, :] = jnp.zeros((1, 256), jnp.float32)
                st_ref[t, hq, ROW_Q, :] = qn
    st0[0, 0, ROW_W, :] = jnp.broadcast_to(jnp.max(widest, axis=1, keepdims=True), (1, 256))

    row = lax.broadcasted_iota(jnp.int32, (1, 256), 1) % STRIP
    key = lax.broadcasted_iota(jnp.int32, (512, 1), 0)
    key_pos = (key // 256) * 512 + ((key % 256) // STRIP) * 128 + c * STRIP + key % STRIP

    def masks(w, i):
        row_pos = i * 512 + x * 128 + (c if w == 0 else 1 - c) * STRIP + row
        return key_pos <= row_pos, c * STRIP <= row_pos

    def run(fast):
        def diagonal(h, carry):
            unit(refs, ch_ref, h, h, fast, masks)
            return carry

        lax.fori_loop(0, 2, diagonal, 0)
        unit(refs, ch_ref, 0, 1, fast)

    both_ways(is_fast(st0, [(ch_ref, 2)]), run)


def step_kernel(parts, sc_ref, q0, q1, *refs):
    n = len(parts)
    chunks, refs = refs[:n], ((q0, q1), refs[n + 2 : n + 4], sc_ref[0])

    def run(fast):
        for ch_ref, (halves, at) in zip(chunks, parts):
            before = sc_ref[at]

            def body(u, carry, ch_ref=ch_ref, halves=halves):
                if halves == (0, 1):
                    half, tp = jnp.where(u == 1, 1, 0), jnp.where(u == 2, 0, 1)
                elif halves == (0,):
                    half, tp = 0, 1 - u
                else:
                    half, tp = 0, 1
                unit(refs, ch_ref, half, tp, fast)
                return carry

            count = {(0, 1): 1 + 2 * before, (0,): 1 + before, (1,): before}[halves]
            lax.fori_loop(0, count, body, 0)

    both_ways(is_fast(refs[1][0], [(ch, len(p[0])) for ch, p in zip(chunks, parts)]), run)


ST = (jax.ShapeDtypeStruct((4, 2, DH + 8, 256), jnp.float32),) * 2


def cost(units):
    work = units * 8 * 512 * 256
    return pl.CostEstimate(flops=4 * work * DH, bytes_accessed=6000000, transcendentals=work)


def small(kernel, out_shape, n_in, scalars=True):
    outs = jax.tree.map(lambda _: VMEM, out_shape)
    return pl.pallas_call(
        kernel,
        out_shape=out_shape,
        in_specs=[SMEM] * scalars + [VMEM] * n_in,
        out_specs=outs,
        compiler_params=pltpu.CompilerParams(vmem_limit_bytes=12 * 1024 * 1024),
        cost_estimate=pl.CostEstimate(flops=1000000, bytes_accessed=1000000, transcendentals=0),
    )


def own_step(sc, q0, q1, chunk):
    return pl.pallas_call(
        own_kernel,
        out_shape=ST,
        in_specs=[SMEM, VMEM, VMEM, VMEM],
        out_specs=(VMEM,) * 2,
        name="own",
        compiler_params=pltpu.CompilerParams(vmem_limit_bytes=24 * 1024 * 1024),
        cost_estimate=cost(6),
    )(sc, q0, q1, chunk)


def ring_step(sc, q0, q1, state, chunks, parts):
    n = len(chunks)
    return pl.pallas_call(
        functools.partial(step_kernel, parts),
        out_shape=ST,
        in_specs=[SMEM, VMEM, VMEM] + [VMEM] * (n + 2),
        out_specs=(VMEM,) * 2,
        input_output_aliases={3 + n + i: i for i in range(2)},
        name="ring",
        compiler_params=pltpu.CompilerParams(vmem_limit_bytes=24 * 1024 * 1024),
        cost_estimate=cost(8),
    )(sc, q0, q1, *chunks, *state)


def kv_send_kernel(k_ref, v_ref, out_ref):
    for g in range(KV):
        k, v = k_ref[:, g * DH : (g + 1) * DH], v_ref[:, g * DH : (g + 1) * DH]
        for i in range(4):
            out_ref[g * 4 + i, :STRIP, :] = k
            out_ref[g * 4 + i, STRIP:, :] = v


def q_send_kernel(sc_ref, q_ref, *outs):
    for d in range(4):
        to = jnp.bitwise_and(sc_ref[0] + d, 3)
        outs[d][...] = q_ref[:, pl.ds(pl.multiple_of(to * 8 * DH, 8 * DH), 8 * DH)]


def merge_kernel(sc_ref, s_ref, r_ref, *outs):
    for d in range(4):
        t = jnp.bitwise_and(sc_ref[0] + d, 3)
        for hq in range(2):
            m0, l0 = s_ref[t, hq, ROW_M, :], s_ref[t, hq, ROW_L, :]
            m1, l1 = r_ref[t, hq, ROW_M, :], r_ref[t, hq, ROW_L, :]
            m = jnp.maximum(m0, m1)
            f0, f1 = jnp.exp2(m0 - m), jnp.exp2(m1 - m)
            inv = 1.0 / (f0 * l0 + f1 * l1)
            out = (f0 * inv) * s_ref[t, hq, :DH, :] + (f1 * inv) * r_ref[t, hq, :DH, :]
            rows = out.T.astype(jnp.bfloat16)
            for i in range(4):
                at = (hq * 4 + i) * DH
                outs[d][:, at : at + DH] = rows[i * STRIP : (i + 1) * STRIP, :]


def place_kernel(sc_ref, *refs):
    for d in range(4):
        at = jnp.bitwise_and(sc_ref[0] - d + 4, 3)
        refs[4][:, pl.ds(pl.multiple_of(at * 8 * DH, 8 * DH), 8 * DH)] = refs[d][...]


def per_device(queries, keys, values):
    y = lax.axis_index(("yh", "yl"))
    z, x, c = lax.axis_index("z"), lax.axis_index("x"), lax.axis_index("c")
    nz, ny = lax.axis_size("z"), 4
    swap = [(0, 1), (1, 0)]
    up = [(i, (i + 1) % nz) for i in range(nz)]
    down = [(i, (i - 1) % nz) for i in range(nz)]
    flags = [(z - k >= 0).astype(jnp.int32) for k in range(1, 5)]
    wraps = [(z + k >= nz).astype(jnp.int32) for k in range(1, 5)]
    sc = jnp.stack([y, x, c, *flags, *wraps]).astype(jnp.int32)

    def regroup(pieces):
        moved = []
        for d in range(1, ny):
            moved.append(lax.ppermute(pieces[d], ("yh", "yl"), [(i, (i + d) % ny) for i in range(ny)]))
        return [pieces[0], *moved]

    bf16 = jnp.bfloat16
    piece = jax.ShapeDtypeStruct((STRIP, 8 * DH), bf16)
    sent = jax.ShapeDtypeStruct((16, 2 * STRIP, DH), bf16)
    kv = small(kv_send_kernel, sent, 2, False)(keys, values)
    kv = lax.all_to_all(kv, ("yh", "yl", "x"), split_axis=0, concat_axis=0, tiled=True)
    q0 = jnp.stack(regroup(small(q_send_kernel, (piece,) * 4, 1)(sc, queries)))
    q1 = lax.ppermute(q0, "c", swap)
    chunk = prep(kv)

    fwd, bwd = [chunk], [chunk]
    for _ in range(1, 4):
        fwd.append(lax.ppermute(fwd[-1], "z", up))
        bwd.append(lax.ppermute(bwd[-1], "z", down))
    far_l = lax.ppermute(fwd[3][:HALF], "z", up)
    far_h = lax.ppermute(bwd[3][HALF:], "z", down)

    state = own_step(sc, q0, q1, chunk)
    for k in range(1, 4):
        parts = (((0, 1), 2 + k), ((0, 1), 6 + k))
        state = ring_step(sc, q0, q1, state, (fwd[k], bwd[k]), parts)
    state = ring_step(sc, q0, q1, state, (far_l, far_h), (((0,), 6), ((1,), 6)))
    other = lax.ppermute(state[1], "c", swap)
    pieces = small(merge_kernel, (piece,) * 4, 2)(sc, state[0], other)
    out = jax.ShapeDtypeStruct((STRIP, H * DH), bf16)
    return small(place_kernel, out, 4)(sc, *regroup(pieces))


def solution(mesh):
    fine = Mesh(mesh.devices.reshape(2, 8, 2, 4, 2), AXES)
    return jax.shard_map(
        per_device,
        mesh=fine,
        in_specs=(P(AXES, None),) * 3,
        out_specs=P(AXES, None),
        check_vma=False,
    )
```

profile of v0, /device:TPU:240, one launch (start us, length us, event | category | flops | bytes accessed | tf_op | source)
XLA Modules:
  0.0 154.6 jit_solution(12337332121248082086)
XLA Ops:
  0.0 0.0 copy-start.1
  0.0 0.8 copy-done.1
  0.8 0.0 copy-start.2
  0.8 0.8 copy-done.2
  1.7 0.0 copy-start
  1.7 0.9 shard_map.38
  2.5 7.3 %all-to-all-start = ((bf16[16,128,128]{2,1,0:T(8,128)(2,1)}), bf16[16,128,128]{2,1,0:T(8,128)(2,1)S(1)}, u32[]{:S(2)}, u32[]{:S(2)}) async-start(bf16[16,128,128]{2,1,0:T(8,128)(2,1)} %shard_map.38), calls=%async_computation | async-start | bytes 1048576 | tf_op jit(solution)/shard_map/all_to_all | solution.py:305
  9.8 0.1 stack.94.sc_ref
  9.9 0.0 copy-done
  9.9 0.6 shard_map.37
  10.5 1.2 collective-permute-start
  11.8 0.9 collective-permute-start.1
  12.6 0.7 collective-permute-start.2
  13.3 5.5 %all-to-all-done.kv_ref = bf16[16,128,128]{2,1,0:T(8,128)(2,1)S(1)} async-done(((bf16[16,128,128]{2,1,0:T(8,128)(2,1)}), bf16[16,128,128]{2,1,0:T(8,128)(2,1)S(1)}, u32[]{:S(2)}, u32[]{:S(2)}) %all-to-all-start) | async-done | bytes 524320 | tf_op jit(solution)/shard_map/all_to_all | solution.py:305
  18.9 0.3 prep.1.ch_ref
  19.2 1.1 collective-permute-start.8
  20.3 2.2 %collective-permute-start.4 = (bf16[2080,128]{1,0:T(8,128)(2,1)S(1)}, bf16[2080,128]{1,0:T(8,128)(2,1)S(1)}, u32[]{:S(2)}, u32[]{:S(2)}) collective-permute-start(bf16[2080,128]{1,0:T(8,128)(2,1)S(1)} %prep.1.ch_ref), channel_id=1, source_target_pairs={{0,16},{16,32},{32,48},{48,64},{64,80},{80,96},{96,112},{112,0},{1... | collective-permute-start | bytes 1597448 | tf_op jit(solution)/shard_map/ppermute | solution.py:312
  22.5 0.0 collective-permute-done
  22.5 0.0 collective-permute-done.1
  22.5 1.1 collective-permute-done.2
  23.6 0.1 pad_maximum_fusion.q0
  23.6 0.1 collective-permute-start.3
  23.7 9.7 %collective-permute-done.8.refs_1_ = bf16[2080,128]{1,0:T(8,128)(2,1)S(1)} collective-permute-done((bf16[2080,128]{1,0:T(8,128)(2,1)S(1)}, bf16[2080,128]{1,0:T(8,128)(2,1)S(1)}, u32[]{:S(2)}, u32[]{:S(2)}) %collective-permute-start.8) | collective-permute-done | bytes 532512 | tf_op jit(solution)/shard_map/ppermute | solution.py:313
  33.4 0.0 collective-permute-start.9
  33.4 0.0 collective-permute-done.4.refs_0_
  33.4 3.2 %collective-permute-start.5 = (bf16[2080,128]{1,0:T(8,128)(2,1)S(1)}, bf16[2080,128]{1,0:T(8,128)(2,1)S(1)}, u32[]{:S(2)}, u32[]{:S(2)}) collective-permute-start(bf16[2080,128]{1,0:T(8,128)(2,1)S(1)} %collective-permute-done.4.refs_0_), channel_id=1, source_target_pairs={{0,16},{16,32},{32,48},{48,64},{64,80},{80,96},{96,112},{112,0},{1... | collective-permute-start | bytes 1597448 | tf_op jit(solution)/shard_map/ppermute | solution.py:312
  36.7 0.0 collective-permute-done.3.q1
  36.7 5.5 %own.1 = (f32[4,2,136,256]{3,2,1,0:T(8,128)S(1)}, f32[4,2,136,256]{3,2,1,0:T(8,128)S(1)}) custom-call(s32[11]{0:T(128)S(1)} %stack.94.sc_ref, bf16[4,64,1024]{2,1,0:T(8,128)(2,1)S(1)} %pad_maximum_fusion.q0, bf16[4,64,1024]{2,1,0:T(8,128)(2,1)S(1)} %collective-permute-done.3.q1, bf16[2080,128]{1,0:T(8,128)(2,1)S(1)} %prep.1.ch_ref), custom_call_target="tpu_custom_call" | custom-call | flops 3221225472 | bytes 6000000 | tf_op jit(solution)/shard_map/own/pallas_call | solution.py:223
  42.2 4.5 %collective-permute-done.9.refs_1_ = bf16[2080,128]{1,0:T(8,128)(2,1)S(1)} collective-permute-done((bf16[2080,128]{1,0:T(8,128)(2,1)S(1)}, bf16[2080,128]{1,0:T(8,128)(2,1)S(1)}, u32[]{:S(2)}, u32[]{:S(2)}) %collective-permute-start.9) | collective-permute-done | bytes 532512 | tf_op jit(solution)/shard_map/ppermute | solution.py:313
  46.7 0.0 collective-permute-start.10
  46.7 0.0 collective-permute-done.5.refs_0_
  46.7 3.2 %collective-permute-start.6 = (bf16[2080,128]{1,0:T(8,128)(2,1)S(1)}, bf16[2080,128]{1,0:T(8,128)(2,1)S(1)}, u32[]{:S(2)}, u32[]{:S(2)}) collective-permute-start(bf16[2080,128]{1,0:T(8,128)(2,1)S(1)} %collective-permute-done.5.refs_0_), channel_id=1, source_target_pairs={{0,16},{16,32},{32,48},{48,64},{64,80},{80,96},{96,112},{112,0},{1... | collective-permute-start | bytes 1597448 | tf_op jit(solution)/shard_map/ppermute | solution.py:312
  50.0 8.0 %ring.4 = (f32[4,2,136,256]{3,2,1,0:T(8,128)S(1)}, f32[4,2,136,256]{3,2,1,0:T(8,128)S(1)}) custom-call(s32[11]{0:T(128)S(1)} %stack.94.sc_ref, bf16[4,64,1024]{2,1,0:T(8,128)(2,1)S(1)} %pad_maximum_fusion.q0, bf16[4,64,1024]{2,1,0:T(8,128)(2,1)S(1)} %collective-permute-done.3.q1, ...), custom_call_target="tpu_custom_call", output_to_operand_aliasing={{0}: (5, {}), {1}: (6, {})} | custom-call | flops 4294967296 | bytes 6000000 | tf_op jit(solution)/shard_map/ring/pallas_call | solution.py:236
  57.9 8.0 %ring.5 = (f32[4,2,136,256]{3,2,1,0:T(8,128)S(1)}, f32[4,2,136,256]{3,2,1,0:T(8,128)S(1)}) custom-call(s32[11]{0:T(128)S(1)} %stack.94.sc_ref, bf16[4,64,1024]{2,1,0:T(8,128)(2,1)S(1)} %pad_maximum_fusion.q0, bf16[4,64,1024]{2,1,0:T(8,128)(2,1)S(1)} %collective-permute-done.3.q1, ...), custom_call_target="tpu_custom_call", output_to_operand_aliasing={{0}: (5, {}), {1}: (6, {})} | custom-call | flops 4294967296 | bytes 6000000 | tf_op jit(solution)/shard_map/ring/pallas_call | solution.py:236
  65.9 0.0 collective-permute-done.10.refs_1_
  66.0 15.9 %collective-permute-start.11 = (bf16[1040,128]{1,0:T(8,128)(2,1)S(1)}, bf16[1040,128]{1,0:T(8,128)(2,1)S(1)}, u32[]{:S(2)}, u32[]{:S(2)}) collective-permute-start(bf16[1040,128]{1,0:T(8,128)(2,1)S(1)} %slice.9), channel_id=1, source_target_pairs={{0,112},{16,0},{32,16},{48,32},{64,48},{80,64},{96,80},{112,96},{1... | collective-permute-start | bytes 798728 | tf_op jit(solution)/shard_map/ppermute | solution.py:315
  81.9 0.0 collective-permute-done.6.refs_0_
  81.9 0.1 collective-permute-start.7
  82.0 27.5 %ring.6 = (f32[4,2,136,256]{3,2,1,0:T(8,128)S(1)}, f32[4,2,136,256]{3,2,1,0:T(8,128)S(1)}) custom-call(s32[11]{0:T(128)S(1)} %stack.94.sc_ref, bf16[4,64,1024]{2,1,0:T(8,128)(2,1)S(1)} %pad_maximum_fusion.q0, bf16[4,64,1024]{2,1,0:T(8,128)(2,1)S(1)} %collective-permute-done.3.q1, ...), custom_call_target="tpu_custom_call", output_to_operand_aliasing={{0}: (5, {}), {1}: (6, {})} | custom-call | flops 4294967296 | bytes 6000000 | tf_op jit(solution)/shard_map/ring/pallas_call | solution.py:236
  109.5 0.0 collective-permute-done.11.refs_1_
  109.5 0.0 collective-permute-done.7.refs_0_
  109.5 4.5 %ring.7 = (f32[4,2,136,256]{3,2,1,0:T(8,128)S(1)}, f32[4,2,136,256]{3,2,1,0:T(8,128)S(1)}) custom-call(s32[11]{0:T(128)S(1)} %stack.94.sc_ref, bf16[4,64,1024]{2,1,0:T(8,128)(2,1)S(1)} %pad_maximum_fusion.q0, bf16[4,64,1024]{2,1,0:T(8,128)(2,1)S(1)} %collective-permute-done.3.q1, ...), custom_call_target="tpu_custom_call", output_to_operand_aliasing={{0}: (5, {}), {1}: (6, {})} | custom-call | flops 4294967296 | bytes 6000000 | tf_op jit(solution)/shard_map/ring/pallas_call | solution.py:236
  114.1 25.5 %collective-permute-start.12 = (f32[4,2,136,256]{3,2,1,0:T(8,128)S(1)}, f32[4,2,136,256]{3,2,1,0:T(8,128)S(1)}, u32[]{:S(2)}, u32[]{:S(2)}) collective-permute-start(f32[4,2,136,256]{3,2,1,0:T(8,128)S(1)} %get-tuple-element.36), channel_id=1, source_target_pairs={{0,1},{1,0},{2,3},{3,2},{4,5},{5,4},{6,7},{7,6},{8,9},{9,8},{10,11... | collective-permute-start | bytes 3342344 | tf_op jit(solution)/shard_map/ppermute | solution.py:322
  139.6 2.4 %collective-permute-done.12.r_ref = f32[4,2,136,256]{3,2,1,0:T(8,128)S(1)} collective-permute-done((f32[4,2,136,256]{3,2,1,0:T(8,128)S(1)}, f32[4,2,136,256]{3,2,1,0:T(8,128)S(1)}, u32[]{:S(2)}, u32[]{:S(2)}) %collective-permute-start.12) | collective-permute-done | bytes 1114144 | tf_op jit(solution)/shard_map/ppermute | solution.py:322
  142.0 0.8 shard_map.39
  142.8 1.0 collective-permute-start.13
  143.7 1.3 collective-permute-start.14
  145.0 2.0 %collective-permute-start.15 = (bf16[64,1024]{1,0:T(8,128)(2,1)S(1)}, bf16[64,1024]{1,0:T(8,128)(2,1)S(1)}, u32[]{:S(2)}, u32[]{:S(2)}) collective-permute-start(bf16[64,1024]{1,0:T(8,128)(2,1)S(1)} %get-tuple-element.40), channel_id=1, source_target_pairs={{0,136},{8,0},{128,8},{136,128},{1,137},{9,1},{129,9},{137,129},{2... | collective-permute-start | bytes 393224 | tf_op jit(solution)/shard_map/ppermute | solution.py:298
  147.1 2.0 %collective-permute-done.13.refs_1_ = bf16[64,1024]{1,0:T(8,128)(2,1)S(1)} collective-permute-done((bf16[64,1024]{1,0:T(8,128)(2,1)S(1)}, bf16[64,1024]{1,0:T(8,128)(2,1)S(1)}, u32[]{:S(2)}, u32[]{:S(2)}) %collective-permute-start.13) | collective-permute-done | bytes 131104 | tf_op jit(solution)/shard_map/ppermute | solution.py:298
  149.1 2.5 %collective-permute-done.14.refs_2_ = bf16[64,1024]{1,0:T(8,128)(2,1)S(1)} collective-permute-done((bf16[64,1024]{1,0:T(8,128)(2,1)S(1)}, bf16[64,1024]{1,0:T(8,128)(2,1)S(1)}, u32[]{:S(2)}, u32[]{:S(2)}) %collective-permute-start.14) | collective-permute-done | bytes 131104 | tf_op jit(solution)/shard_map/ppermute | solution.py:298
  151.6 1.7 %collective-permute-done.15.refs_3_ = bf16[64,1024]{1,0:T(8,128)(2,1)S(1)} collective-permute-done((bf16[64,1024]{1,0:T(8,128)(2,1)S(1)}, bf16[64,1024]{1,0:T(8,128)(2,1)S(1)}, u32[]{:S(2)}, u32[]{:S(2)}) %collective-permute-start.15) | collective-permute-done | bytes 131104 | tf_op jit(solution)/shard_map/ppermute | solution.py:298
  153.2 1.4 shard_map.40
  (2 shorter events, 0.0 us)
Async XLA Ops:
  0.0 0.8 copy-start.1
  0.8 0.8 copy-start.2
  1.7 8.2 %copy-start = (bf16[64,4096]{1,0:T(8,128)(2,1)S(1)}, bf16[64,4096]{1,0:T(8,128)(2,1)}, u32[]{:S(2)}) copy-start(bf16[64,4096]{1,0:T(8,128)(2,1)} %q_ref.1) | copy-start | bytes 1572868
  2.5 16.3 %all-to-all-start = ((bf16[16,128,128]{2,1,0:T(8,128)(2,1)}), bf16[16,128,128]{2,1,0:T(8,128)(2,1)S(1)}, u32[]{:S(2)}, u32[]{:S(2)}) async-start(bf16[16,128,128]{2,1,0:T(8,128)(2,1)} %shard_map.38), calls=%async_computation | async-start | bytes 1048576 | tf_op jit(solution)/shard_map/all_to_all | solution.py:305
  10.5 12.0 %collective-permute-start = (bf16[64,1024]{1,0:T(8,128)(2,1)S(1)}, bf16[64,1024]{1,0:T(8,128)(2,1)S(1)}, u32[]{:S(2)}, u32[]{:S(2)}) collective-permute-start(bf16[64,1024]{1,0:T(8,128)(2,1)S(1)} %get-tuple-element.24), channel_id=1, source_target_pairs={{0,8},{8,128},{128,136},{136,0},{1,9},{9,129},{129,137},{137,1},{2... | collective-permute-start | bytes 393224 | tf_op jit(solution)/shard_map/ppermute | solution.py:298
  11.8 10.8 %collective-permute-start.1 = (bf16[64,1024]{1,0:T(8,128)(2,1)S(1)}, bf16[64,1024]{1,0:T(8,128)(2,1)S(1)}, u32[]{:S(2)}, u32[]{:S(2)}) collective-permute-start(bf16[64,1024]{1,0:T(8,128)(2,1)S(1)} %get-tuple-element.25), channel_id=1, source_target_pairs={{0,128},{8,136},{128,0},{136,8},{1,129},{9,137},{129,1},{137,9},{2... | collective-permute-start | bytes 393224 | tf_op jit(solution)/shard_map/ppermute | solution.py:298
  12.6 11.0 %collective-permute-start.2 = (bf16[64,1024]{1,0:T(8,128)(2,1)S(1)}, bf16[64,1024]{1,0:T(8,128)(2,1)S(1)}, u32[]{:S(2)}, u32[]{:S(2)}) collective-permute-start(bf16[64,1024]{1,0:T(8,128)(2,1)S(1)} %get-tuple-element.26), channel_id=1, source_target_pairs={{0,136},{8,0},{128,8},{136,128},{1,137},{9,1},{129,9},{137,129},{2... | collective-permute-start | bytes 393224 | tf_op jit(solution)/shard_map/ppermute | solution.py:298
  19.2 14.2 %collective-permute-start.8 = (bf16[2080,128]{1,0:T(8,128)(2,1)S(1)}, bf16[2080,128]{1,0:T(8,128)(2,1)S(1)}, u32[]{:S(2)}, u32[]{:S(2)}) collective-permute-start(bf16[2080,128]{1,0:T(8,128)(2,1)S(1)} %prep.1.ch_ref), channel_id=1, source_target_pairs={{0,112},{16,0},{32,16},{48,32},{64,48},{80,64},{96,80},{112,96},{1... | collective-permute-start | bytes 1597448 | tf_op jit(solution)/shard_map/ppermute | solution.py:313
  20.3 13.2 %collective-permute-start.4 = (bf16[2080,128]{1,0:T(8,128)(2,1)S(1)}, bf16[2080,128]{1,0:T(8,128)(2,1)S(1)}, u32[]{:S(2)}, u32[]{:S(2)}) collective-permute-start(bf16[2080,128]{1,0:T(8,128)(2,1)S(1)} %prep.1.ch_ref), channel_id=1, source_target_pairs={{0,16},{16,32},{32,48},{48,64},{64,80},{80,96},{96,112},{112,0},{1... | collective-permute-start | bytes 1597448 | tf_op jit(solution)/shard_map/ppermute | solution.py:312
  23.6 13.0 %collective-permute-start.3 = (bf16[4,64,1024]{2,1,0:T(8,128)(2,1)S(1)}, bf16[4,64,1024]{2,1,0:T(8,128)(2,1)S(1)}, u32[]{:S(2)}, u32[]{:S(2)}) collective-permute-start(bf16[4,64,1024]{2,1,0:T(8,128)(2,1)S(1)} %pad_maximum_fusion.q0), channel_id=1, source_target_pairs={{0,1},{1,0},{2,3},{3,2},{4,5},{5,4},{6,7},{7,6},{8,9},{9,8},{10,11... | collective-permute-start | bytes 1572872 | tf_op jit(solution)/shard_map/ppermute | solution.py:307
  33.4 13.3 %collective-permute-start.9 = (bf16[2080,128]{1,0:T(8,128)(2,1)S(1)}, bf16[2080,128]{1,0:T(8,128)(2,1)S(1)}, u32[]{:S(2)}, u32[]{:S(2)}) collective-permute-start(bf16[2080,128]{1,0:T(8,128)(2,1)S(1)} %collective-permute-done.8.refs_1_), channel_id=1, source_target_pairs={{0,112},{16,0},{32,16},{48,32},{64,48},{80,64},{96,80},{112,96},{1... | collective-permute-start | bytes 1597448 | tf_op jit(solution)/shard_map/ppermute | solution.py:313
  33.4 13.3 %collective-permute-start.5 = (bf16[2080,128]{1,0:T(8,128)(2,1)S(1)}, bf16[2080,128]{1,0:T(8,128)(2,1)S(1)}, u32[]{:S(2)}, u32[]{:S(2)}) collective-permute-start(bf16[2080,128]{1,0:T(8,128)(2,1)S(1)} %collective-permute-done.4.refs_0_), channel_id=1, source_target_pairs={{0,16},{16,32},{32,48},{48,64},{64,80},{80,96},{96,112},{112,0},{1... | collective-permute-start | bytes 1597448 | tf_op jit(solution)/shard_map/ppermute | solution.py:312
  46.7 19.2 %collective-permute-start.10 = (bf16[2080,128]{1,0:T(8,128)(2,1)S(1)}, bf16[2080,128]{1,0:T(8,128)(2,1)S(1)}, u32[]{:S(2)}, u32[]{:S(2)}) collective-permute-start(bf16[2080,128]{1,0:T(8,128)(2,1)S(1)} %collective-permute-done.9.refs_1_), channel_id=1, source_target_pairs={{0,112},{16,0},{32,16},{48,32},{64,48},{80,64},{96,80},{112,96},{1... | collective-permute-start | bytes 1597448 | tf_op jit(solution)/shard_map/ppermute | solution.py:313
  46.7 35.2 %collective-permute-start.6 = (bf16[2080,128]{1,0:T(8,128)(2,1)S(1)}, bf16[2080,128]{1,0:T(8,128)(2,1)S(1)}, u32[]{:S(2)}, u32[]{:S(2)}) collective-permute-start(bf16[2080,128]{1,0:T(8,128)(2,1)S(1)} %collective-permute-done.5.refs_0_), channel_id=1, source_target_pairs={{0,16},{16,32},{32,48},{48,64},{64,80},{80,96},{96,112},{112,0},{1... | collective-permute-start | bytes 1597448 | tf_op jit(solution)/shard_map/ppermute | solution.py:312
  66.0 43.5 %collective-permute-start.11 = (bf16[1040,128]{1,0:T(8,128)(2,1)S(1)}, bf16[1040,128]{1,0:T(8,128)(2,1)S(1)}, u32[]{:S(2)}, u32[]{:S(2)}) collective-permute-start(bf16[1040,128]{1,0:T(8,128)(2,1)S(1)} %slice.9), channel_id=1, source_target_pairs={{0,112},{16,0},{32,16},{48,32},{64,48},{80,64},{96,80},{112,96},{1... | collective-permute-start | bytes 798728 | tf_op jit(solution)/shard_map/ppermute | solution.py:315
  81.9 27.6 %collective-permute-start.7 = (bf16[1040,128]{1,0:T(8,128)(2,1)S(1)}, bf16[1040,128]{1,0:T(8,128)(2,1)S(1)}, u32[]{:S(2)}, u32[]{:S(2)}) collective-permute-start(bf16[1040,128]{1,0:T(8,128)(2,1)S(1)} %slice.8), channel_id=1, source_target_pairs={{0,16},{16,32},{32,48},{48,64},{64,80},{80,96},{96,112},{112,0},{1... | collective-permute-start | bytes 798728 | tf_op jit(solution)/shard_map/ppermute | solution.py:314
  114.1 27.9 %collective-permute-start.12 = (f32[4,2,136,256]{3,2,1,0:T(8,128)S(1)}, f32[4,2,136,256]{3,2,1,0:T(8,128)S(1)}, u32[]{:S(2)}, u32[]{:S(2)}) collective-permute-start(f32[4,2,136,256]{3,2,1,0:T(8,128)S(1)} %get-tuple-element.36), channel_id=1, source_target_pairs={{0,1},{1,0},{2,3},{3,2},{4,5},{5,4},{6,7},{7,6},{8,9},{9,8},{10,11... | collective-permute-start | bytes 3342344 | tf_op jit(solution)/shard_map/ppermute | solution.py:322
  142.8 6.3 %collective-permute-start.13 = (bf16[64,1024]{1,0:T(8,128)(2,1)S(1)}, bf16[64,1024]{1,0:T(8,128)(2,1)S(1)}, u32[]{:S(2)}, u32[]{:S(2)}) collective-permute-start(bf16[64,1024]{1,0:T(8,128)(2,1)S(1)} %get-tuple-element.38), channel_id=1, source_target_pairs={{0,8},{8,128},{128,136},{136,0},{1,9},{9,129},{129,137},{137,1},{2... | collective-permute-start | bytes 393224 | tf_op jit(solution)/shard_map/ppermute | solution.py:298
  143.7 7.8 %collective-permute-start.14 = (bf16[64,1024]{1,0:T(8,128)(2,1)S(1)}, bf16[64,1024]{1,0:T(8,128)(2,1)S(1)}, u32[]{:S(2)}, u32[]{:S(2)}) collective-permute-start(bf16[64,1024]{1,0:T(8,128)(2,1)S(1)} %get-tuple-element.39), channel_id=1, source_target_pairs={{0,128},{8,136},{128,0},{136,8},{1,129},{9,137},{129,1},{137,9},{2... | collective-permute-start | bytes 393224 | tf_op jit(solution)/shard_map/ppermute | solution.py:298
  145.0 8.2 %collective-permute-start.15 = (bf16[64,1024]{1,0:T(8,128)(2,1)S(1)}, bf16[64,1024]{1,0:T(8,128)(2,1)S(1)}, u32[]{:S(2)}, u32[]{:S(2)}) collective-permute-start(bf16[64,1024]{1,0:T(8,128)(2,1)S(1)} %get-tuple-element.40), channel_id=1, source_target_pairs={{0,136},{8,0},{128,8},{136,128},{1,137},{9,1},{129,9},{137,129},{2... | collective-permute-start | bytes 393224 | tf_op jit(solution)/shard_map/ppermute | solution.py:298
where the time goes:
time: 156 us; the launch traced here: 155 us
  starting transfers between devices  65.8 us (42%)
  Pallas kernels  57.4 us (37%)
  waiting for transfers between devices  29.3 us (19%)
  local copies, waits for them, and re-layouts  1.81 us (1%)
    pallas_call x4, Pallas kernels, ring_step(): pl.pallas_call(functools.partial(step_kernel, parts), out_shape=ST, in_sp...  47.9 us
    ppermute x1, starting transfers between devices, per_device(): other = lax.ppermute(state[1], 'c', swap)  25.5 us
    ppermute x1, starting transfers between devices, per_device(): far_h = lax.ppermute(bwd[3][HALF:], 'z', down)  15.9 us
    ppermute x3, waiting for transfers between devices, per_device(): bwd.append(lax.ppermute(bwd[-1], 'z', down))  14.2 us
    ppermute x3, starting transfers between devices, per_device(): fwd.append(lax.ppermute(fwd[-1], 'z', up))  8.7 us
    all_to_all x1, starting transfers between devices, per_device(): lax.all_to_all(kv, ('yh', 'yl', 'x'), split_axis=0, concat_axis=0, tiled=...  7.28 us
    ppermute x6, waiting for transfers between devices, regroup(): lax.ppermute(pieces[d], ('yh', 'yl'), [(i, (i + d) % ny) for i in range(n...  7.23 us
    ppermute x6, starting transfers between devices, regroup(): lax.ppermute(pieces[d], ('yh', 'yl'), [(i, (i + d) % ny) for i in range(n...  7.12 us
  transfers between devices with their start and end apart: 17, of which 8 were waited for; matrix products, arithmetic and copies ran while one was open for 0% of the time, Pallas kernels for 32%

commit v1 on v0

--- a/solution.py
+++ b/solution.py
@@ -259,6 +259,11 @@
         outs[d][...] = q_ref[:, pl.ds(pl.multiple_of(to * 8 * DH, 8 * DH), 8 * DH)]
 
 
+def join_kernel(a_ref, b_ref, c_ref, d_ref, out_ref):
+    for d, ref in enumerate((a_ref, b_ref, c_ref, d_ref)):
+        out_ref[d] = ref[...]
+
+
 def merge_kernel(sc_ref, s_ref, r_ref, *outs):
     for d in range(4):
         t = jnp.bitwise_and(sc_ref[0] + d, 3)
@@ -303,7 +308,8 @@
     sent = jax.ShapeDtypeStruct((16, 2 * STRIP, DH), bf16)
     kv = small(kv_send_kernel, sent, 2, False)(keys, values)
     kv = lax.all_to_all(kv, ("yh", "yl", "x"), split_axis=0, concat_axis=0, tiled=True)
-    q0 = jnp.stack(regroup(small(q_send_kernel, (piece,) * 4, 1)(sc, queries)))
+    q_pieces = regroup(small(q_send_kernel, (piece,) * 4, 1)(sc, queries))
+    q0 = small(join_kernel, jax.ShapeDtypeStruct((4, STRIP, 8 * DH), bf16), 4, False)(*q_pieces)
     q1 = lax.ppermute(q0, "c", swap)
     chunk = prep(kv)
 

time: 156 us -> 157 us (level)
  blocking collectives: 0 us -> 16.2 us
  waiting for transfers between devices: 29.3 us -> 17.7 us
  starting transfers between devices: 65.8 us -> 62.2 us
    all_to_all x0 -> x1, blocking collectives: none -> 16.2 us  [per_device(): lax.all_to_all(kv, ('yh', 'yl', 'x'), split_axis=0, concat_axis=0, tiled=...]
    ppermute x3, waiting for transfers between devices: 14.2 us -> 6.9 us  [per_device(): bwd.append(lax.ppermute(bwd[-1], 'z', down))]
    all_to_all x1 -> x0, starting transfers between devices: 7.28 us -> none  [per_device(): lax.all_to_all(kv, ('yh', 'yl', 'x'), split_axis=0, concat_axis=0, tiled=...]
    all_to_all x1 -> x0, waiting for transfers between devices: 5.53 us -> none  [per_device(): lax.all_to_all(kv, ('yh', 'yl', 'x'), split_axis=0, concat_axis=0, tiled=...]
    ppermute x6, starting transfers between devices: 7.12 us -> 10.8 us  [regroup(): lax.ppermute(pieces[d], ('yh', 'yl'), [(i, (i + d) % ny) for i in range(n...]
  transfers between devices with their start and end apart: 17 -> 16, of which waited for: 8 -> 9; matrix products, arithmetic and copies ran while one was open for 0% -> 0% of each run, Pallas kernels for 32% -> 32%
where the time goes in v1:
time: 157 us; the launch traced here: 155 us
  starting transfers between devices  62.2 us (40%)
  Pallas kernels  56.7 us (36%)
  waiting for transfers between devices  17.7 us (11%)
  blocking collectives  16.2 us (10%)
  local copies, waits for them, and re-layouts  1.81 us (1%)
    pallas_call x4, Pallas kernels, ring_step(): pl.pallas_call(functools.partial(step_kernel, parts), out_shape=ST, in_sp...  48 us
    ppermute x1, starting transfers between devices, per_device(): other = lax.ppermute(state[1], 'c', swap)  25.5 us
    all_to_all x1, blocking collectives, per_device(): lax.all_to_all(kv, ('yh', 'yl', 'x'), split_axis=0, concat_axis=0, tiled=...  16.2 us
    ppermute x1, starting transfers between devices, per_device(): far_h = lax.ppermute(bwd[3][HALF:], 'z', down)  15.9 us
    ppermute x6, starting transfers between devices, regroup(): lax.ppermute(pieces[d], ('yh', 'yl'), [(i, (i + d) % ny) for i in range(n...  10.8 us
    ppermute x3, starting transfers between devices, per_device(): fwd.append(lax.ppermute(fwd[-1], 'z', up))  8.7 us
    ppermute x6, waiting for transfers between devices, regroup(): lax.ppermute(pieces[d], ('yh', 'yl'), [(i, (i + d) % ny) for i in range(n...  8.37 us
    ppermute x3, waiting for transfers between devices, per_device(): bwd.append(lax.ppermute(bwd[-1], 'z', down))  6.9 us
  transfers between devices with their start and end apart: 16, of which 9 were waited for; matrix products, arithmetic and copies ran while one was open for 0% of the time, Pallas kernels for 32%

profile of v1, /device:TPU:240, one launch (start us, length us, event | category | flops | bytes accessed | tf_op | source)
XLA Modules:
  0.0 154.7 jit_solution(2805545533683874358)
XLA Ops:
  0.0 0.0 copy-start.1
  0.0 0.8 copy-done.1
  0.8 0.0 copy-start.2
  0.8 0.8 copy-done.2
  1.7 0.1 shard_map.39
  1.8 0.0 copy-start
  1.8 16.2 %all_to_all.5.kv_ref = bf16[16,128,128]{2,1,0:T(8,128)(2,1)S(1)} all-to-all(bf16[16,128,128]{2,1,0:T(8,128)(2,1)S(1)} %shard_map.39), channel_id=1, replica_groups=mesh['yh'=2,'z'=8,'yl'=2,'x'=4,'c'=2] {'yh','yl','x'}, dimensions={0} | all-to-all | bytes 1048576 | tf_op jit(solution)/shard_map/all_to_all | solution.py:310
  17.9 0.3 prep.1.ch_ref
  18.2 1.1 collective-permute-start.8
  19.3 2.2 %collective-permute-start.4 = (bf16[2080,128]{1,0:T(8,128)(2,1)S(1)}, bf16[2080,128]{1,0:T(8,128)(2,1)S(1)}, u32[]{:S(2)}, u32[]{:S(2)}) collective-permute-start(bf16[2080,128]{1,0:T(8,128)(2,1)S(1)} %prep.1.ch_ref), channel_id=1, source_target_pairs={{0,16},{16,32},{32,48},{48,64},{64,80},{80,96},{96,112},{112,0},{1... | collective-permute-start | bytes 1597448 | tf_op jit(solution)/shard_map/ppermute | solution.py:318
  21.5 0.1 stack.79.sc_ref
  21.6 0.0 copy-done
  21.6 0.6 shard_map.37
  22.2 1.5 collective-permute-start
  23.8 1.3 collective-permute-start.1
  25.1 2.5 %collective-permute-start.2 = (bf16[64,1024]{1,0:T(8,128)(2,1)S(1)}, bf16[64,1024]{1,0:T(8,128)(2,1)S(1)}, u32[]{:S(2)}, u32[]{:S(2)}) collective-permute-start(bf16[64,1024]{1,0:T(8,128)(2,1)S(1)} %get-tuple-element.26), channel_id=1, source_target_pairs={{0,136},{8,0},{128,8},{136,128},{1,137},{9,1},{129,9},{137,129},{2... | collective-permute-start | bytes 393224 | tf_op jit(solution)/shard_map/ppermute | solution.py:303
  27.6 1.0 collective-permute-done.b_ref
  28.6 1.7 %collective-permute-done.1.c_ref = bf16[64,1024]{1,0:T(8,128)(2,1)S(1)} collective-permute-done((bf16[64,1024]{1,0:T(8,128)(2,1)S(1)}, bf16[64,1024]{1,0:T(8,128)(2,1)S(1)}, u32[]{:S(2)}, u32[]{:S(2)}) %collective-permute-start.1) | collective-permute-done | bytes 131104 | tf_op jit(solution)/shard_map/ppermute | solution.py:303
  30.2 0.5 collective-permute-done.2.d_ref
  30.8 0.1 collective-permute-start.3
  30.9 1.6 %collective-permute-done.8.refs_1_ = bf16[2080,128]{1,0:T(8,128)(2,1)S(1)} collective-permute-done((bf16[2080,128]{1,0:T(8,128)(2,1)S(1)}, bf16[2080,128]{1,0:T(8,128)(2,1)S(1)}, u32[]{:S(2)}, u32[]{:S(2)}) %collective-permute-start.8) | collective-permute-done | bytes 532512 | tf_op jit(solution)/shard_map/ppermute | solution.py:319
  32.6 0.0 collective-permute-start.9
  32.6 0.0 collective-permute-done.4.refs_0_
  32.6 3.2 %collective-permute-start.5 = (bf16[2080,128]{1,0:T(8,128)(2,1)S(1)}, bf16[2080,128]{1,0:T(8,128)(2,1)S(1)}, u32[]{:S(2)}, u32[]{:S(2)}) collective-permute-start(bf16[2080,128]{1,0:T(8,128)(2,1)S(1)} %collective-permute-done.4.refs_0_), channel_id=1, source_target_pairs={{0,16},{16,32},{32,48},{48,64},{64,80},{80,96},{96,112},{112,0},{1... | collective-permute-start | bytes 1597448 | tf_op jit(solution)/shard_map/ppermute | solution.py:318
  35.8 0.0 collective-permute-done.3.q1
  35.8 5.6 %own.1 = (f32[4,2,136,256]{3,2,1,0:T(8,128)S(1)}, f32[4,2,136,256]{3,2,1,0:T(8,128)S(1)}) custom-call(s32[11]{0:T(128)S(1)} %stack.79.sc_ref, bf16[4,64,1024]{2,1,0:T(8,128)(2,1)S(1)} %shard_map.38.q0, bf16[4,64,1024]{2,1,0:T(8,128)(2,1)S(1)} %collective-permute-done.3.q1, bf16[2080,128]{1,0:T(8,128)(2,1)S(1)} %prep.1.ch_ref), custom_call_target="tpu_custom_call" | custom-call | flops 3221225472 | bytes 6000000 | tf_op jit(solution)/shard_map/own/pallas_call | solution.py:223
  41.4 5.3 %collective-permute-done.9.refs_1_ = bf16[2080,128]{1,0:T(8,128)(2,1)S(1)} collective-permute-done((bf16[2080,128]{1,0:T(8,128)(2,1)S(1)}, bf16[2080,128]{1,0:T(8,128)(2,1)S(1)}, u32[]{:S(2)}, u32[]{:S(2)}) %collective-permute-start.9) | collective-permute-done | bytes 532512 | tf_op jit(solution)/shard_map/ppermute | solution.py:319
  46.6 0.0 collective-permute-start.10
  46.6 0.0 collective-permute-done.5.refs_0_
  46.7 3.2 %collective-permute-start.6 = (bf16[2080,128]{1,0:T(8,128)(2,1)S(1)}, bf16[2080,128]{1,0:T(8,128)(2,1)S(1)}, u32[]{:S(2)}, u32[]{:S(2)}) collective-permute-start(bf16[2080,128]{1,0:T(8,128)(2,1)S(1)} %collective-permute-done.5.refs_0_), channel_id=1, source_target_pairs={{0,16},{16,32},{32,48},{48,64},{64,80},{80,96},{96,112},{112,0},{1... | collective-permute-start | bytes 1597448 | tf_op jit(solution)/shard_map/ppermute | solution.py:318
  49.9 8.0 %ring.4 = (f32[4,2,136,256]{3,2,1,0:T(8,128)S(1)}, f32[4,2,136,256]{3,2,1,0:T(8,128)S(1)}) custom-call(s32[11]{0:T(128)S(1)} %stack.79.sc_ref, bf16[4,64,1024]{2,1,0:T(8,128)(2,1)S(1)} %shard_map.38.q0, bf16[4,64,1024]{2,1,0:T(8,128)(2,1)S(1)} %collective-permute-done.3.q1, ...), custom_call_target="tpu_custom_call", output_to_operand_aliasing={{0}: (5, {}), {1}: (6, {})} | custom-call | flops 4294967296 | bytes 6000000 | tf_op jit(solution)/shard_map/ring/pallas_call | solution.py:236
  57.9 8.0 %ring.5 = (f32[4,2,136,256]{3,2,1,0:T(8,128)S(1)}, f32[4,2,136,256]{3,2,1,0:T(8,128)S(1)}) custom-call(s32[11]{0:T(128)S(1)} %stack.79.sc_ref, bf16[4,64,1024]{2,1,0:T(8,128)(2,1)S(1)} %shard_map.38.q0, bf16[4,64,1024]{2,1,0:T(8,128)(2,1)S(1)} %collective-permute-done.3.q1, ...), custom_call_target="tpu_custom_call", output_to_operand_aliasing={{0}: (5, {}), {1}: (6, {})} | custom-call | flops 4294967296 | bytes 6000000 | tf_op jit(solution)/shard_map/ring/pallas_call | solution.py:236
  65.9 0.0 collective-permute-done.10.refs_1_
  65.9 15.9 %collective-permute-start.11 = (bf16[1040,128]{1,0:T(8,128)(2,1)S(1)}, bf16[1040,128]{1,0:T(8,128)(2,1)S(1)}, u32[]{:S(2)}, u32[]{:S(2)}) collective-permute-start(bf16[1040,128]{1,0:T(8,128)(2,1)S(1)} %slice.9), channel_id=1, source_target_pairs={{0,112},{16,0},{32,16},{48,32},{64,48},{80,64},{96,80},{112,96},{1... | collective-permute-start | bytes 798728 | tf_op jit(solution)/shard_map/ppermute | solution.py:321
  81.8 0.0 collective-permute-done.6.refs_0_
  81.9 0.1 collective-permute-start.7
  81.9 27.5 %ring.6 = (f32[4,2,136,256]{3,2,1,0:T(8,128)S(1)}, f32[4,2,136,256]{3,2,1,0:T(8,128)S(1)}) custom-call(s32[11]{0:T(128)S(1)} %stack.79.sc_ref, bf16[4,64,1024]{2,1,0:T(8,128)(2,1)S(1)} %shard_map.38.q0, bf16[4,64,1024]{2,1,0:T(8,128)(2,1)S(1)} %collective-permute-done.3.q1, ...), custom_call_target="tpu_custom_call", output_to_operand_aliasing={{0}: (5, {}), {1}: (6, {})} | custom-call | flops 4294967296 | bytes 6000000 | tf_op jit(solution)/shard_map/ring/pallas_call | solution.py:236
  109.4 0.0 collective-permute-done.11.refs_1_
  109.4 0.0 collective-permute-done.7.refs_0_
  109.4 4.5 %ring.7 = (f32[4,2,136,256]{3,2,1,0:T(8,128)S(1)}, f32[4,2,136,256]{3,2,1,0:T(8,128)S(1)}) custom-call(s32[11]{0:T(128)S(1)} %stack.79.sc_ref, bf16[4,64,1024]{2,1,0:T(8,128)(2,1)S(1)} %shard_map.38.q0, bf16[4,64,1024]{2,1,0:T(8,128)(2,1)S(1)} %collective-permute-done.3.q1, ...), custom_call_target="tpu_custom_call", output_to_operand_aliasing={{0}: (5, {}), {1}: (6, {})} | custom-call | flops 4294967296 | bytes 6000000 | tf_op jit(solution)/shard_map/ring/pallas_call | solution.py:236
  114.0 25.5 %collective-permute-start.12 = (f32[4,2,136,256]{3,2,1,0:T(8,128)S(1)}, f32[4,2,136,256]{3,2,1,0:T(8,128)S(1)}, u32[]{:S(2)}, u32[]{:S(2)}) collective-permute-start(f32[4,2,136,256]{3,2,1,0:T(8,128)S(1)} %get-tuple-element.36), channel_id=1, source_target_pairs={{0,1},{1,0},{2,3},{3,2},{4,5},{5,4},{6,7},{7,6},{8,9},{9,8},{10,11... | collective-permute-start | bytes 3342344 | tf_op jit(solution)/shard_map/ppermute | solution.py:328
  139.5 2.4 %collective-permute-done.12.r_ref = f32[4,2,136,256]{3,2,1,0:T(8,128)S(1)} collective-permute-done((f32[4,2,136,256]{3,2,1,0:T(8,128)S(1)}, f32[4,2,136,256]{3,2,1,0:T(8,128)S(1)}, u32[]{:S(2)}, u32[]{:S(2)}) %collective-permute-start.12) | collective-permute-done | bytes 1114144 | tf_op jit(solution)/shard_map/ppermute | solution.py:328
  141.9 0.8 shard_map.40
  142.7 3.3 %collective-permute-start.13 = (bf16[64,1024]{1,0:T(8,128)(2,1)S(1)}, bf16[64,1024]{1,0:T(8,128)(2,1)S(1)}, u32[]{:S(2)}, u32[]{:S(2)}) collective-permute-start(bf16[64,1024]{1,0:T(8,128)(2,1)S(1)} %get-tuple-element.38), channel_id=1, source_target_pairs={{0,8},{8,128},{128,136},{136,0},{1,9},{9,129},{129,137},{137,1},{2... | collective-permute-start | bytes 393224 | tf_op jit(solution)/shard_map/ppermute | solution.py:303
  146.0 0.1 collective-permute-start.14
  146.1 2.1 %collective-permute-start.15 = (bf16[64,1024]{1,0:T(8,128)(2,1)S(1)}, bf16[64,1024]{1,0:T(8,128)(2,1)S(1)}, u32[]{:S(2)}, u32[]{:S(2)}) collective-permute-start(bf16[64,1024]{1,0:T(8,128)(2,1)S(1)} %get-tuple-element.40), channel_id=1, source_target_pairs={{0,136},{8,0},{128,8},{136,128},{1,137},{9,1},{129,9},{137,129},{2... | collective-permute-start | bytes 393224 | tf_op jit(solution)/shard_map/ppermute | solution.py:303
  148.1 1.7 %collective-permute-done.13.refs_1_ = bf16[64,1024]{1,0:T(8,128)(2,1)S(1)} collective-permute-done((bf16[64,1024]{1,0:T(8,128)(2,1)S(1)}, bf16[64,1024]{1,0:T(8,128)(2,1)S(1)}, u32[]{:S(2)}, u32[]{:S(2)}) %collective-permute-start.13) | collective-permute-done | bytes 131104 | tf_op jit(solution)/shard_map/ppermute | solution.py:303
  149.9 3.1 %collective-permute-done.14.refs_2_ = bf16[64,1024]{1,0:T(8,128)(2,1)S(1)} collective-permute-done((bf16[64,1024]{1,0:T(8,128)(2,1)S(1)}, bf16[64,1024]{1,0:T(8,128)(2,1)S(1)}, u32[]{:S(2)}, u32[]{:S(2)}) %collective-permute-start.14) | collective-permute-done | bytes 131104 | tf_op jit(solution)/shard_map/ppermute | solution.py:303
  153.0 0.3 collective-permute-done.15.refs_3_
  153.3 1.4 shard_map.41
  (3 shorter events, 0.1 us)
Async XLA Ops:
  0.0 0.8 copy-start.1
  0.8 0.8 copy-start.2
  1.8 19.9 %copy-start = (bf16[64,4096]{1,0:T(8,128)(2,1)S(1)}, bf16[64,4096]{1,0:T(8,128)(2,1)}, u32[]{:S(2)}) copy-start(bf16[64,4096]{1,0:T(8,128)(2,1)} %q_ref.1) | copy-start | bytes 1572868
  18.2 14.3 %collective-permute-start.8 = (bf16[2080,128]{1,0:T(8,128)(2,1)S(1)}, bf16[2080,128]{1,0:T(8,128)(2,1)S(1)}, u32[]{:S(2)}, u32[]{:S(2)}) collective-permute-start(bf16[2080,128]{1,0:T(8,128)(2,1)S(1)} %prep.1.ch_ref), channel_id=1, source_target_pairs={{0,112},{16,0},{32,16},{48,32},{64,48},{80,64},{96,80},{112,96},{1... | collective-permute-start | bytes 1597448 | tf_op jit(solution)/shard_map/ppermute | solution.py:319
  19.3 13.3 %collective-permute-start.4 = (bf16[2080,128]{1,0:T(8,128)(2,1)S(1)}, bf16[2080,128]{1,0:T(8,128)(2,1)S(1)}, u32[]{:S(2)}, u32[]{:S(2)}) collective-permute-start(bf16[2080,128]{1,0:T(8,128)(2,1)S(1)} %prep.1.ch_ref), channel_id=1, source_target_pairs={{0,16},{16,32},{32,48},{48,64},{64,80},{80,96},{96,112},{112,0},{1... | collective-permute-start | bytes 1597448 | tf_op jit(solution)/shard_map/ppermute | solution.py:318
  22.2 6.4 %collective-permute-start = (bf16[64,1024]{1,0:T(8,128)(2,1)S(1)}, bf16[64,1024]{1,0:T(8,128)(2,1)S(1)}, u32[]{:S(2)}, u32[]{:S(2)}) collective-permute-start(bf16[64,1024]{1,0:T(8,128)(2,1)S(1)} %get-tuple-element.24), channel_id=1, source_target_pairs={{0,8},{8,128},{128,136},{136,0},{1,9},{9,129},{129,137},{137,1},{2... | collective-permute-start | bytes 393224 | tf_op jit(solution)/shard_map/ppermute | solution.py:303
  23.8 6.5 %collective-permute-start.1 = (bf16[64,1024]{1,0:T(8,128)(2,1)S(1)}, bf16[64,1024]{1,0:T(8,128)(2,1)S(1)}, u32[]{:S(2)}, u32[]{:S(2)}) collective-permute-start(bf16[64,1024]{1,0:T(8,128)(2,1)S(1)} %get-tuple-element.25), channel_id=1, source_target_pairs={{0,128},{8,136},{128,0},{136,8},{1,129},{9,137},{129,1},{137,9},{2... | collective-permute-start | bytes 393224 | tf_op jit(solution)/shard_map/ppermute | solution.py:303
  25.1 5.7 %collective-permute-start.2 = (bf16[64,1024]{1,0:T(8,128)(2,1)S(1)}, bf16[64,1024]{1,0:T(8,128)(2,1)S(1)}, u32[]{:S(2)}, u32[]{:S(2)}) collective-permute-start(bf16[64,1024]{1,0:T(8,128)(2,1)S(1)} %get-tuple-element.26), channel_id=1, source_target_pairs={{0,136},{8,0},{128,8},{136,128},{1,137},{9,1},{129,9},{137,129},{2... | collective-permute-start | bytes 393224 | tf_op jit(solution)/shard_map/ppermute | solution.py:303
  30.8 5.0 %collective-permute-start.3 = (bf16[4,64,1024]{2,1,0:T(8,128)(2,1)S(1)}, bf16[4,64,1024]{2,1,0:T(8,128)(2,1)S(1)}, u32[]{:S(2)}, u32[]{:S(2)}) collective-permute-start(bf16[4,64,1024]{2,1,0:T(8,128)(2,1)S(1)} %shard_map.38.q0), channel_id=1, source_target_pairs={{0,1},{1,0},{2,3},{3,2},{4,5},{5,4},{6,7},{7,6},{8,9},{9,8},{10,11... | collective-permute-start | bytes 1572872 | tf_op jit(solution)/shard_map/ppermute | solution.py:313
  32.6 14.1 %collective-permute-start.9 = (bf16[2080,128]{1,0:T(8,128)(2,1)S(1)}, bf16[2080,128]{1,0:T(8,128)(2,1)S(1)}, u32[]{:S(2)}, u32[]{:S(2)}) collective-permute-start(bf16[2080,128]{1,0:T(8,128)(2,1)S(1)} %collective-permute-done.8.refs_1_), channel_id=1, source_target_pairs={{0,112},{16,0},{32,16},{48,32},{64,48},{80,64},{96,80},{112,96},{1... | collective-permute-start | bytes 1597448 | tf_op jit(solution)/shard_map/ppermute | solution.py:319
  32.6 14.1 %collective-permute-start.5 = (bf16[2080,128]{1,0:T(8,128)(2,1)S(1)}, bf16[2080,128]{1,0:T(8,128)(2,1)S(1)}, u32[]{:S(2)}, u32[]{:S(2)}) collective-permute-start(bf16[2080,128]{1,0:T(8,128)(2,1)S(1)} %collective-permute-done.4.refs_0_), channel_id=1, source_target_pairs={{0,16},{16,32},{32,48},{48,64},{64,80},{80,96},{96,112},{112,0},{1... | collective-permute-start | bytes 1597448 | tf_op jit(solution)/shard_map/ppermute | solution.py:318
  46.6 19.2 %collective-permute-start.10 = (bf16[2080,128]{1,0:T(8,128)(2,1)S(1)}, bf16[2080,128]{1,0:T(8,128)(2,1)S(1)}, u32[]{:S(2)}, u32[]{:S(2)}) collective-permute-start(bf16[2080,128]{1,0:T(8,128)(2,1)S(1)} %collective-permute-done.9.refs_1_), channel_id=1, source_target_pairs={{0,112},{16,0},{32,16},{48,32},{64,48},{80,64},{96,80},{112,96},{1... | collective-permute-start | bytes 1597448 | tf_op jit(solution)/shard_map/ppermute | solution.py:319
  46.7 35.2 %collective-permute-start.6 = (bf16[2080,128]{1,0:T(8,128)(2,1)S(1)}, bf16[2080,128]{1,0:T(8,128)(2,1)S(1)}, u32[]{:S(2)}, u32[]{:S(2)}) collective-permute-start(bf16[2080,128]{1,0:T(8,128)(2,1)S(1)} %collective-permute-done.5.refs_0_), channel_id=1, source_target_pairs={{0,16},{16,32},{32,48},{48,64},{64,80},{80,96},{96,112},{112,0},{1... | collective-permute-start | bytes 1597448 | tf_op jit(solution)/shard_map/ppermute | solution.py:318
  65.9 43.5 %collective-permute-start.11 = (bf16[1040,128]{1,0:T(8,128)(2,1)S(1)}, bf16[1040,128]{1,0:T(8,128)(2,1)S(1)}, u32[]{:S(2)}, u32[]{:S(2)}) collective-permute-start(bf16[1040,128]{1,0:T(8,128)(2,1)S(1)} %slice.9), channel_id=1, source_target_pairs={{0,112},{16,0},{32,16},{48,32},{64,48},{80,64},{96,80},{112,96},{1... | collective-permute-start | bytes 798728 | tf_op jit(solution)/shard_map/ppermute | solution.py:321
  81.9 27.6 %collective-permute-start.7 = (bf16[1040,128]{1,0:T(8,128)(2,1)S(1)}, bf16[1040,128]{1,0:T(8,128)(2,1)S(1)}, u32[]{:S(2)}, u32[]{:S(2)}) collective-permute-start(bf16[1040,128]{1,0:T(8,128)(2,1)S(1)} %slice.8), channel_id=1, source_target_pairs={{0,16},{16,32},{32,48},{48,64},{64,80},{80,96},{96,112},{112,0},{1... | collective-permute-start | bytes 798728 | tf_op jit(solution)/shard_map/ppermute | solution.py:320
  114.0 27.9 %collective-permute-start.12 = (f32[4,2,136,256]{3,2,1,0:T(8,128)S(1)}, f32[4,2,136,256]{3,2,1,0:T(8,128)S(1)}, u32[]{:S(2)}, u32[]{:S(2)}) collective-permute-start(f32[4,2,136,256]{3,2,1,0:T(8,128)S(1)} %get-tuple-element.36), channel_id=1, source_target_pairs={{0,1},{1,0},{2,3},{3,2},{4,5},{5,4},{6,7},{7,6},{8,9},{9,8},{10,11... | collective-permute-start | bytes 3342344 | tf_op jit(solution)/shard_map/ppermute | solution.py:328
  142.7 7.2 %collective-permute-start.13 = (bf16[64,1024]{1,0:T(8,128)(2,1)S(1)}, bf16[64,1024]{1,0:T(8,128)(2,1)S(1)}, u32[]{:S(2)}, u32[]{:S(2)}) collective-permute-start(bf16[64,1024]{1,0:T(8,128)(2,1)S(1)} %get-tuple-element.38), channel_id=1, source_target_pairs={{0,8},{8,128},{128,136},{136,0},{1,9},{9,129},{129,137},{137,1},{2... | collective-permute-start | bytes 393224 | tf_op jit(solution)/shard_map/ppermute | solution.py:303
  146.0 7.0 %collective-permute-start.14 = (bf16[64,1024]{1,0:T(8,128)(2,1)S(1)}, bf16[64,1024]{1,0:T(8,128)(2,1)S(1)}, u32[]{:S(2)}, u32[]{:S(2)}) collective-permute-start(bf16[64,1024]{1,0:T(8,128)(2,1)S(1)} %get-tuple-element.39), channel_id=1, source_target_pairs={{0,128},{8,136},{128,0},{136,8},{1,129},{9,137},{129,1},{137,9},{2... | collective-permute-start | bytes 393224 | tf_op jit(solution)/shard_map/ppermute | solution.py:303
  146.1 7.3 %collective-permute-start.15 = (bf16[64,1024]{1,0:T(8,128)(2,1)S(1)}, bf16[64,1024]{1,0:T(8,128)(2,1)S(1)}, u32[]{:S(2)}, u32[]{:S(2)}) collective-permute-start(bf16[64,1024]{1,0:T(8,128)(2,1)S(1)} %get-tuple-element.40), channel_id=1, source_target_pairs={{0,136},{8,0},{128,8},{136,128},{1,137},{9,1},{129,9},{137,129},{2... | collective-permute-start | bytes 393224 | tf_op jit(solution)/shard_map/ppermute | solution.py:303

commit v2 on v1

--- a/solution.py
+++ b/solution.py
@@ -20,6 +20,7 @@
 AXES = ("yh", "z", "yl", "x", "c")
 VMEM = pl.BlockSpec(memory_space=pltpu.VMEM)
 SMEM = pl.BlockSpec(memory_space=pltpu.SMEM)
+ANY = pl.BlockSpec(memory_space=pl.ANY)
 
 
 def prep_kernel(kv_ref, out_ref):
@@ -88,8 +89,8 @@
         return (None, None) if masks is None else masks(w, i)
 
     if fast:
-        todo = [(w, i, hq) for i in range(2) for w in range(2) for hq in range(2)]
-        ahead = 2
+        todo = [(w, i, hq) for i in range(2) for w in range(len(q_refs)) for hq in range(2)]
+        ahead = 4
         scores = [qk(k_blk, rows_of(q_refs[w], y, 2 * tp + i, hq)) for w, i, hq in todo[:ahead]]
         for n, (w, i, hq) in enumerate(todo):
             if n + ahead < len(todo):
@@ -103,7 +104,7 @@
             m_new = jnp.maximum(st_refs[w][t, hq, ROW_M, :], bound)
             finish_piece(st_refs[w], t, hq, vt_blk, scores[n], m_new, mask)
         return
-    for w in range(2):
+    for w in range(len(q_refs)):
 
         def body(n, carry, w=w):
             i, hq = n // 2, n % 2
@@ -154,7 +155,8 @@
                 st_ref[t, hq, ROW_M, :] = jnp.full((1, 256), NEG, jnp.float32)
                 st_ref[t, hq, ROW_L, :] = jnp.zeros((1, 256), jnp.float32)
                 st_ref[t, hq, ROW_Q, :] = qn
-    st0[0, 0, ROW_W, :] = jnp.broadcast_to(jnp.max(widest, axis=1, keepdims=True), (1, 256))
+    for st_ref in (st0, st1):
+        st_ref[0, 0, ROW_W, :] = jnp.broadcast_to(jnp.max(widest, axis=1, keepdims=True), (1, 256))
 
     row = lax.broadcasted_iota(jnp.int32, (1, 256), 1) % STRIP
     key = lax.broadcasted_iota(jnp.int32, (512, 1), 0)
@@ -175,9 +177,9 @@
     both_ways(is_fast(st0, [(ch_ref, 2)]), run)
 
 
-def step_kernel(parts, sc_ref, q0, q1, *refs):
-    n = len(parts)
-    chunks, refs = refs[:n], ((q0, q1), refs[n + 2 : n + 4], sc_ref[0])
+def step_kernel(parts, n_rows, sc_ref, *refs):
+    q_refs, refs = refs[:n_rows], refs[n_rows:]
+    chunks, refs = refs[: len(parts)], (q_refs, refs[-n_rows:], sc_ref[0])
 
     def run(fast):
         for ch_ref, (halves, at) in zip(chunks, parts):
@@ -207,14 +209,14 @@
     return pl.CostEstimate(flops=4 * work * DH, bytes_accessed=6000000, transcendentals=work)
 
 
-def small(kernel, out_shape, n_in, scalars=True):
-    outs = jax.tree.map(lambda _: VMEM, out_shape)
+def small(kernel, out_shape, n_in, scalars=True, in_space=VMEM, out_space=VMEM, scratch=(), limit=12):
     return pl.pallas_call(
         kernel,
         out_shape=out_shape,
-        in_specs=[SMEM] * scalars + [VMEM] * n_in,
-        out_specs=outs,
-        compiler_params=pltpu.CompilerParams(vmem_limit_bytes=12 * 1024 * 1024),
+        in_specs=[SMEM] * scalars + [in_space] * n_in,
+        out_specs=jax.tree.map(lambda _: out_space, out_shape),
+        scratch_shapes=scratch,
+        compiler_params=pltpu.CompilerParams(vmem_limit_bytes=limit * 1024 * 1024),
         cost_estimate=pl.CostEstimate(flops=1000000, bytes_accessed=1000000, transcendentals=0),
     )
 
@@ -231,21 +233,26 @@
     )(sc, q0, q1, chunk)
 
 
-def ring_step(sc, q0, q1, state, chunks, parts):
-    n = len(chunks)
+def ring_step(sc, qs, state, chunks, parts):
+    n, n_rows = len(chunks), len(qs)
     return pl.pallas_call(
-        functools.partial(step_kernel, parts),
-        out_shape=ST,
-        in_specs=[SMEM, VMEM, VMEM] + [VMEM] * (n + 2),
-        out_specs=(VMEM,) * 2,
-        input_output_aliases={3 + n + i: i for i in range(2)},
+        functools.partial(step_kernel, parts, n_rows),
+        out_shape=ST[:n_rows],
+        in_specs=[SMEM] + [VMEM] * (n + 2 * n_rows),
+        out_specs=(VMEM,) * n_rows,
+        input_output_aliases={1 + n_rows + n + i: i for i in range(n_rows)},
         name="ring",
         compiler_params=pltpu.CompilerParams(vmem_limit_bytes=24 * 1024 * 1024),
-        cost_estimate=cost(8),
-    )(sc, q0, q1, *chunks, *state)
-
-
-def kv_send_kernel(k_ref, v_ref, out_ref):
+        cost_estimate=cost(2 * n * n_rows),
+    )(sc, *qs, *chunks, *state)
+
+
+def kv_send_kernel(k_hbm, v_hbm, out_ref, k_ref, v_ref, sems):
+    copies = [pltpu.make_async_copy(a, b, sems.at[i]) for i, (a, b) in enumerate(((k_hbm, k_ref), (v_hbm, v_ref)))]
+    for copy in copies:
+        copy.start()
+    for copy in copies:
+        copy.wait()
     for g in range(KV):
         k, v = k_ref[:, g * DH : (g + 1) * DH], v_ref[:, g * DH : (g + 1) * DH]
         for i in range(4):
@@ -281,9 +288,16 @@
 
 
 def place_kernel(sc_ref, *refs):
+    pieces, out_hbm, sems = refs[:4], refs[4], refs[5]
+    copies = []
     for d in range(4):
-        at = jnp.bitwise_and(sc_ref[0] - d + 4, 3)
-        refs[4][:, pl.ds(pl.multiple_of(at * 8 * DH, 8 * DH), 8 * DH)] = refs[d][...]
+        at = jnp.bitwise_and(sc_ref[0] - d + 4, 3) * (8 * DH)
+        columns = pl.ds(pl.multiple_of(at, 8 * DH), 8 * DH)
+        copies.append(pltpu.make_async_copy(pieces[d], out_hbm.at[:, columns], sems.at[d]))
+    for copy in copies:
+        copy.start()
+    for copy in copies:
+        copy.wait()
 
 
 def per_device(queries, keys, values):
@@ -306,7 +320,8 @@
     bf16 = jnp.bfloat16
     piece = jax.ShapeDtypeStruct((STRIP, 8 * DH), bf16)
     sent = jax.ShapeDtypeStruct((16, 2 * STRIP, DH), bf16)
-    kv = small(kv_send_kernel, sent, 2, False)(keys, values)
+    held = [pltpu.VMEM((STRIP, KV * DH), bf16)] * 2 + [pltpu.SemaphoreType.DMA((2,))]
+    kv = small(kv_send_kernel, sent, 2, False, ANY, VMEM, held, 63)(keys, values)
     kv = lax.all_to_all(kv, ("yh", "yl", "x"), split_axis=0, concat_axis=0, tiled=True)
     q_pieces = regroup(small(q_send_kernel, (piece,) * 4, 1)(sc, queries))
     q0 = small(join_kernel, jax.ShapeDtypeStruct((4, STRIP, 8 * DH), bf16), 4, False)(*q_pieces)
@@ -323,12 +338,15 @@
     state = own_step(sc, q0, q1, chunk)
     for k in range(1, 4):
         parts = (((0, 1), 2 + k), ((0, 1), 6 + k))
-        state = ring_step(sc, q0, q1, state, (fwd[k], bwd[k]), parts)
-    state = ring_step(sc, q0, q1, state, (far_l, far_h), (((0,), 6), ((1,), 6)))
-    other = lax.ppermute(state[1], "c", swap)
-    pieces = small(merge_kernel, (piece,) * 4, 2)(sc, state[0], other)
+        state = ring_step(sc, (q0, q1), state, (fwd[k], bwd[k]), parts)
+    far = ((far_l, far_h), (((0,), 6), ((1,), 6)))
+    (theirs,) = ring_step(sc, (q1,), state[1:], *far)
+    other = lax.ppermute(theirs, "c", swap)
+    (ours,) = ring_step(sc, (q0,), state[:1], *far)
+    pieces = small(merge_kernel, (piece,) * 4, 2)(sc, ours, other)
     out = jax.ShapeDtypeStruct((STRIP, H * DH), bf16)
-    return small(place_kernel, out, 4)(sc, *regroup(pieces))
+    sems = [pltpu.SemaphoreType.DMA((4,))]
+    return small(place_kernel, out, 4, True, VMEM, ANY, sems)(sc, *regroup(pieces))
 
 
 def solution(mesh):

time: 157 us -> 156 us (level)
  local copies, waits for them, and re-layouts: 1.81 us -> 0.13 us
  waiting for transfers between devices: 17.7 us -> 16.1 us
    ppermute x3, waiting for transfers between devices: 0.01 us -> 7.27 us  [per_device(): fwd.append(lax.ppermute(fwd[-1], 'z', up))]
    ppermute x3, waiting for transfers between devices: 6.9 us -> 0.61 us  [per_device(): bwd.append(lax.ppermute(bwd[-1], 'z', down))]
    ppermute x3, starting transfers between devices: 8.7 us -> 4.37 us  [per_device(): fwd.append(lax.ppermute(fwd[-1], 'z', up))]
    ppermute x1, waiting for transfers between devices: 2.38 us -> 0.01 us  [per_device(): other = lax.ppermute(theirs, 'c', swap)]
    ppermute x1, starting transfers between devices: 15.9 us -> 17.9 us  [per_device(): far_h = lax.ppermute(bwd[3][HALF:], 'z', down)]
    ppermute x1, starting transfers between devices: 25.5 us -> 27.3 us  [per_device(): other = lax.ppermute(theirs, 'c', swap)]
    unnamed x6 -> x2, local copies, waits for them, and re-layouts: 1.68 us -> 0.01 us
    pallas_call x7 -> x8, Pallas kernels: 50.2 us -> 51.3 us  [the longest x5 47.3 us: ring_step(): pl.pallas_call(functools.partial(step_kernel, parts, n_rows), out_shape=S...]
  transfers between devices with their start and end apart: 16 -> 16, of which waited for: 9 -> 9; matrix products, arithmetic and copies ran while one was open for 0% -> 0% of each run, Pallas kernels for 32% -> 33%
where the time goes in v2:
time: 156 us; the launch traced here: 153 us
  starting transfers between devices  62.8 us (40%)
  Pallas kernels  57.4 us (37%)
  blocking collectives  16.4 us (11%)
  waiting for transfers between devices  16.1 us (10%)
    pallas_call x5, Pallas kernels, ring_step(): pl.pallas_call(functools.partial(step_kernel, parts, n_rows), out_shape=S...  47.3 us
    ppermute x1, starting transfers between devices, per_device(): other = lax.ppermute(theirs, 'c', swap)  27.3 us
    ppermute x1, starting transfers between devices, per_device(): far_h = lax.ppermute(bwd[3][HALF:], 'z', down)  17.9 us
    all_to_all x1, blocking collectives, per_device(): lax.all_to_all(kv, ('yh', 'yl', 'x'), split_axis=0, concat_axis=0, tiled=...  16.4 us
    ppermute x6, starting transfers between devices, regroup(): lax.ppermute(pieces[d], ('yh', 'yl'), [(i, (i + d) % ny) for i in range(n...  10.5 us
    ppermute x6, waiting for transfers between devices, regroup(): lax.ppermute(pieces[d], ('yh', 'yl'), [(i, (i + d) % ny) for i in range(n...  8.17 us
    ppermute x3, waiting for transfers between devices, per_device(): fwd.append(lax.ppermute(fwd[-1], 'z', up))  7.27 us
    pallas_call x1, Pallas kernels, own_step(): pl.pallas_call(own_kernel, out_shape=ST, in_specs=[SMEM, VMEM, VMEM, VMEM...  5.2 us
  transfers between devices with their start and end apart: 16, of which 9 were waited for; matrix products, arithmetic and copies ran while one was open for 0% of the time, Pallas kernels for 33%

profile of v2, /device:TPU:240, one launch (start us, length us, event | category | flops | bytes accessed | tf_op | source)
XLA Modules:
  0.0 153.1 jit_solution(14648207738075760949)
XLA Ops:
  0.0 1.7 %shard_map.39 = bf16[16,128,128]{2,1,0:T(8,128)(2,1)} custom-call(bf16[64,512]{1,0:T(8,128)(2,1)} %k_hbm.1, bf16[64,512]{1,0:T(8,128)(2,1)} %v_hbm.1), custom_call_target="tpu_custom_call" | custom-call | flops 1000000 | bytes 1000000 | tf_op jit(solution)/shard_map/pallas_call | solution.py:324
  1.8 0.0 copy-start
  1.8 16.4 %all_to_all.5.kv_ref = bf16[16,128,128]{2,1,0:T(8,128)(2,1)S(1)} all-to-all(bf16[16,128,128]{2,1,0:T(8,128)(2,1)} %shard_map.39), channel_id=1, replica_groups=mesh['yh'=2,'z'=8,'yl'=2,'x'=4,'c'=2] {'yh','yl','x'}, dimensions={0} | all-to-all | bytes 1048576 | tf_op jit(solution)/shard_map/all_to_all | solution.py:325
  18.1 0.3 prep.1.ch_ref
  18.4 0.1 collective-permute-start.3
  18.5 2.0 %collective-permute-start.7 = (bf16[2080,128]{1,0:T(8,128)(2,1)S(1)}, bf16[2080,128]{1,0:T(8,128)(2,1)S(1)}, u32[]{:S(2)}, u32[]{:S(2)}) collective-permute-start(bf16[2080,128]{1,0:T(8,128)(2,1)S(1)} %prep.1.ch_ref), channel_id=1, source_target_pairs={{0,112},{16,0},{32,16},{48,32},{64,48},{80,64},{96,80},{112,96},{1... | collective-permute-start | bytes 1597448 | tf_op jit(solution)/shard_map/ppermute | solution.py:334
  20.6 0.1 stack.79.sc_ref
  20.6 0.0 copy-done
  20.6 0.6 shard_map.37
  21.2 1.5 %collective-permute-start = (bf16[64,1024]{1,0:T(8,128)(2,1)S(1)}, bf16[64,1024]{1,0:T(8,128)(2,1)S(1)}, u32[]{:S(2)}, u32[]{:S(2)}) collective-permute-start(bf16[64,1024]{1,0:T(8,128)(2,1)S(1)} %get-tuple-element.22), channel_id=1, source_target_pairs={{0,8},{8,128},{128,136},{136,0},{1,9},{9,129},{129,137},{137,1},{2... | collective-permute-start | bytes 393224 | tf_op jit(solution)/shard_map/ppermute | solution.py:317
  22.8 1.3 collective-permute-start.1
  24.1 2.5 %collective-permute-start.2 = (bf16[64,1024]{1,0:T(8,128)(2,1)S(1)}, bf16[64,1024]{1,0:T(8,128)(2,1)S(1)}, u32[]{:S(2)}, u32[]{:S(2)}) collective-permute-start(bf16[64,1024]{1,0:T(8,128)(2,1)S(1)} %get-tuple-element.24), channel_id=1, source_target_pairs={{0,136},{8,0},{128,8},{136,128},{1,137},{9,1},{129,9},{137,129},{2... | collective-permute-start | bytes 393224 | tf_op jit(solution)/shard_map/ppermute | solution.py:317
  26.6 1.0 collective-permute-done.b_ref
  27.6 1.7 %collective-permute-done.1.c_ref = bf16[64,1024]{1,0:T(8,128)(2,1)S(1)} collective-permute-done((bf16[64,1024]{1,0:T(8,128)(2,1)S(1)}, bf16[64,1024]{1,0:T(8,128)(2,1)S(1)}, u32[]{:S(2)}, u32[]{:S(2)}) %collective-permute-start.1) | collective-permute-done | bytes 131104 | tf_op jit(solution)/shard_map/ppermute | solution.py:317
  29.2 0.5 collective-permute-done.2.d_ref
  29.8 0.1 collective-permute-start.11
  29.9 1.6 %collective-permute-done.3.refs_2_ = bf16[2080,128]{1,0:T(8,128)(2,1)S(1)} collective-permute-done((bf16[2080,128]{1,0:T(8,128)(2,1)S(1)}, bf16[2080,128]{1,0:T(8,128)(2,1)S(1)}, u32[]{:S(2)}, u32[]{:S(2)}) %collective-permute-start.3) | collective-permute-done | bytes 532512 | tf_op jit(solution)/shard_map/ppermute | solution.py:333
  31.6 1.5 collective-permute-start.4
  33.1 0.0 collective-permute-done.7.refs_3_
  33.1 0.5 collective-permute-start.8
  33.6 0.0 collective-permute-done.11.q1.refs_1_.refs_0_
  33.6 5.2 %own.1 = (f32[4,2,136,256]{3,2,1,0:T(8,128)S(1)}, f32[4,2,136,256]{3,2,1,0:T(8,128)S(1)}) custom-call(s32[11]{0:T(128)S(1)} %stack.79.sc_ref, bf16[4,64,1024]{2,1,0:T(8,128)(2,1)S(1)} %shard_map.38.q0.refs_0_, bf16[4,64,1024]{2,1,0:T(8,128)(2,1)S(1)} %collective-permute-done.11.q1.refs_1_.refs_0_, bf16[2080,128]{1,0:T(8,128)(2,1)S(1)} %prep.1.ch_ref), custom_call_target="tpu_custom_call" | custom-call | flops 3221225472 | bytes 6000000 | tf_op jit(solution)/shard_map/own/pallas_call | solution.py:225
  38.8 5.6 %collective-permute-done.4.refs_2_ = bf16[2080,128]{1,0:T(8,128)(2,1)S(1)} collective-permute-done((bf16[2080,128]{1,0:T(8,128)(2,1)S(1)}, bf16[2080,128]{1,0:T(8,128)(2,1)S(1)}, u32[]{:S(2)}, u32[]{:S(2)}) %collective-permute-start.4) | collective-permute-done | bytes 532512 | tf_op jit(solution)/shard_map/ppermute | solution.py:333
  44.4 2.8 %collective-permute-start.5 = (bf16[2080,128]{1,0:T(8,128)(2,1)S(1)}, bf16[2080,128]{1,0:T(8,128)(2,1)S(1)}, u32[]{:S(2)}, u32[]{:S(2)}) collective-permute-start(bf16[2080,128]{1,0:T(8,128)(2,1)S(1)} %collective-permute-done.4.refs_2_), channel_id=1, source_target_pairs={{0,16},{16,32},{32,48},{48,64},{64,80},{80,96},{96,112},{112,0},{1... | collective-permute-start | bytes 1597448 | tf_op jit(solution)/shard_map/ppermute | solution.py:333
  47.2 0.0 collective-permute-done.8.refs_3_
  47.2 0.0 collective-permute-start.9
  47.2 7.2 %ring.5 = (f32[4,2,136,256]{3,2,1,0:T(8,128)S(1)}, f32[4,2,136,256]{3,2,1,0:T(8,128)S(1)}) custom-call(s32[11]{0:T(128)S(1)} %stack.79.sc_ref, bf16[4,64,1024]{2,1,0:T(8,128)(2,1)S(1)} %shard_map.38.q0.refs_0_, bf16[4,64,1024]{2,1,0:T(8,128)(2,1)S(1)} %collective-permute-done.11.q1.refs_1_.refs_0_, ...), custom_call_target="tpu_custom_call", output_to_operand_aliasing={{0}: (5, {}), {1}: (6, {})} | custom-call | flops 4294967296 | bytes 6000000 | tf_op jit(solution)/shard_map/ring/pallas_call | solution.py:238
  54.4 7.1 %ring.6 = (f32[4,2,136,256]{3,2,1,0:T(8,128)S(1)}, f32[4,2,136,256]{3,2,1,0:T(8,128)S(1)}) custom-call(s32[11]{0:T(128)S(1)} %stack.79.sc_ref, bf16[4,64,1024]{2,1,0:T(8,128)(2,1)S(1)} %shard_map.38.q0.refs_0_, bf16[4,64,1024]{2,1,0:T(8,128)(2,1)S(1)} %collective-permute-done.11.q1.refs_1_.refs_0_, ...), custom_call_target="tpu_custom_call", output_to_operand_aliasing={{0}: (5, {}), {1}: (6, {})} | custom-call | flops 4294967296 | bytes 6000000 | tf_op jit(solution)/shard_map/ring/pallas_call | solution.py:238
  61.5 0.6 collective-permute-done.9.refs_3_
  62.1 17.9 %collective-permute-start.10 = (bf16[1040,128]{1,0:T(8,128)(2,1)S(1)}, bf16[1040,128]{1,0:T(8,128)(2,1)S(1)}, u32[]{:S(2)}, u32[]{:S(2)}) collective-permute-start(bf16[1040,128]{1,0:T(8,128)(2,1)S(1)} %slice.9), channel_id=1, source_target_pairs={{0,112},{16,0},{32,16},{48,32},{64,48},{80,64},{96,80},{112,96},{1... | collective-permute-start | bytes 798728 | tf_op jit(solution)/shard_map/ppermute | solution.py:336
  80.0 0.0 collective-permute-done.5.refs_2_
  80.1 0.1 collective-permute-start.6
  80.1 27.5 %ring.7 = (f32[4,2,136,256]{3,2,1,0:T(8,128)S(1)}, f32[4,2,136,256]{3,2,1,0:T(8,128)S(1)}) custom-call(s32[11]{0:T(128)S(1)} %stack.79.sc_ref, bf16[4,64,1024]{2,1,0:T(8,128)(2,1)S(1)} %shard_map.38.q0.refs_0_, bf16[4,64,1024]{2,1,0:T(8,128)(2,1)S(1)} %collective-permute-done.11.q1.refs_1_.refs_0_, ...), custom_call_target="tpu_custom_call", output_to_operand_aliasing={{0}: (5, {}), {1}: (6, {})} | custom-call | flops 4294967296 | bytes 6000000 | tf_op jit(solution)/shard_map/ring/pallas_call | solution.py:238
  107.6 0.0 collective-permute-done.10.refs_2_
  107.6 0.0 collective-permute-done.6.refs_1_
  107.6 2.9 %ring.9 = f32[4,2,136,256]{3,2,1,0:T(8,128)S(1)} custom-call(s32[11]{0:T(128)S(1)} %stack.79.sc_ref, bf16[4,64,1024]{2,1,0:T(8,128)(2,1)S(1)} %collective-permute-done.11.q1.refs_1_.refs_0_, bf16[1040,128]{1,0:T(8,128)(2,1)S(1)} %collective-permute-done.6.refs_1_, ...), custom_call_target="tpu_custom_call", output_to_operand_aliasing={{}: (4, {})} | custom-call | flops 2147483648 | bytes 6000000 | tf_op jit(solution)/shard_map/ring/pallas_call | solution.py:238
  110.6 27.3 %collective-permute-start.12 = (f32[4,2,136,256]{3,2,1,0:T(8,128)S(1)}, f32[4,2,136,256]{3,2,1,0:T(8,128)S(1)}, u32[]{:S(2)}, u32[]{:S(2)}) collective-permute-start(f32[4,2,136,256]{3,2,1,0:T(8,128)S(1)} %ring.9), channel_id=1, source_target_pairs={{0,1},{1,0},{2,3},{3,2},{4,5},{5,4},{6,7},{7,6},{8,9},{9,8},{10,11... | collective-permute-start | bytes 3342344 | tf_op jit(solution)/shard_map/ppermute | solution.py:344
  137.9 2.7 %ring.8.s_ref = f32[4,2,136,256]{3,2,1,0:T(8,128)S(1)} custom-call(s32[11]{0:T(128)S(1)} %stack.79.sc_ref, bf16[4,64,1024]{2,1,0:T(8,128)(2,1)S(1)} %shard_map.38.q0.refs_0_, bf16[1040,128]{1,0:T(8,128)(2,1)S(1)} %collective-permute-done.6.refs_1_, bf16[1040,128]{1,0:T(8,128)(2,1)S(1)} %collective-permute-done.10.refs_2_, ...), custom_call_target="tpu_custom_call", output_to_operand_aliasing={{}: (4, {})} | custom-call | flops 2147483648 | bytes 6000000 | tf_op jit(solution)/shard_map/ring/pallas_call | solution.py:238
  140.6 0.0 collective-permute-done.12.r_ref
  140.6 0.9 shard_map.40
  141.4 3.0 %collective-permute-start.13 = (bf16[64,1024]{1,0:T(8,128)(2,1)S(1)}, bf16[64,1024]{1,0:T(8,128)(2,1)S(1)}, u32[]{:S(2)}, u32[]{:S(2)}) collective-permute-start(bf16[64,1024]{1,0:T(8,128)(2,1)S(1)} %get-tuple-element.34), channel_id=1, source_target_pairs={{0,8},{8,128},{128,136},{136,0},{1,9},{9,129},{129,137},{137,1},{2... | collective-permute-start | bytes 393224 | tf_op jit(solution)/shard_map/ppermute | solution.py:317
  144.4 0.1 collective-permute-start.14
  144.5 2.1 %collective-permute-start.15 = (bf16[64,1024]{1,0:T(8,128)(2,1)S(1)}, bf16[64,1024]{1,0:T(8,128)(2,1)S(1)}, u32[]{:S(2)}, u32[]{:S(2)}) collective-permute-start(bf16[64,1024]{1,0:T(8,128)(2,1)S(1)} %get-tuple-element.36), channel_id=1, source_target_pairs={{0,136},{8,0},{128,8},{136,128},{1,137},{9,1},{129,9},{137,129},{2... | collective-permute-start | bytes 393224 | tf_op jit(solution)/shard_map/ppermute | solution.py:317
  146.6 1.8 %collective-permute-done.13.refs_1_ = bf16[64,1024]{1,0:T(8,128)(2,1)S(1)} collective-permute-done((bf16[64,1024]{1,0:T(8,128)(2,1)S(1)}, bf16[64,1024]{1,0:T(8,128)(2,1)S(1)}, u32[]{:S(2)}, u32[]{:S(2)}) %collective-permute-start.13) | collective-permute-done | bytes 131104 | tf_op jit(solution)/shard_map/ppermute | solution.py:317
  148.3 2.8 %collective-permute-done.14.refs_2_ = bf16[64,1024]{1,0:T(8,128)(2,1)S(1)} collective-permute-done((bf16[64,1024]{1,0:T(8,128)(2,1)S(1)}, bf16[64,1024]{1,0:T(8,128)(2,1)S(1)}, u32[]{:S(2)}, u32[]{:S(2)}) %collective-permute-start.14) | collective-permute-done | bytes 131104 | tf_op jit(solution)/shard_map/ppermute | solution.py:317
  151.1 0.5 collective-permute-done.15.refs_3_
  151.6 1.4 shard_map.41
  (3 shorter events, 0.1 us)
Async XLA Ops:
  1.8 18.9 %copy-start = (bf16[64,4096]{1,0:T(8,128)(2,1)S(1)}, bf16[64,4096]{1,0:T(8,128)(2,1)}, u32[]{:S(2)}) copy-start(bf16[64,4096]{1,0:T(8,128)(2,1)} %q_ref.1) | copy-start | bytes 1572868
  18.4 13.1 %collective-permute-start.3 = (bf16[2080,128]{1,0:T(8,128)(2,1)S(1)}, bf16[2080,128]{1,0:T(8,128)(2,1)S(1)}, u32[]{:S(2)}, u32[]{:S(2)}) collective-permute-start(bf16[2080,128]{1,0:T(8,128)(2,1)S(1)} %prep.1.ch_ref), channel_id=1, source_target_pairs={{0,16},{16,32},{32,48},{48,64},{64,80},{80,96},{96,112},{112,0},{1... | collective-permute-start | bytes 1597448 | tf_op jit(solution)/shard_map/ppermute | solution.py:333
  18.5 14.5 %collective-permute-start.7 = (bf16[2080,128]{1,0:T(8,128)(2,1)S(1)}, bf16[2080,128]{1,0:T(8,128)(2,1)S(1)}, u32[]{:S(2)}, u32[]{:S(2)}) collective-permute-start(bf16[2080,128]{1,0:T(8,128)(2,1)S(1)} %prep.1.ch_ref), channel_id=1, source_target_pairs={{0,112},{16,0},{32,16},{48,32},{64,48},{80,64},{96,80},{112,96},{1... | collective-permute-start | bytes 1597448 | tf_op jit(solution)/shard_map/ppermute | solution.py:334
  21.2 6.4 %collective-permute-start = (bf16[64,1024]{1,0:T(8,128)(2,1)S(1)}, bf16[64,1024]{1,0:T(8,128)(2,1)S(1)}, u32[]{:S(2)}, u32[]{:S(2)}) collective-permute-start(bf16[64,1024]{1,0:T(8,128)(2,1)S(1)} %get-tuple-element.22), channel_id=1, source_target_pairs={{0,8},{8,128},{128,136},{136,0},{1,9},{9,129},{129,137},{137,1},{2... | collective-permute-start | bytes 393224 | tf_op jit(solution)/shard_map/ppermute | solution.py:317
  22.8 6.5 %collective-permute-start.1 = (bf16[64,1024]{1,0:T(8,128)(2,1)S(1)}, bf16[64,1024]{1,0:T(8,128)(2,1)S(1)}, u32[]{:S(2)}, u32[]{:S(2)}) collective-permute-start(bf16[64,1024]{1,0:T(8,128)(2,1)S(1)} %get-tuple-element.23), channel_id=1, source_target_pairs={{0,128},{8,136},{128,0},{136,8},{1,129},{9,137},{129,1},{137,9},{2... | collective-permute-start | bytes 393224 | tf_op jit(solution)/shard_map/ppermute | solution.py:317
  24.1 5.7 %collective-permute-start.2 = (bf16[64,1024]{1,0:T(8,128)(2,1)S(1)}, bf16[64,1024]{1,0:T(8,128)(2,1)S(1)}, u32[]{:S(2)}, u32[]{:S(2)}) collective-permute-start(bf16[64,1024]{1,0:T(8,128)(2,1)S(1)} %get-tuple-element.24), channel_id=1, source_target_pairs={{0,136},{8,0},{128,8},{136,128},{1,137},{9,1},{129,9},{137,129},{2... | collective-permute-start | bytes 393224 | tf_op jit(solution)/shard_map/ppermute | solution.py:317
  29.8 3.8 %collective-permute-start.11 = (bf16[4,64,1024]{2,1,0:T(8,128)(2,1)S(1)}, bf16[4,64,1024]{2,1,0:T(8,128)(2,1)S(1)}, u32[]{:S(2)}, u32[]{:S(2)}) collective-permute-start(bf16[4,64,1024]{2,1,0:T(8,128)(2,1)S(1)} %shard_map.38.q0.refs_0_), channel_id=1, source_target_pairs={{0,1},{1,0},{2,3},{3,2},{4,5},{5,4},{6,7},{7,6},{8,9},{9,8},{10,11... | collective-permute-start | bytes 1572872 | tf_op jit(solution)/shard_map/ppermute | solution.py:328
  31.6 12.9 %collective-permute-start.4 = (bf16[2080,128]{1,0:T(8,128)(2,1)S(1)}, bf16[2080,128]{1,0:T(8,128)(2,1)S(1)}, u32[]{:S(2)}, u32[]{:S(2)}) collective-permute-start(bf16[2080,128]{1,0:T(8,128)(2,1)S(1)} %collective-permute-done.3.refs_2_), channel_id=1, source_target_pairs={{0,16},{16,32},{32,48},{48,64},{64,80},{80,96},{96,112},{112,0},{1... | collective-permute-start | bytes 1597448 | tf_op jit(solution)/shard_map/ppermute | solution.py:333
  33.1 14.2 %collective-permute-start.8 = (bf16[2080,128]{1,0:T(8,128)(2,1)S(1)}, bf16[2080,128]{1,0:T(8,128)(2,1)S(1)}, u32[]{:S(2)}, u32[]{:S(2)}) collective-permute-start(bf16[2080,128]{1,0:T(8,128)(2,1)S(1)} %collective-permute-done.7.refs_3_), channel_id=1, source_target_pairs={{0,112},{16,0},{32,16},{48,32},{64,48},{80,64},{96,80},{112,96},{1... | collective-permute-start | bytes 1597448 | tf_op jit(solution)/shard_map/ppermute | solution.py:334
  44.4 35.6 %collective-permute-start.5 = (bf16[2080,128]{1,0:T(8,128)(2,1)S(1)}, bf16[2080,128]{1,0:T(8,128)(2,1)S(1)}, u32[]{:S(2)}, u32[]{:S(2)}) collective-permute-start(bf16[2080,128]{1,0:T(8,128)(2,1)S(1)} %collective-permute-done.4.refs_2_), channel_id=1, source_target_pairs={{0,16},{16,32},{32,48},{48,64},{64,80},{80,96},{96,112},{112,0},{1... | collective-permute-start | bytes 1597448 | tf_op jit(solution)/shard_map/ppermute | solution.py:333
  47.2 14.9 %collective-permute-start.9 = (bf16[2080,128]{1,0:T(8,128)(2,1)S(1)}, bf16[2080,128]{1,0:T(8,128)(2,1)S(1)}, u32[]{:S(2)}, u32[]{:S(2)}) collective-permute-start(bf16[2080,128]{1,0:T(8,128)(2,1)S(1)} %collective-permute-done.8.refs_3_), channel_id=1, source_target_pairs={{0,112},{16,0},{32,16},{48,32},{64,48},{80,64},{96,80},{112,96},{1... | collective-permute-start | bytes 1597448 | tf_op jit(solution)/shard_map/ppermute | solution.py:334
  62.1 45.5 %collective-permute-start.10 = (bf16[1040,128]{1,0:T(8,128)(2,1)S(1)}, bf16[1040,128]{1,0:T(8,128)(2,1)S(1)}, u32[]{:S(2)}, u32[]{:S(2)}) collective-permute-start(bf16[1040,128]{1,0:T(8,128)(2,1)S(1)} %slice.9), channel_id=1, source_target_pairs={{0,112},{16,0},{32,16},{48,32},{64,48},{80,64},{96,80},{112,96},{1... | collective-permute-start | bytes 798728 | tf_op jit(solution)/shard_map/ppermute | solution.py:336
  80.1 27.6 %collective-permute-start.6 = (bf16[1040,128]{1,0:T(8,128)(2,1)S(1)}, bf16[1040,128]{1,0:T(8,128)(2,1)S(1)}, u32[]{:S(2)}, u32[]{:S(2)}) collective-permute-start(bf16[1040,128]{1,0:T(8,128)(2,1)S(1)} %slice.8), channel_id=1, source_target_pairs={{0,16},{16,32},{32,48},{48,64},{64,80},{80,96},{96,112},{112,0},{1... | collective-permute-start | bytes 798728 | tf_op jit(solution)/shard_map/ppermute | solution.py:335
  110.6 30.0 %collective-permute-start.12 = (f32[4,2,136,256]{3,2,1,0:T(8,128)S(1)}, f32[4,2,136,256]{3,2,1,0:T(8,128)S(1)}, u32[]{:S(2)}, u32[]{:S(2)}) collective-permute-start(f32[4,2,136,256]{3,2,1,0:T(8,128)S(1)} %ring.9), channel_id=1, source_target_pairs={{0,1},{1,0},{2,3},{3,2},{4,5},{5,4},{6,7},{7,6},{8,9},{9,8},{10,11... | collective-permute-start | bytes 3342344 | tf_op jit(solution)/shard_map/ppermute | solution.py:344
  141.4 6.9 %collective-permute-start.13 = (bf16[64,1024]{1,0:T(8,128)(2,1)S(1)}, bf16[64,1024]{1,0:T(8,128)(2,1)S(1)}, u32[]{:S(2)}, u32[]{:S(2)}) collective-permute-start(bf16[64,1024]{1,0:T(8,128)(2,1)S(1)} %get-tuple-element.34), channel_id=1, source_target_pairs={{0,8},{8,128},{128,136},{136,0},{1,9},{9,129},{129,137},{137,1},{2... | collective-permute-start | bytes 393224 | tf_op jit(solution)/shard_map/ppermute | solution.py:317
  144.4 6.7 %collective-permute-start.14 = (bf16[64,1024]{1,0:T(8,128)(2,1)S(1)}, bf16[64,1024]{1,0:T(8,128)(2,1)S(1)}, u32[]{:S(2)}, u32[]{:S(2)}) collective-permute-start(bf16[64,1024]{1,0:T(8,128)(2,1)S(1)} %get-tuple-element.35), channel_id=1, source_target_pairs={{0,128},{8,136},{128,0},{136,8},{1,129},{9,137},{129,1},{137,9},{2... | collective-permute-start | bytes 393224 | tf_op jit(solution)/shard_map/ppermute | solution.py:317
  144.5 7.1 %collective-permute-start.15 = (bf16[64,1024]{1,0:T(8,128)(2,1)S(1)}, bf16[64,1024]{1,0:T(8,128)(2,1)S(1)}, u32[]{:S(2)}, u32[]{:S(2)}) collective-permute-start(bf16[64,1024]{1,0:T(8,128)(2,1)S(1)} %get-tuple-element.36), channel_id=1, source_target_pairs={{0,136},{8,0},{128,8},{136,128},{1,137},{9,1},{129,9},{137,129},{2... | collective-permute-start | bytes 393224 | tf_op jit(solution)/shard_map/ppermute | solution.py:317

commit v3 on v2

--- a/solution.py
+++ b/solution.py
@@ -62,60 +62,77 @@
     return lax.dot_general(k_blk, rows, (((1,), (1,)), ((), ())), preferred_element_type=jnp.float32)
 
 
-def finish_piece(st_ref, t, hq, vt_blk, s, m_new, mask):
-    m_old = st_ref[t, hq, ROW_M, :]
-    l_old = st_ref[t, hq, ROW_L, :]
+def load_half(get, half):
+    base = pl.multiple_of(half * HALF, 16)
+    vt_blk = jnp.concatenate([get(base + 512 + b * 128, 128) for b in range(4)], axis=1)
+    kn = get(base + 1024, 16).astype(jnp.float32)[0:1, :]
+    return get(base, 512), vt_blk, jnp.concatenate([kn, kn], axis=1)
+
+
+def update(st_ref, t, hq, m_new, m_old, total, pv):
+    alpha = jnp.exp2(m_old - m_new)
+    st_ref[t, hq, ROW_M, :] = m_new
+    st_ref[t, hq, ROW_L, :] = alpha * st_ref[t, hq, ROW_L, :] + total
+    st_ref[t, hq, 0:DH, :] = alpha * st_ref[t, hq, 0:DH, :] + pv
+
+
+def weigh(vt_blk, s, m_new, mask):
     p = jnp.exp2(s * C2 - m_new)
     if mask is not None:
         p = jnp.where(mask, p, 0.0)
-    alpha = jnp.exp2(m_old - m_new)
     pv = lax.dot_general(
         vt_blk, p.astype(jnp.bfloat16), (((1,), (0,)), ((), ())), preferred_element_type=jnp.float32
     )
-    st_ref[t, hq, ROW_M, :] = m_new
-    st_ref[t, hq, ROW_L, :] = alpha * l_old + jnp.sum(p, axis=0, keepdims=True)
-    st_ref[t, hq, 0:DH, :] = alpha * st_ref[t, hq, 0:DH, :] + pv
-
-
-def unit(refs, ch_ref, half, tp, fast, masks=None):
+    return jnp.sum(p, axis=0, keepdims=True), pv
+
+
+def fast_unit(refs, get, halves, tp, masks=None):
     q_refs, st_refs, y = refs
-    base = pl.multiple_of(half * HALF, 16)
-    k_blk = ch_ref[pl.ds(base, 512), :]
-    vt_blk = jnp.concatenate([ch_ref[pl.ds(base + 512 + b * 128, 128), :] for b in range(4)], axis=1)
-    kn = ch_ref[pl.ds(base + 1024, 16), :].astype(jnp.float32)[0:1, :]
-    kn = jnp.concatenate([kn, kn], axis=1)
-
-    def mask_of(w, i):
-        return (None, None) if masks is None else masks(w, i)
-
-    if fast:
-        todo = [(w, i, hq) for i in range(2) for w in range(len(q_refs)) for hq in range(2)]
-        ahead = 4
-        scores = [qk(k_blk, rows_of(q_refs[w], y, 2 * tp + i, hq)) for w, i, hq in todo[:ahead]]
-        for n, (w, i, hq) in enumerate(todo):
-            if n + ahead < len(todo):
-                w2, i2, hq2 = todo[n + ahead]
-                scores.append(qk(k_blk, rows_of(q_refs[w2], y, 2 * tp + i2, hq2)))
-            t = 2 * tp + i
-            mask, some = mask_of(w, i)
-            bound = st_refs[w][t, hq, ROW_Q, :] * kn
-            if some is not None:
-                bound = jnp.where(some, bound, NEG)
-            m_new = jnp.maximum(st_refs[w][t, hq, ROW_M, :], bound)
-            finish_piece(st_refs[w], t, hq, vt_blk, scores[n], m_new, mask)
-        return
+    blocks = [load_half(get, half) for half in halves]
+    kn = functools.reduce(jnp.maximum, [b[2] for b in blocks])
+    todo = [(w, i, hq) for i in range(2) for w in range(len(q_refs)) for hq in range(2)]
+    items = [(p, b) for p in todo for b in range(len(blocks))]
+    scores = []
+
+    def issue(n):
+        if n < len(items):
+            (w, i, hq), b = items[n]
+            scores.append(qk(blocks[b][0], rows_of(q_refs[w], y, 2 * tp + i, hq)))
+
+    for n in range(4):
+        issue(n)
+    for n, (w, i, hq) in enumerate(todo):
+        t = 2 * tp + i
+        mask, some = (None, None) if masks is None else masks(w, i)
+        bound = st_refs[w][t, hq, ROW_Q, :] * kn
+        if some is not None:
+            bound = jnp.where(some, bound, NEG)
+        m_old = st_refs[w][t, hq, ROW_M, :]
+        m_new = jnp.maximum(m_old, bound)
+        total, pv = None, None
+        for b in range(len(blocks)):
+            at = n * len(blocks) + b
+            issue(at + 4)
+            part = weigh(blocks[b][1], scores[at], m_new, mask)
+            total, pv = part if b == 0 else (total + part[0], pv + part[1])
+        update(st_refs[w], t, hq, m_new, m_old, total, pv)
+
+
+def slow_unit(refs, get, half, tp, masks=None):
+    q_refs, st_refs, y = refs
+    k_blk, vt_blk, _ = load_half(get, half)
     for w in range(len(q_refs)):
 
         def body(n, carry, w=w):
             i, hq = n // 2, n % 2
             t = 2 * tp + i
-            mask, _ = mask_of(w, i)
+            mask = None if masks is None else masks(w, i)[0]
             s = qk(k_blk, rows_of(q_refs[w], y, t, hq))
             if mask is not None:
                 s = jnp.where(mask, s, NEG)
-            top = jnp.maximum(jnp.max(s, axis=0, keepdims=True) * C2, NEG)
-            m_new = jnp.maximum(st_refs[w][t, hq, ROW_M, :], top)
-            finish_piece(st_refs[w], t, hq, vt_blk, s, m_new, mask)
+            m_old = st_refs[w][t, hq, ROW_M, :]
+            m_new = jnp.maximum(m_old, jnp.maximum(jnp.max(s, axis=0, keepdims=True) * C2, NEG))
+            update(st_refs[w], t, hq, m_new, m_old, *weigh(vt_blk, s, m_new, mask))
             return carry
 
         lax.fori_loop(0, 4, body, 0)
@@ -131,10 +148,9 @@
         run(False)
 
 
-def is_fast(st_ref, chunks):
+def is_fast(st_ref, gets):
     kn = functools.reduce(
-        jnp.maximum,
-        [ch[h * HALF + 1024 : h * HALF + 1040, :].astype(jnp.float32) for ch, halves in chunks for h in range(halves)],
+        jnp.maximum, [get(h * HALF + 1024, 16).astype(jnp.float32) for get in gets for h in range(2)]
     )
     return jnp.max(kn[0:1, :] * st_ref[0, 0, ROW_W, 0:DH]) <= 60.0
 
@@ -166,39 +182,59 @@
         row_pos = i * 512 + x * 128 + (c if w == 0 else 1 - c) * STRIP + row
         return key_pos <= row_pos, c * STRIP <= row_pos
 
+    def get(at, n):
+        return ch_ref[pl.ds(at, n), :]
+
     def run(fast):
         def diagonal(h, carry):
-            unit(refs, ch_ref, h, h, fast, masks)
+            if fast:
+                fast_unit(refs, get, (h,), h, masks)
+            else:
+                slow_unit(refs, get, h, h, masks)
             return carry
 
         lax.fori_loop(0, 2, diagonal, 0)
-        unit(refs, ch_ref, 0, 1, fast)
-
-    both_ways(is_fast(st0, [(ch_ref, 2)]), run)
-
-
-def step_kernel(parts, n_rows, sc_ref, *refs):
-    q_refs, refs = refs[:n_rows], refs[n_rows:]
-    chunks, refs = refs[: len(parts)], (q_refs, refs[-n_rows:], sc_ref[0])
+        if fast:
+            fast_unit(refs, get, (0,), 1)
+        else:
+            slow_unit(refs, get, 0, 1)
+
+    both_ways(is_fast(st0, [get]), run)
+
+
+def step_kernel(n_chunks, first, n_rows, sc_ref, *refs):
+    q_refs, given, held = refs[:n_rows], refs[n_rows : n_rows + 2], refs[-1]
+    refs = (q_refs, refs[-1 - n_rows : -1], sc_ref[0])
+    if n_chunks == 2:
+        held[0], held[1] = given[0][...], given[1][...]
+    else:
+        held[0, :HALF, :], held[0, HALF:, :] = given[0][...], given[1][...]
+
+    def chunk(j):
+        return lambda at, n: held[j, pl.ds(at, n), :]
 
     def run(fast):
-        for ch_ref, (halves, at) in zip(chunks, parts):
-            before = sc_ref[at]
-
-            def body(u, carry, ch_ref=ch_ref, halves=halves):
-                if halves == (0, 1):
-                    half, tp = jnp.where(u == 1, 1, 0), jnp.where(u == 2, 0, 1)
-                elif halves == (0,):
-                    half, tp = 0, 1 - u
-                else:
-                    half, tp = 0, 1
-                unit(refs, ch_ref, half, tp, fast)
-                return carry
-
-            count = {(0, 1): 1 + 2 * before, (0,): 1 + before, (1,): before}[halves]
-            lax.fori_loop(0, count, body, 0)
-
-    both_ways(is_fast(refs[1][0], [(ch, len(p[0])) for ch, p in zip(chunks, parts)]), run)
+        def each(j, carry):
+            before = sc_ref[first + 4 * j]
+            if fast:
+
+                @pl.when(before == 1)
+                def _():
+                    fast_unit(refs, chunk(j), (0, 1), 1)
+
+                fast_unit(refs, chunk(j), (0,), 1 - before)
+            else:
+
+                def body(u, carry):
+                    slow_unit(refs, chunk(j), jnp.where(u == 1, 1, 0), jnp.where(u == 2, 0, 1))
+                    return carry
+
+                lax.fori_loop(0, 1 + 2 * before, body, 0)
+            return carry
+
+        lax.fori_loop(0, n_chunks, each, 0)
+
+    both_ways(is_fast(refs[1][0], [chunk(j) for j in range(n_chunks)]), run)
 
 
 ST = (jax.ShapeDtypeStruct((4, 2, DH + 8, 256), jnp.float32),) * 2
@@ -233,17 +269,18 @@
     )(sc, q0, q1, chunk)
 
 
-def ring_step(sc, qs, state, chunks, parts):
-    n, n_rows = len(chunks), len(qs)
+def ring_step(sc, qs, state, chunks, n_chunks, first):
+    n_rows = len(qs)
     return pl.pallas_call(
-        functools.partial(step_kernel, parts, n_rows),
+        functools.partial(step_kernel, n_chunks, first, n_rows),
         out_shape=ST[:n_rows],
-        in_specs=[SMEM] + [VMEM] * (n + 2 * n_rows),
+        in_specs=[SMEM] + [VMEM] * (2 + 2 * n_rows),
         out_specs=(VMEM,) * n_rows,
-        input_output_aliases={1 + n_rows + n + i: i for i in range(n_rows)},
+        input_output_aliases={3 + n_rows + i: i for i in range(n_rows)},
+        scratch_shapes=[pltpu.VMEM((n_chunks, 2 * HALF, DH), jnp.bfloat16)],
         name="ring",
         compiler_params=pltpu.CompilerParams(vmem_limit_bytes=24 * 1024 * 1024),
-        cost_estimate=cost(2 * n * n_rows),
+        cost_estimate=cost(2 * n_chunks * n_rows),
     )(sc, *qs, *chunks, *state)
 
 
@@ -337,9 +374,8 @@
 
     state = own_step(sc, q0, q1, chunk)
     for k in range(1, 4):
-        parts = (((0, 1), 2 + k), ((0, 1), 6 + k))
-        state = ring_step(sc, (q0, q1), state, (fwd[k], bwd[k]), parts)
-    far = ((far_l, far_h), (((0,), 6), ((1,), 6)))
+        state = ring_step(sc, (q0, q1), state, (fwd[k], bwd[k]), 2, 2 + k)
+    far = ((far_l, far_h), 1, 6)
     (theirs,) = ring_step(sc, (q1,), state[1:], *far)
     other = lax.ppermute(theirs, "c", swap)
     (ours,) = ring_step(sc, (q0,), state[:1], *far)

time: 156 us -> 156 us (level)
  no operation moved by 1% of the time
where the time goes in v3:
time: 156 us; the launch traced here: 153 us
  starting transfers between devices  63 us (40%)
  Pallas kernels  56.8 us (36%)
  waiting for transfers between devices  16.6 us (11%)
  blocking collectives  16.4 us (11%)
    pallas_call x5, Pallas kernels, ring_step(): pl.pallas_call(functools.partial(step_kernel, n_chunks, first, n_rows), o...  46.7 us
    ppermute x1, starting transfers between devices, per_device(): other = lax.ppermute(theirs, 'c', swap)  27.5 us
    ppermute x1, starting transfers between devices, per_device(): far_h = lax.ppermute(bwd[3][HALF:], 'z', down)  17.9 us
    all_to_all x1, blocking collectives, per_device(): lax.all_to_all(kv, ('yh', 'yl', 'x'), split_axis=0, concat_axis=0, tiled=...  16.4 us
    ppermute x6, starting transfers between devices, regroup(): lax.ppermute(pieces[d], ('yh', 'yl'), [(i, (i + d) % ny) for i in range(n...  10.5 us
    ppermute x6, waiting for transfers between devices, regroup(): lax.ppermute(pieces[d], ('yh', 'yl'), [(i, (i + d) % ny) for i in range(n...  8.34 us
    ppermute x3, waiting for transfers between devices, per_device(): fwd.append(lax.ppermute(fwd[-1], 'z', up))  7.3 us
    pallas_call x1, Pallas kernels, own_step(): pl.pallas_call(own_kernel, out_shape=ST, in_specs=[SMEM, VMEM, VMEM, VMEM...  5.17 us
  transfers between devices with their start and end apart: 16, of which 9 were waited for; matrix products, arithmetic and copies ran while one was open for 0% of the time, Pallas kernels for 33%

profile of v3, /device:TPU:240, one launch (start us, length us, event | category | flops | bytes accessed | tf_op | source)
XLA Modules:
  0.0 153.2 jit_solution(17055829681870745734)
XLA Ops:
  0.0 1.7 %shard_map.39 = bf16[16,128,128]{2,1,0:T(8,128)(2,1)} custom-call(bf16[64,512]{1,0:T(8,128)(2,1)} %k_hbm.1, bf16[64,512]{1,0:T(8,128)(2,1)} %v_hbm.1), custom_call_target="tpu_custom_call" | custom-call | flops 1000000 | bytes 1000000 | tf_op jit(solution)/shard_map/pallas_call | solution.py:361
  1.8 0.0 copy-start
  1.8 16.4 %all_to_all.5.kv_ref = bf16[16,128,128]{2,1,0:T(8,128)(2,1)S(1)} all-to-all(bf16[16,128,128]{2,1,0:T(8,128)(2,1)} %shard_map.39), channel_id=1, replica_groups=mesh['yh'=2,'z'=8,'yl'=2,'x'=4,'c'=2] {'yh','yl','x'}, dimensions={0} | all-to-all | bytes 1048576 | tf_op jit(solution)/shard_map/all_to_all | solution.py:362
  18.1 0.3 prep.1.ch_ref
  18.4 0.1 collective-permute-start.3
  18.5 2.0 %collective-permute-start.7 = (bf16[2080,128]{1,0:T(8,128)(2,1)S(1)}, bf16[2080,128]{1,0:T(8,128)(2,1)S(1)}, u32[]{:S(2)}, u32[]{:S(2)}) collective-permute-start(bf16[2080,128]{1,0:T(8,128)(2,1)S(1)} %prep.1.ch_ref), channel_id=1, source_target_pairs={{0,112},{16,0},{32,16},{48,32},{64,48},{80,64},{96,80},{112,96},{1... | collective-permute-start | bytes 1597448 | tf_op jit(solution)/shard_map/ppermute | solution.py:371
  20.6 0.1 stack.79.sc_ref
  20.6 0.0 copy-done
  20.6 0.6 shard_map.37
  21.2 1.5 %collective-permute-start = (bf16[64,1024]{1,0:T(8,128)(2,1)S(1)}, bf16[64,1024]{1,0:T(8,128)(2,1)S(1)}, u32[]{:S(2)}, u32[]{:S(2)}) collective-permute-start(bf16[64,1024]{1,0:T(8,128)(2,1)S(1)} %get-tuple-element.22), channel_id=1, source_target_pairs={{0,8},{8,128},{128,136},{136,0},{1,9},{9,129},{129,137},{137,1},{2... | collective-permute-start | bytes 393224 | tf_op jit(solution)/shard_map/ppermute | solution.py:354
  22.8 1.3 collective-permute-start.1
  24.1 2.5 %collective-permute-start.2 = (bf16[64,1024]{1,0:T(8,128)(2,1)S(1)}, bf16[64,1024]{1,0:T(8,128)(2,1)S(1)}, u32[]{:S(2)}, u32[]{:S(2)}) collective-permute-start(bf16[64,1024]{1,0:T(8,128)(2,1)S(1)} %get-tuple-element.24), channel_id=1, source_target_pairs={{0,136},{8,0},{128,8},{136,128},{1,137},{9,1},{129,9},{137,129},{2... | collective-permute-start | bytes 393224 | tf_op jit(solution)/shard_map/ppermute | solution.py:354
  26.6 1.0 collective-permute-done.b_ref
  27.6 1.7 %collective-permute-done.1.c_ref = bf16[64,1024]{1,0:T(8,128)(2,1)S(1)} collective-permute-done((bf16[64,1024]{1,0:T(8,128)(2,1)S(1)}, bf16[64,1024]{1,0:T(8,128)(2,1)S(1)}, u32[]{:S(2)}, u32[]{:S(2)}) %collective-permute-start.1) | collective-permute-done | bytes 131104 | tf_op jit(solution)/shard_map/ppermute | solution.py:354
  29.2 0.5 collective-permute-done.2.d_ref
  29.8 0.1 collective-permute-start.11
  29.9 1.6 %collective-permute-done.3.refs_2_ = bf16[2080,128]{1,0:T(8,128)(2,1)S(1)} collective-permute-done((bf16[2080,128]{1,0:T(8,128)(2,1)S(1)}, bf16[2080,128]{1,0:T(8,128)(2,1)S(1)}, u32[]{:S(2)}, u32[]{:S(2)}) %collective-permute-start.3) | collective-permute-done | bytes 532512 | tf_op jit(solution)/shard_map/ppermute | solution.py:370
  31.6 1.5 collective-permute-start.4
  33.1 0.0 collective-permute-done.7.refs_3_
  33.1 0.5 collective-permute-start.8
  33.6 0.0 collective-permute-done.11.q1.refs_1_.refs_0_
  33.6 5.2 %own.1 = (f32[4,2,136,256]{3,2,1,0:T(8,128)S(1)}, f32[4,2,136,256]{3,2,1,0:T(8,128)S(1)}) custom-call(s32[11]{0:T(128)S(1)} %stack.79.sc_ref, bf16[4,64,1024]{2,1,0:T(8,128)(2,1)S(1)} %shard_map.38.q0.refs_0_, bf16[4,64,1024]{2,1,0:T(8,128)(2,1)S(1)} %collective-permute-done.11.q1.refs_1_.refs_0_, bf16[2080,128]{1,0:T(8,128)(2,1)S(1)} %prep.1.ch_ref), custom_call_target="tpu_custom_call" | custom-call | flops 3221225472 | bytes 6000000 | tf_op jit(solution)/shard_map/own/pallas_call | solution.py:261
  38.8 5.7 %collective-permute-done.4.refs_2_ = bf16[2080,128]{1,0:T(8,128)(2,1)S(1)} collective-permute-done((bf16[2080,128]{1,0:T(8,128)(2,1)S(1)}, bf16[2080,128]{1,0:T(8,128)(2,1)S(1)}, u32[]{:S(2)}, u32[]{:S(2)}) %collective-permute-start.4) | collective-permute-done | bytes 532512 | tf_op jit(solution)/shard_map/ppermute | solution.py:370
  44.4 2.8 %collective-permute-start.5 = (bf16[2080,128]{1,0:T(8,128)(2,1)S(1)}, bf16[2080,128]{1,0:T(8,128)(2,1)S(1)}, u32[]{:S(2)}, u32[]{:S(2)}) collective-permute-start(bf16[2080,128]{1,0:T(8,128)(2,1)S(1)} %collective-permute-done.4.refs_2_), channel_id=1, source_target_pairs={{0,16},{16,32},{32,48},{48,64},{64,80},{80,96},{96,112},{112,0},{1... | collective-permute-start | bytes 1597448 | tf_op jit(solution)/shard_map/ppermute | solution.py:370
  47.2 0.0 collective-permute-done.8.refs_3_
  47.2 0.0 collective-permute-start.9
  47.2 7.0 %ring.5 = (f32[4,2,136,256]{3,2,1,0:T(8,128)S(1)}, f32[4,2,136,256]{3,2,1,0:T(8,128)S(1)}) custom-call(s32[11]{0:T(128)S(1)} %stack.79.sc_ref, bf16[4,64,1024]{2,1,0:T(8,128)(2,1)S(1)} %shard_map.38.q0.refs_0_, bf16[4,64,1024]{2,1,0:T(8,128)(2,1)S(1)} %collective-permute-done.11.q1.refs_1_.refs_0_, ...), custom_call_target="tpu_custom_call", output_to_operand_aliasing={{0}: (5, {}), {1}: (6, {})} | custom-call | flops 4294967296 | bytes 6000000 | tf_op jit(solution)/shard_map/ring/pallas_call | solution.py:274
  54.2 7.0 %ring.6 = (f32[4,2,136,256]{3,2,1,0:T(8,128)S(1)}, f32[4,2,136,256]{3,2,1,0:T(8,128)S(1)}) custom-call(s32[11]{0:T(128)S(1)} %stack.79.sc_ref, bf16[4,64,1024]{2,1,0:T(8,128)(2,1)S(1)} %shard_map.38.q0.refs_0_, bf16[4,64,1024]{2,1,0:T(8,128)(2,1)S(1)} %collective-permute-done.11.q1.refs_1_.refs_0_, ...), custom_call_target="tpu_custom_call", output_to_operand_aliasing={{0}: (5, {}), {1}: (6, {})} | custom-call | flops 4294967296 | bytes 6000000 | tf_op jit(solution)/shard_map/ring/pallas_call | solution.py:274
  61.2 0.9 collective-permute-done.9.refs_3_
  62.1 17.9 %collective-permute-start.10 = (bf16[1040,128]{1,0:T(8,128)(2,1)S(1)}, bf16[1040,128]{1,0:T(8,128)(2,1)S(1)}, u32[]{:S(2)}, u32[]{:S(2)}) collective-permute-start(bf16[1040,128]{1,0:T(8,128)(2,1)S(1)} %slice.9), channel_id=1, source_target_pairs={{0,112},{16,0},{32,16},{48,32},{64,48},{80,64},{96,80},{112,96},{1... | collective-permute-start | bytes 798728 | tf_op jit(solution)/shard_map/ppermute | solution.py:373
  80.1 0.0 collective-permute-done.5.refs_2_
  80.1 0.1 collective-permute-start.6
  80.2 27.8 %ring.7 = (f32[4,2,136,256]{3,2,1,0:T(8,128)S(1)}, f32[4,2,136,256]{3,2,1,0:T(8,128)S(1)}) custom-call(s32[11]{0:T(128)S(1)} %stack.79.sc_ref, bf16[4,64,1024]{2,1,0:T(8,128)(2,1)S(1)} %shard_map.38.q0.refs_0_, bf16[4,64,1024]{2,1,0:T(8,128)(2,1)S(1)} %collective-permute-done.11.q1.refs_1_.refs_0_, ...), custom_call_target="tpu_custom_call", output_to_operand_aliasing={{0}: (5, {}), {1}: (6, {})} | custom-call | flops 4294967296 | bytes 6000000 | tf_op jit(solution)/shard_map/ring/pallas_call | solution.py:274
  108.0 0.0 collective-permute-done.10.refs_2_
  108.0 0.0 collective-permute-done.6.refs_1_
  108.0 2.5 %ring.9 = f32[4,2,136,256]{3,2,1,0:T(8,128)S(1)} custom-call(s32[11]{0:T(128)S(1)} %stack.79.sc_ref, bf16[4,64,1024]{2,1,0:T(8,128)(2,1)S(1)} %collective-permute-done.11.q1.refs_1_.refs_0_, bf16[1040,128]{1,0:T(8,128)(2,1)S(1)} %collective-permute-done.6.refs_1_, ...), custom_call_target="tpu_custom_call", output_to_operand_aliasing={{}: (4, {})} | custom-call | flops 1073741824 | bytes 6000000 | tf_op jit(solution)/shard_map/ring/pallas_call | solution.py:274
  110.5 27.5 %collective-permute-start.12 = (f32[4,2,136,256]{3,2,1,0:T(8,128)S(1)}, f32[4,2,136,256]{3,2,1,0:T(8,128)S(1)}, u32[]{:S(2)}, u32[]{:S(2)}) collective-permute-start(f32[4,2,136,256]{3,2,1,0:T(8,128)S(1)} %ring.9), channel_id=1, source_target_pairs={{0,1},{1,0},{2,3},{3,2},{4,5},{5,4},{6,7},{7,6},{8,9},{9,8},{10,11... | collective-permute-start | bytes 3342344 | tf_op jit(solution)/shard_map/ppermute | solution.py:380
  138.0 2.5 %ring.8.s_ref = f32[4,2,136,256]{3,2,1,0:T(8,128)S(1)} custom-call(s32[11]{0:T(128)S(1)} %stack.79.sc_ref, bf16[4,64,1024]{2,1,0:T(8,128)(2,1)S(1)} %shard_map.38.q0.refs_0_, bf16[1040,128]{1,0:T(8,128)(2,1)S(1)} %collective-permute-done.6.refs_1_, bf16[1040,128]{1,0:T(8,128)(2,1)S(1)} %collective-permute-done.10.refs_2_, ...), custom_call_target="tpu_custom_call", output_to_operand_aliasing={{}: (4, {})} | custom-call | flops 1073741824 | bytes 6000000 | tf_op jit(solution)/shard_map/ring/pallas_call | solution.py:274
  140.5 0.0 collective-permute-done.12.r_ref
  140.5 0.9 shard_map.40
  141.4 3.0 %collective-permute-start.13 = (bf16[64,1024]{1,0:T(8,128)(2,1)S(1)}, bf16[64,1024]{1,0:T(8,128)(2,1)S(1)}, u32[]{:S(2)}, u32[]{:S(2)}) collective-permute-start(bf16[64,1024]{1,0:T(8,128)(2,1)S(1)} %get-tuple-element.34), channel_id=1, source_target_pairs={{0,8},{8,128},{128,136},{136,0},{1,9},{9,129},{129,137},{137,1},{2... | collective-permute-start | bytes 393224 | tf_op jit(solution)/shard_map/ppermute | solution.py:354
  144.4 0.1 collective-permute-start.14
  144.5 2.1 %collective-permute-start.15 = (bf16[64,1024]{1,0:T(8,128)(2,1)S(1)}, bf16[64,1024]{1,0:T(8,128)(2,1)S(1)}, u32[]{:S(2)}, u32[]{:S(2)}) collective-permute-start(bf16[64,1024]{1,0:T(8,128)(2,1)S(1)} %get-tuple-element.36), channel_id=1, source_target_pairs={{0,136},{8,0},{128,8},{136,128},{1,137},{9,1},{129,9},{137,129},{2... | collective-permute-start | bytes 393224 | tf_op jit(solution)/shard_map/ppermute | solution.py:354
  146.5 1.8 %collective-permute-done.13.refs_1_ = bf16[64,1024]{1,0:T(8,128)(2,1)S(1)} collective-permute-done((bf16[64,1024]{1,0:T(8,128)(2,1)S(1)}, bf16[64,1024]{1,0:T(8,128)(2,1)S(1)}, u32[]{:S(2)}, u32[]{:S(2)}) %collective-permute-start.13) | collective-permute-done | bytes 131104 | tf_op jit(solution)/shard_map/ppermute | solution.py:354
  148.3 3.0 %collective-permute-done.14.refs_2_ = bf16[64,1024]{1,0:T(8,128)(2,1)S(1)} collective-permute-done((bf16[64,1024]{1,0:T(8,128)(2,1)S(1)}, bf16[64,1024]{1,0:T(8,128)(2,1)S(1)}, u32[]{:S(2)}, u32[]{:S(2)}) %collective-permute-start.14) | collective-permute-done | bytes 131104 | tf_op jit(solution)/shard_map/ppermute | solution.py:354
  151.2 0.4 collective-permute-done.15.refs_3_
  151.7 1.4 shard_map.41
  (3 shorter events, 0.1 us)
Async XLA Ops:
  1.8 18.9 %copy-start = (bf16[64,4096]{1,0:T(8,128)(2,1)S(1)}, bf16[64,4096]{1,0:T(8,128)(2,1)}, u32[]{:S(2)}) copy-start(bf16[64,4096]{1,0:T(8,128)(2,1)} %q_ref.1) | copy-start | bytes 1572868
  18.4 13.1 %collective-permute-start.3 = (bf16[2080,128]{1,0:T(8,128)(2,1)S(1)}, bf16[2080,128]{1,0:T(8,128)(2,1)S(1)}, u32[]{:S(2)}, u32[]{:S(2)}) collective-permute-start(bf16[2080,128]{1,0:T(8,128)(2,1)S(1)} %prep.1.ch_ref), channel_id=1, source_target_pairs={{0,16},{16,32},{32,48},{48,64},{64,80},{80,96},{96,112},{112,0},{1... | collective-permute-start | bytes 1597448 | tf_op jit(solution)/shard_map/ppermute | solution.py:370
  18.5 14.5 %collective-permute-start.7 = (bf16[2080,128]{1,0:T(8,128)(2,1)S(1)}, bf16[2080,128]{1,0:T(8,128)(2,1)S(1)}, u32[]{:S(2)}, u32[]{:S(2)}) collective-permute-start(bf16[2080,128]{1,0:T(8,128)(2,1)S(1)} %prep.1.ch_ref), channel_id=1, source_target_pairs={{0,112},{16,0},{32,16},{48,32},{64,48},{80,64},{96,80},{112,96},{1... | collective-permute-start | bytes 1597448 | tf_op jit(solution)/shard_map/ppermute | solution.py:371
  21.2 6.4 %collective-permute-start = (bf16[64,1024]{1,0:T(8,128)(2,1)S(1)}, bf16[64,1024]{1,0:T(8,128)(2,1)S(1)}, u32[]{:S(2)}, u32[]{:S(2)}) collective-permute-start(bf16[64,1024]{1,0:T(8,128)(2,1)S(1)} %get-tuple-element.22), channel_id=1, source_target_pairs={{0,8},{8,128},{128,136},{136,0},{1,9},{9,129},{129,137},{137,1},{2... | collective-permute-start | bytes 393224 | tf_op jit(solution)/shard_map/ppermute | solution.py:354
  22.8 6.5 %collective-permute-start.1 = (bf16[64,1024]{1,0:T(8,128)(2,1)S(1)}, bf16[64,1024]{1,0:T(8,128)(2,1)S(1)}, u32[]{:S(2)}, u32[]{:S(2)}) collective-permute-start(bf16[64,1024]{1,0:T(8,128)(2,1)S(1)} %get-tuple-element.23), channel_id=1, source_target_pairs={{0,128},{8,136},{128,0},{136,8},{1,129},{9,137},{129,1},{137,9},{2... | collective-permute-start | bytes 393224 | tf_op jit(solution)/shard_map/ppermute | solution.py:354
  24.1 5.7 %collective-permute-start.2 = (bf16[64,1024]{1,0:T(8,128)(2,1)S(1)}, bf16[64,1024]{1,0:T(8,128)(2,1)S(1)}, u32[]{:S(2)}, u32[]{:S(2)}) collective-permute-start(bf16[64,1024]{1,0:T(8,128)(2,1)S(1)} %get-tuple-element.24), channel_id=1, source_target_pairs={{0,136},{8,0},{128,8},{136,128},{1,137},{9,1},{129,9},{137,129},{2... | collective-permute-start | bytes 393224 | tf_op jit(solution)/shard_map/ppermute | solution.py:354
  29.8 3.8 %collective-permute-start.11 = (bf16[4,64,1024]{2,1,0:T(8,128)(2,1)S(1)}, bf16[4,64,1024]{2,1,0:T(8,128)(2,1)S(1)}, u32[]{:S(2)}, u32[]{:S(2)}) collective-permute-start(bf16[4,64,1024]{2,1,0:T(8,128)(2,1)S(1)} %shard_map.38.q0.refs_0_), channel_id=1, source_target_pairs={{0,1},{1,0},{2,3},{3,2},{4,5},{5,4},{6,7},{7,6},{8,9},{9,8},{10,11... | collective-permute-start | bytes 1572872 | tf_op jit(solution)/shard_map/ppermute | solution.py:365
  31.6 12.9 %collective-permute-start.4 = (bf16[2080,128]{1,0:T(8,128)(2,1)S(1)}, bf16[2080,128]{1,0:T(8,128)(2,1)S(1)}, u32[]{:S(2)}, u32[]{:S(2)}) collective-permute-start(bf16[2080,128]{1,0:T(8,128)(2,1)S(1)} %collective-permute-done.3.refs_2_), channel_id=1, source_target_pairs={{0,16},{16,32},{32,48},{48,64},{64,80},{80,96},{96,112},{112,0},{1... | collective-permute-start | bytes 1597448 | tf_op jit(solution)/shard_map/ppermute | solution.py:370
  33.1 14.2 %collective-permute-start.8 = (bf16[2080,128]{1,0:T(8,128)(2,1)S(1)}, bf16[2080,128]{1,0:T(8,128)(2,1)S(1)}, u32[]{:S(2)}, u32[]{:S(2)}) collective-permute-start(bf16[2080,128]{1,0:T(8,128)(2,1)S(1)} %collective-permute-done.7.refs_3_), channel_id=1, source_target_pairs={{0,112},{16,0},{32,16},{48,32},{64,48},{80,64},{96,80},{112,96},{1... | collective-permute-start | bytes 1597448 | tf_op jit(solution)/shard_map/ppermute | solution.py:371
  44.4 35.6 %collective-permute-start.5 = (bf16[2080,128]{1,0:T(8,128)(2,1)S(1)}, bf16[2080,128]{1,0:T(8,128)(2,1)S(1)}, u32[]{:S(2)}, u32[]{:S(2)}) collective-permute-start(bf16[2080,128]{1,0:T(8,128)(2,1)S(1)} %collective-permute-done.4.refs_2_), channel_id=1, source_target_pairs={{0,16},{16,32},{32,48},{48,64},{64,80},{80,96},{96,112},{112,0},{1... | collective-permute-start | bytes 1597448 | tf_op jit(solution)/shard_map/ppermute | solution.py:370
  47.2 14.9 %collective-permute-start.9 = (bf16[2080,128]{1,0:T(8,128)(2,1)S(1)}, bf16[2080,128]{1,0:T(8,128)(2,1)S(1)}, u32[]{:S(2)}, u32[]{:S(2)}) collective-permute-start(bf16[2080,128]{1,0:T(8,128)(2,1)S(1)} %collective-permute-done.8.refs_3_), channel_id=1, source_target_pairs={{0,112},{16,0},{32,16},{48,32},{64,48},{80,64},{96,80},{112,96},{1... | collective-permute-start | bytes 1597448 | tf_op jit(solution)/shard_map/ppermute | solution.py:371
  62.1 45.9 %collective-permute-start.10 = (bf16[1040,128]{1,0:T(8,128)(2,1)S(1)}, bf16[1040,128]{1,0:T(8,128)(2,1)S(1)}, u32[]{:S(2)}, u32[]{:S(2)}) collective-permute-start(bf16[1040,128]{1,0:T(8,128)(2,1)S(1)} %slice.9), channel_id=1, source_target_pairs={{0,112},{16,0},{32,16},{48,32},{64,48},{80,64},{96,80},{112,96},{1... | collective-permute-start | bytes 798728 | tf_op jit(solution)/shard_map/ppermute | solution.py:373
  80.1 27.9 %collective-permute-start.6 = (bf16[1040,128]{1,0:T(8,128)(2,1)S(1)}, bf16[1040,128]{1,0:T(8,128)(2,1)S(1)}, u32[]{:S(2)}, u32[]{:S(2)}) collective-permute-start(bf16[1040,128]{1,0:T(8,128)(2,1)S(1)} %slice.8), channel_id=1, source_target_pairs={{0,16},{16,32},{32,48},{48,64},{64,80},{80,96},{96,112},{112,0},{1... | collective-permute-start | bytes 798728 | tf_op jit(solution)/shard_map/ppermute | solution.py:372
  110.5 30.0 %collective-permute-start.12 = (f32[4,2,136,256]{3,2,1,0:T(8,128)S(1)}, f32[4,2,136,256]{3,2,1,0:T(8,128)S(1)}, u32[]{:S(2)}, u32[]{:S(2)}) collective-permute-start(f32[4,2,136,256]{3,2,1,0:T(8,128)S(1)} %ring.9), channel_id=1, source_target_pairs={{0,1},{1,0},{2,3},{3,2},{4,5},{5,4},{6,7},{7,6},{8,9},{9,8},{10,11... | collective-permute-start | bytes 3342344 | tf_op jit(solution)/shard_map/ppermute | solution.py:380
  141.4 6.9 %collective-permute-start.13 = (bf16[64,1024]{1,0:T(8,128)(2,1)S(1)}, bf16[64,1024]{1,0:T(8,128)(2,1)S(1)}, u32[]{:S(2)}, u32[]{:S(2)}) collective-permute-start(bf16[64,1024]{1,0:T(8,128)(2,1)S(1)} %get-tuple-element.34), channel_id=1, source_target_pairs={{0,8},{8,128},{128,136},{136,0},{1,9},{9,129},{129,137},{137,1},{2... | collective-permute-start | bytes 393224 | tf_op jit(solution)/shard_map/ppermute | solution.py:354
  144.4 6.8 %collective-permute-start.14 = (bf16[64,1024]{1,0:T(8,128)(2,1)S(1)}, bf16[64,1024]{1,0:T(8,128)(2,1)S(1)}, u32[]{:S(2)}, u32[]{:S(2)}) collective-permute-start(bf16[64,1024]{1,0:T(8,128)(2,1)S(1)} %get-tuple-element.35), channel_id=1, source_target_pairs={{0,128},{8,136},{128,0},{136,8},{1,129},{9,137},{129,1},{137,9},{2... | collective-permute-start | bytes 393224 | tf_op jit(solution)/shard_map/ppermute | solution.py:354
  144.5 7.2 %collective-permute-start.15 = (bf16[64,1024]{1,0:T(8,128)(2,1)S(1)}, bf16[64,1024]{1,0:T(8,128)(2,1)S(1)}, u32[]{:S(2)}, u32[]{:S(2)}) collective-permute-start(bf16[64,1024]{1,0:T(8,128)(2,1)S(1)} %get-tuple-element.36), channel_id=1, source_target_pairs={{0,136},{8,0},{128,8},{136,128},{1,137},{9,1},{129,9},{137,129},{2... | collective-permute-start | bytes 393224 | tf_op jit(solution)/shard_map/ppermute | solution.py:354

commit v4 on v3

--- a/solution.py
+++ b/solution.py
@@ -48,7 +48,7 @@
         in_specs=[VMEM],
         out_specs=VMEM,
         name="prep",
-        compiler_params=pltpu.CompilerParams(vmem_limit_bytes=8 * 1024 * 1024),
+        compiler_params=pltpu.CompilerParams(vmem_limit_bytes=2 * 1024 * 1024),
         cost_estimate=pl.CostEstimate(flops=1000000, bytes_accessed=1000000, transcendentals=0),
     )(kv)
 
@@ -203,12 +203,10 @@
 
 
 def step_kernel(n_chunks, first, n_rows, sc_ref, *refs):
-    q_refs, given, held = refs[:n_rows], refs[n_rows : n_rows + 2], refs[-1]
+    q_refs, given, held = refs[:n_rows], refs[n_rows : n_rows + n_chunks], refs[-1]
     refs = (q_refs, refs[-1 - n_rows : -1], sc_ref[0])
-    if n_chunks == 2:
-        held[0], held[1] = given[0][...], given[1][...]
-    else:
-        held[0, :HALF, :], held[0, HALF:, :] = given[0][...], given[1][...]
+    for j in range(n_chunks):
+        held[j] = given[j][...]
 
     def chunk(j):
         return lambda at, n: held[j, pl.ds(at, n), :]
@@ -245,7 +243,7 @@
     return pl.CostEstimate(flops=4 * work * DH, bytes_accessed=6000000, transcendentals=work)
 
 
-def small(kernel, out_shape, n_in, scalars=True, in_space=VMEM, out_space=VMEM, scratch=(), limit=12):
+def small(kernel, out_shape, n_in, scalars=True, in_space=VMEM, out_space=VMEM, scratch=(), limit=4):
     return pl.pallas_call(
         kernel,
         out_shape=out_shape,
@@ -264,37 +262,42 @@
         in_specs=[SMEM, VMEM, VMEM, VMEM],
         out_specs=(VMEM,) * 2,
         name="own",
-        compiler_params=pltpu.CompilerParams(vmem_limit_bytes=24 * 1024 * 1024),
+        compiler_params=pltpu.CompilerParams(vmem_limit_bytes=8 * 1024 * 1024),
         cost_estimate=cost(6),
     )(sc, q0, q1, chunk)
 
 
-def ring_step(sc, qs, state, chunks, n_chunks, first):
-    n_rows = len(qs)
+def ring_step(sc, qs, state, chunks, first):
+    n, n_rows = len(chunks), len(qs)
     return pl.pallas_call(
-        functools.partial(step_kernel, n_chunks, first, n_rows),
+        functools.partial(step_kernel, n, first, n_rows),
         out_shape=ST[:n_rows],
-        in_specs=[SMEM] + [VMEM] * (2 + 2 * n_rows),
+        in_specs=[SMEM] + [VMEM] * (n + 2 * n_rows),
         out_specs=(VMEM,) * n_rows,
-        input_output_aliases={3 + n_rows + i: i for i in range(n_rows)},
-        scratch_shapes=[pltpu.VMEM((n_chunks, 2 * HALF, DH), jnp.bfloat16)],
+        input_output_aliases={1 + n_rows + n + i: i for i in range(n_rows)},
+        scratch_shapes=[pltpu.VMEM((n, 2 * HALF, DH), jnp.bfloat16)],
         name="ring",
-        compiler_params=pltpu.CompilerParams(vmem_limit_bytes=24 * 1024 * 1024),
-        cost_estimate=cost(2 * n_chunks * n_rows),
+        compiler_params=pltpu.CompilerParams(vmem_limit_bytes=8 * 1024 * 1024),
+        cost_estimate=cost(2 * n * n_rows),
     )(sc, *qs, *chunks, *state)
 
 
-def kv_send_kernel(k_hbm, v_hbm, out_ref, k_ref, v_ref, sems):
-    copies = [pltpu.make_async_copy(a, b, sems.at[i]) for i, (a, b) in enumerate(((k_hbm, k_ref), (v_hbm, v_ref)))]
+def spread(raw_ref, out_ref):
+    for g in range(KV):
+        block = raw_ref[:, g * DH : (g + 1) * DH]
+        for i in range(4):
+            out_ref[g * 4 + i] = block
+
+
+def kv_send_kernel(k_hbm, v_hbm, out_ref, raw_ref, sems):
+    copies = [
+        pltpu.make_async_copy(a, raw_ref.at[pl.ds(i * STRIP, STRIP)], sems.at[i]) for i, a in enumerate((k_hbm, v_hbm))
+    ]
     for copy in copies:
         copy.start()
     for copy in copies:
         copy.wait()
-    for g in range(KV):
-        k, v = k_ref[:, g * DH : (g + 1) * DH], v_ref[:, g * DH : (g + 1) * DH]
-        for i in range(4):
-            out_ref[g * 4 + i, :STRIP, :] = k
-            out_ref[g * 4 + i, STRIP:, :] = v
+    spread(raw_ref, out_ref)
 
 
 def q_send_kernel(sc_ref, q_ref, *outs):
@@ -357,9 +360,14 @@
     bf16 = jnp.bfloat16
     piece = jax.ShapeDtypeStruct((STRIP, 8 * DH), bf16)
     sent = jax.ShapeDtypeStruct((16, 2 * STRIP, DH), bf16)
-    held = [pltpu.VMEM((STRIP, KV * DH), bf16)] * 2 + [pltpu.SemaphoreType.DMA((2,))]
-    kv = small(kv_send_kernel, sent, 2, False, ANY, VMEM, held, 63)(keys, values)
+    raw = jax.ShapeDtypeStruct((2 * STRIP, KV * DH), bf16)
+    sems = [pltpu.SemaphoreType.DMA((2,))]
+    kv, raw = small(kv_send_kernel, (sent, raw), 2, False, ANY, VMEM, sems, 63)(keys, values)
     kv = lax.all_to_all(kv, ("yh", "yl", "x"), split_axis=0, concat_axis=0, tiled=True)
+    raw = lax.ppermute(raw, "z", [(i, (i + nz // 2) % nz) for i in range(nz)])
+    far = small(spread, sent, 1, False)(raw)
+    far = lax.all_to_all(far, ("yh", "yl", "x"), split_axis=0, concat_axis=0, tiled=True)
+    far = prep(far)
     q_pieces = regroup(small(q_send_kernel, (piece,) * 4, 1)(sc, queries))
     q0 = small(join_kernel, jax.ShapeDtypeStruct((4, STRIP, 8 * DH), bf16), 4, False)(*q_pieces)
     q1 = lax.ppermute(q0, "c", swap)
@@ -369,16 +377,14 @@
     for _ in range(1, 4):
         fwd.append(lax.ppermute(fwd[-1], "z", up))
         bwd.append(lax.ppermute(bwd[-1], "z", down))
-    far_l = lax.ppermute(fwd[3][:HALF], "z", up)
-    far_h = lax.ppermute(bwd[3][HALF:], "z", down)
 
     state = own_step(sc, q0, q1, chunk)
-    for k in range(1, 4):
-        state = ring_step(sc, (q0, q1), state, (fwd[k], bwd[k]), 2, 2 + k)
-    far = ((far_l, far_h), 1, 6)
-    (theirs,) = ring_step(sc, (q1,), state[1:], *far)
+    for k in range(1, 3):
+        state = ring_step(sc, (q0, q1), state, (fwd[k], bwd[k]), 2 + k)
+    state = ring_step(sc, (q0, q1), state, (far,), 6)
+    (theirs,) = ring_step(sc, (q1,), state[1:], (fwd[3], bwd[3]), 5)
     other = lax.ppermute(theirs, "c", swap)
-    (ours,) = ring_step(sc, (q0,), state[:1], *far)
+    (ours,) = ring_step(sc, (q0,), state[:1], (fwd[3], bwd[3]), 5)
     pieces = small(merge_kernel, (piece,) * 4, 2)(sc, ours, other)
     out = jax.ShapeDtypeStruct((STRIP, H * DH), bf16)
     sems = [pltpu.SemaphoreType.DMA((4,))]

time: 156 us -> 151 us (0.968)
  waiting for transfers between devices: 16.6 us -> 12.1 us
    ppermute x2 -> x1, starting transfers between devices: 18 us -> 1.44 us  [per_device(): raw = lax.ppermute(raw, 'z', [(i, (i + nz // 2) % nz) for i in range(nz)])]
    ppermute x1, starting transfers between devices: 27.5 us -> 39.5 us  [per_device(): other = lax.ppermute(theirs, 'c', swap)]
    all_to_all x0 -> x1, starting transfers between devices: none -> 7.43 us  [per_device(): lax.all_to_all(kv, ('yh', 'yl', 'x'), split_axis=0, concat_axis=0, tiled=...]
    ppermute x3, waiting for transfers between devices: 7.3 us -> 0.01 us  [per_device(): fwd.append(lax.ppermute(fwd[-1], 'z', up))]
    all_to_all x0 -> x1, waiting for transfers between devices: none -> 4.09 us  [per_device(): lax.all_to_all(kv, ('yh', 'yl', 'x'), split_axis=0, concat_axis=0, tiled=...]
    ppermute x6, starting transfers between devices: 10.5 us -> 8.23 us  [regroup(): lax.ppermute(pieces[d], ('yh', 'yl'), [(i, (i + d) % ny) for i in range(n...]
    pallas_call x6 -> x7, Pallas kernels: 48.5 us -> 48.5 us  [the longest x5 46.6 us: ring_step(): pl.pallas_call(functools.partial(step_kernel, n, first, n_rows), out_shap...]
  transfers between devices with their start and end apart: 16 -> 16, of which waited for: 9 -> 6; matrix products, arithmetic and copies ran while one was open for 0% -> 0% of each run, Pallas kernels for 33% -> 26%
where the time goes in v4:
time: 151 us; the launch traced here: 148 us
  starting transfers between devices  62.1 us (41%)
  Pallas kernels  57.2 us (38%)
  blocking collectives  16.1 us (11%)
  waiting for transfers between devices  12.1 us (8%)
    pallas_call x5, Pallas kernels, ring_step(): pl.pallas_call(functools.partial(step_kernel, n, first, n_rows), out_shap...  46.6 us
    ppermute x1, starting transfers between devices, per_device(): other = lax.ppermute(theirs, 'c', swap)  39.5 us
    all_to_all x1, blocking collectives, per_device(): lax.all_to_all(far, ('yh', 'yl', 'x'), split_axis=0, concat_axis=0, tiled...  16.1 us
    ppermute x6, starting transfers between devices, regroup(): lax.ppermute(pieces[d], ('yh', 'yl'), [(i, (i + d) % ny) for i in range(n...  8.23 us
    ppermute x6, waiting for transfers between devices, regroup(): lax.ppermute(pieces[d], ('yh', 'yl'), [(i, (i + d) % ny) for i in range(n...  8.03 us
    all_to_all x1, starting transfers between devices, per_device(): lax.all_to_all(kv, ('yh', 'yl', 'x'), split_axis=0, concat_axis=0, tiled=...  7.43 us
    pallas_call x1, Pallas kernels, own_step(): pl.pallas_call(own_kernel, out_shape=ST, in_specs=[SMEM, VMEM, VMEM, VMEM...  5.26 us
    ppermute x3, starting transfers between devices, per_device(): fwd.append(lax.ppermute(fwd[-1], 'z', up))  4.11 us
  transfers between devices with their start and end apart: 16, of which 6 were waited for; matrix products, arithmetic and copies ran while one was open for 0% of the time, Pallas kernels for 26%

profile of v4, /device:TPU:240, one launch (start us, length us, event | category | flops | bytes accessed | tf_op | source)
XLA Modules:
  0.0 148.0 jit_solution(3017643371052391100)
XLA Ops:
  0.0 0.0 copy-start
  0.0 1.8 %shard_map.39 = (bf16[16,128,128]{2,1,0:T(8,128)(2,1)}, bf16[128,512]{1,0:T(8,128)(2,1)}) custom-call(bf16[64,512]{1,0:T(8,128)(2,1)} %k_hbm.1, bf16[64,512]{1,0:T(8,128)(2,1)} %v_hbm.1), custom_call_target="tpu_custom_call" | custom-call | flops 1000000 | bytes 1000000 | tf_op jit(solution)/shard_map/pallas_call | solution.py:365
  1.8 0.0 copy-start.1
  1.8 7.4 %all-to-all-start = ((bf16[16,128,128]{2,1,0:T(8,128)(2,1)}), bf16[16,128,128]{2,1,0:T(8,128)(2,1)S(1)}, u32[]{:S(2)}, u32[]{:S(2)}) async-start(bf16[16,128,128]{2,1,0:T(8,128)(2,1)} %get-tuple-element.27), calls=%async_computation | async-start | bytes 1048576 | tf_op jit(solution)/shard_map/all_to_all | solution.py:366
  9.3 0.1 stack.79.sc_ref
  9.3 0.0 copy-done
  9.3 0.6 shard_map.37
  9.9 1.2 collective-permute-start
  11.2 0.9 collective-permute-start.1
  12.0 0.7 collective-permute-start.2
  12.8 0.0 copy-done.1
  12.8 1.4 collective-permute-start.10
  14.2 4.1 %all-to-all-done.kv_ref = bf16[16,128,128]{2,1,0:T(8,128)(2,1)S(1)} async-done(((bf16[16,128,128]{2,1,0:T(8,128)(2,1)}), bf16[16,128,128]{2,1,0:T(8,128)(2,1)S(1)}, u32[]{:S(2)}, u32[]{:S(2)}) %all-to-all-start) | async-done | bytes 524320 | tf_op jit(solution)/shard_map/all_to_all | solution.py:366
  18.3 0.3 prep.2.ch_ref
  18.6 0.1 collective-permute-start.3
  18.7 3.2 %collective-permute-done.b_ref = bf16[64,1024]{1,0:T(8,128)(2,1)S(1)} collective-permute-done((bf16[64,1024]{1,0:T(8,128)(2,1)S(1)}, bf16[64,1024]{1,0:T(8,128)(2,1)S(1)}, u32[]{:S(2)}, u32[]{:S(2)}) %collective-permute-start) | collective-permute-done | bytes 131104 | tf_op jit(solution)/shard_map/ppermute | solution.py:357
  21.9 1.0 collective-permute-start.6
  22.9 0.0 collective-permute-done.1.c_ref
  22.9 0.1 collective-permute-done.2.d_ref
  23.0 0.1 collective-permute-start.9
  23.1 0.0 collective-permute-done.10.raw_ref
  23.2 0.1 shard_map.40
  23.2 16.1 %all_to_all.10.kv_ref = bf16[16,128,128]{2,1,0:T(8,128)(2,1)S(1)} all-to-all(bf16[16,128,128]{2,1,0:T(8,128)(2,1)S(1)} %shard_map.40), channel_id=1, replica_groups=mesh['yh'=2,'z'=8,'yl'=2,'x'=4,'c'=2] {'yh','yl','x'}, dimensions={0} | all-to-all | bytes 1048576 | tf_op jit(solution)/shard_map/all_to_all | solution.py:369
  39.4 0.3 prep.3.refs_2_
  39.7 0.0 collective-permute-done.3.refs_2_
  39.7 2.2 %collective-permute-start.4 = (bf16[2080,128]{1,0:T(8,128)(2,1)S(1)}, bf16[2080,128]{1,0:T(8,128)(2,1)S(1)}, u32[]{:S(2)}, u32[]{:S(2)}) collective-permute-start(bf16[2080,128]{1,0:T(8,128)(2,1)S(1)} %collective-permute-done.3.refs_2_), channel_id=1, source_target_pairs={{0,16},{16,32},{32,48},{48,64},{64,80},{80,96},{96,112},{112,0},{1... | collective-permute-start | bytes 1597448 | tf_op jit(solution)/shard_map/ppermute | solution.py:378
  41.9 0.0 collective-permute-done.6.refs_3_
  41.9 0.0 collective-permute-start.7
  41.9 0.0 collective-permute-done.9.q1.refs_1_.refs_0_
  41.9 5.3 %own.1 = (f32[4,2,136,256]{3,2,1,0:T(8,128)S(1)}, f32[4,2,136,256]{3,2,1,0:T(8,128)S(1)}) custom-call(s32[11]{0:T(128)S(1)} %stack.79.sc_ref, bf16[4,64,1024]{2,1,0:T(8,128)(2,1)S(1)} %shard_map.38.q0.refs_0_, bf16[4,64,1024]{2,1,0:T(8,128)(2,1)S(1)} %collective-permute-done.9.q1.refs_1_.refs_0_, bf16[2080,128]{1,0:T(8,128)(2,1)S(1)} %prep.2.ch_ref), custom_call_target="tpu_custom_call" | custom-call | flops 3221225472 | bytes 6000000 | tf_op jit(solution)/shard_map/own/pallas_call | solution.py:259
  47.1 7.1 %ring.5 = (f32[4,2,136,256]{3,2,1,0:T(8,128)S(1)}, f32[4,2,136,256]{3,2,1,0:T(8,128)S(1)}) custom-call(s32[11]{0:T(128)S(1)} %stack.79.sc_ref, bf16[4,64,1024]{2,1,0:T(8,128)(2,1)S(1)} %shard_map.38.q0.refs_0_, bf16[4,64,1024]{2,1,0:T(8,128)(2,1)S(1)} %collective-permute-done.9.q1.refs_1_.refs_0_, ...), custom_call_target="tpu_custom_call", output_to_operand_aliasing={{0}: (5, {}), {1}: (6, {})} | custom-call | flops 4294967296 | bytes 6000000 | tf_op jit(solution)/shard_map/ring/pallas_call | solution.py:272
  54.3 0.0 collective-permute-done.4.refs_2_
  54.3 1.8 %collective-permute-start.5 = (bf16[2080,128]{1,0:T(8,128)(2,1)S(1)}, bf16[2080,128]{1,0:T(8,128)(2,1)S(1)}, u32[]{:S(2)}, u32[]{:S(2)}) collective-permute-start(bf16[2080,128]{1,0:T(8,128)(2,1)S(1)} %collective-permute-done.4.refs_2_), channel_id=1, source_target_pairs={{0,16},{16,32},{32,48},{48,64},{64,80},{80,96},{96,112},{112,0},{1... | collective-permute-start | bytes 1597448 | tf_op jit(solution)/shard_map/ppermute | solution.py:378
  56.1 0.0 collective-permute-done.7.refs_3_
  56.1 0.3 collective-permute-start.8
  56.4 7.0 %ring.6 = (f32[4,2,136,256]{3,2,1,0:T(8,128)S(1)}, f32[4,2,136,256]{3,2,1,0:T(8,128)S(1)}) custom-call(s32[11]{0:T(128)S(1)} %stack.79.sc_ref, bf16[4,64,1024]{2,1,0:T(8,128)(2,1)S(1)} %shard_map.38.q0.refs_0_, bf16[4,64,1024]{2,1,0:T(8,128)(2,1)S(1)} %collective-permute-done.9.q1.refs_1_.refs_0_, ...), custom_call_target="tpu_custom_call", output_to_operand_aliasing={{0}: (5, {}), {1}: (6, {})} | custom-call | flops 4294967296 | bytes 6000000 | tf_op jit(solution)/shard_map/ring/pallas_call | solution.py:272
  63.4 4.0 %ring.7 = (f32[4,2,136,256]{3,2,1,0:T(8,128)S(1)}, f32[4,2,136,256]{3,2,1,0:T(8,128)S(1)}) custom-call(s32[11]{0:T(128)S(1)} %stack.79.sc_ref, bf16[4,64,1024]{2,1,0:T(8,128)(2,1)S(1)} %shard_map.38.q0.refs_0_, bf16[4,64,1024]{2,1,0:T(8,128)(2,1)S(1)} %collective-permute-done.9.q1.refs_1_.refs_0_, ...), custom_call_target="tpu_custom_call", output_to_operand_aliasing={{0}: (4, {}), {1}: (5, {})} | custom-call | flops 2147483648 | bytes 6000000 | tf_op jit(solution)/shard_map/ring/pallas_call | solution.py:272
  67.3 0.0 collective-permute-done.5.refs_1_
  67.4 0.0 collective-permute-done.8.refs_2_
  67.4 14.3 %ring.9 = f32[4,2,136,256]{3,2,1,0:T(8,128)S(1)} custom-call(s32[11]{0:T(128)S(1)} %stack.79.sc_ref, bf16[4,64,1024]{2,1,0:T(8,128)(2,1)S(1)} %collective-permute-done.9.q1.refs_1_.refs_0_, bf16[2080,128]{1,0:T(8,128)(2,1)S(1)} %collective-permute-done.5.refs_1_, ...), custom_call_target="tpu_custom_call", output_to_operand_aliasing={{}: (4, {})} | custom-call | flops 2147483648 | bytes 6000000 | tf_op jit(solution)/shard_map/ring/pallas_call | solution.py:272
  81.7 39.5 %collective-permute-start.11 = (f32[4,2,136,256]{3,2,1,0:T(8,128)S(1)}, f32[4,2,136,256]{3,2,1,0:T(8,128)S(1)}, u32[]{:S(2)}, u32[]{:S(2)}) collective-permute-start(f32[4,2,136,256]{3,2,1,0:T(8,128)S(1)} %ring.9), channel_id=1, source_target_pairs={{0,1},{1,0},{2,3},{3,2},{4,5},{5,4},{6,7},{7,6},{8,9},{9,8},{10,11... | collective-permute-start | bytes 3342344 | tf_op jit(solution)/shard_map/ppermute | solution.py:386
  121.2 14.3 %ring.8.s_ref = f32[4,2,136,256]{3,2,1,0:T(8,128)S(1)} custom-call(s32[11]{0:T(128)S(1)} %stack.79.sc_ref, bf16[4,64,1024]{2,1,0:T(8,128)(2,1)S(1)} %shard_map.38.q0.refs_0_, bf16[2080,128]{1,0:T(8,128)(2,1)S(1)} %collective-permute-done.5.refs_1_, bf16[2080,128]{1,0:T(8,128)(2,1)S(1)} %collective-permute-done.8.refs_2_, ...), custom_call_target="tpu_custom_call", output_to_operand_aliasing={{}: (4, {})} | custom-call | flops 2147483648 | bytes 6000000 | tf_op jit(solution)/shard_map/ring/pallas_call | solution.py:272
  135.5 0.0 collective-permute-done.11.r_ref
  135.5 0.8 shard_map.41
  136.3 1.5 %collective-permute-start.12 = (bf16[64,1024]{1,0:T(8,128)(2,1)S(1)}, bf16[64,1024]{1,0:T(8,128)(2,1)S(1)}, u32[]{:S(2)}, u32[]{:S(2)}) collective-permute-start(bf16[64,1024]{1,0:T(8,128)(2,1)S(1)} %get-tuple-element.38), channel_id=1, source_target_pairs={{0,8},{8,128},{128,136},{136,0},{1,9},{9,129},{129,137},{137,1},{2... | collective-permute-start | bytes 393224 | tf_op jit(solution)/shard_map/ppermute | solution.py:357
  137.9 1.3 collective-permute-start.13
  139.2 2.5 %collective-permute-start.14 = (bf16[64,1024]{1,0:T(8,128)(2,1)S(1)}, bf16[64,1024]{1,0:T(8,128)(2,1)S(1)}, u32[]{:S(2)}, u32[]{:S(2)}) collective-permute-start(bf16[64,1024]{1,0:T(8,128)(2,1)S(1)} %get-tuple-element.40), channel_id=1, source_target_pairs={{0,136},{8,0},{128,8},{136,128},{1,137},{9,1},{129,9},{137,129},{2... | collective-permute-start | bytes 393224 | tf_op jit(solution)/shard_map/ppermute | solution.py:357
  141.7 0.1 collective-permute-done.12.refs_1_
  141.8 3.8 %collective-permute-done.13.refs_2_ = bf16[64,1024]{1,0:T(8,128)(2,1)S(1)} collective-permute-done((bf16[64,1024]{1,0:T(8,128)(2,1)S(1)}, bf16[64,1024]{1,0:T(8,128)(2,1)S(1)}, u32[]{:S(2)}, u32[]{:S(2)}) %collective-permute-start.13) | collective-permute-done | bytes 131104 | tf_op jit(solution)/shard_map/ppermute | solution.py:357
  145.6 0.9 collective-permute-done.14.refs_3_
  146.5 1.4 shard_map.42
  (1 shorter events, 0.0 us)
Async XLA Ops:
  0.0 9.3 %copy-start = (bf16[64,4096]{1,0:T(8,128)(2,1)S(1)}, bf16[64,4096]{1,0:T(8,128)(2,1)}, u32[]{:S(2)}) copy-start(bf16[64,4096]{1,0:T(8,128)(2,1)} %q_ref.1) | copy-start | bytes 1572868
  1.8 11.0 %copy-start.1 = (bf16[128,512]{1,0:T(8,128)(2,1)S(1)}, bf16[128,512]{1,0:T(8,128)(2,1)}, u32[]{:S(2)}) copy-start(bf16[128,512]{1,0:T(8,128)(2,1)} %get-tuple-element.28) | copy-start | bytes 393220
  1.8 16.5 %all-to-all-start = ((bf16[16,128,128]{2,1,0:T(8,128)(2,1)}), bf16[16,128,128]{2,1,0:T(8,128)(2,1)S(1)}, u32[]{:S(2)}, u32[]{:S(2)}) async-start(bf16[16,128,128]{2,1,0:T(8,128)(2,1)} %get-tuple-element.27), calls=%async_computation | async-start | bytes 1048576 | tf_op jit(solution)/shard_map/all_to_all | solution.py:366
  9.9 11.9 %collective-permute-start = (bf16[64,1024]{1,0:T(8,128)(2,1)S(1)}, bf16[64,1024]{1,0:T(8,128)(2,1)S(1)}, u32[]{:S(2)}, u32[]{:S(2)}) collective-permute-start(bf16[64,1024]{1,0:T(8,128)(2,1)S(1)} %get-tuple-element.24), channel_id=1, source_target_pairs={{0,8},{8,128},{128,136},{136,0},{1,9},{9,129},{129,137},{137,1},{2... | collective-permute-start | bytes 393224 | tf_op jit(solution)/shard_map/ppermute | solution.py:357
  11.2 11.7 %collective-permute-start.1 = (bf16[64,1024]{1,0:T(8,128)(2,1)S(1)}, bf16[64,1024]{1,0:T(8,128)(2,1)S(1)}, u32[]{:S(2)}, u32[]{:S(2)}) collective-permute-start(bf16[64,1024]{1,0:T(8,128)(2,1)S(1)} %get-tuple-element.25), channel_id=1, source_target_pairs={{0,128},{8,136},{128,0},{136,8},{1,129},{9,137},{129,1},{137,9},{2... | collective-permute-start | bytes 393224 | tf_op jit(solution)/shard_map/ppermute | solution.py:357
  12.0 11.0 %collective-permute-start.2 = (bf16[64,1024]{1,0:T(8,128)(2,1)S(1)}, bf16[64,1024]{1,0:T(8,128)(2,1)S(1)}, u32[]{:S(2)}, u32[]{:S(2)}) collective-permute-start(bf16[64,1024]{1,0:T(8,128)(2,1)S(1)} %get-tuple-element.26), channel_id=1, source_target_pairs={{0,136},{8,0},{128,8},{136,128},{1,137},{9,1},{129,9},{137,129},{2... | collective-permute-start | bytes 393224 | tf_op jit(solution)/shard_map/ppermute | solution.py:357
  12.8 10.4 %collective-permute-start.10 = (bf16[128,512]{1,0:T(8,128)(2,1)S(1)}, bf16[128,512]{1,0:T(8,128)(2,1)S(1)}, u32[]{:S(2)}, u32[]{:S(2)}) collective-permute-start(bf16[128,512]{1,0:T(8,128)(2,1)S(1)} %copy-done.1), channel_id=1, source_target_pairs={{0,64},{16,80},{32,96},{48,112},{64,0},{80,16},{96,32},{112,48},{1... | collective-permute-start | bytes 393224 | tf_op jit(solution)/shard_map/ppermute | solution.py:367
  18.6 21.0 %collective-permute-start.3 = (bf16[2080,128]{1,0:T(8,128)(2,1)S(1)}, bf16[2080,128]{1,0:T(8,128)(2,1)S(1)}, u32[]{:S(2)}, u32[]{:S(2)}) collective-permute-start(bf16[2080,128]{1,0:T(8,128)(2,1)S(1)} %prep.2.ch_ref), channel_id=1, source_target_pairs={{0,16},{16,32},{32,48},{48,64},{64,80},{80,96},{96,112},{112,0},{1... | collective-permute-start | bytes 1597448 | tf_op jit(solution)/shard_map/ppermute | solution.py:378
  21.9 20.0 %collective-permute-start.6 = (bf16[2080,128]{1,0:T(8,128)(2,1)S(1)}, bf16[2080,128]{1,0:T(8,128)(2,1)S(1)}, u32[]{:S(2)}, u32[]{:S(2)}) collective-permute-start(bf16[2080,128]{1,0:T(8,128)(2,1)S(1)} %prep.2.ch_ref), channel_id=1, source_target_pairs={{0,112},{16,0},{32,16},{48,32},{64,48},{80,64},{96,80},{112,96},{1... | collective-permute-start | bytes 1597448 | tf_op jit(solution)/shard_map/ppermute | solution.py:379
  23.0 18.8 %collective-permute-start.9 = (bf16[4,64,1024]{2,1,0:T(8,128)(2,1)S(1)}, bf16[4,64,1024]{2,1,0:T(8,128)(2,1)S(1)}, u32[]{:S(2)}, u32[]{:S(2)}) collective-permute-start(bf16[4,64,1024]{2,1,0:T(8,128)(2,1)S(1)} %shard_map.38.q0.refs_0_), channel_id=1, source_target_pairs={{0,1},{1,0},{2,3},{3,2},{4,5},{5,4},{6,7},{7,6},{8,9},{9,8},{10,11... | collective-permute-start | bytes 1572872 | tf_op jit(solution)/shard_map/ppermute | solution.py:373
  39.7 14.6 %collective-permute-start.4 = (bf16[2080,128]{1,0:T(8,128)(2,1)S(1)}, bf16[2080,128]{1,0:T(8,128)(2,1)S(1)}, u32[]{:S(2)}, u32[]{:S(2)}) collective-permute-start(bf16[2080,128]{1,0:T(8,128)(2,1)S(1)} %collective-permute-done.3.refs_2_), channel_id=1, source_target_pairs={{0,16},{16,32},{32,48},{48,64},{64,80},{80,96},{96,112},{112,0},{1... | collective-permute-start | bytes 1597448 | tf_op jit(solution)/shard_map/ppermute | solution.py:378
  41.9 14.3 %collective-permute-start.7 = (bf16[2080,128]{1,0:T(8,128)(2,1)S(1)}, bf16[2080,128]{1,0:T(8,128)(2,1)S(1)}, u32[]{:S(2)}, u32[]{:S(2)}) collective-permute-start(bf16[2080,128]{1,0:T(8,128)(2,1)S(1)} %collective-permute-done.6.refs_3_), channel_id=1, source_target_pairs={{0,112},{16,0},{32,16},{48,32},{64,48},{80,64},{96,80},{112,96},{1... | collective-permute-start | bytes 1597448 | tf_op jit(solution)/shard_map/ppermute | solution.py:379
  54.3 13.0 %collective-permute-start.5 = (bf16[2080,128]{1,0:T(8,128)(2,1)S(1)}, bf16[2080,128]{1,0:T(8,128)(2,1)S(1)}, u32[]{:S(2)}, u32[]{:S(2)}) collective-permute-start(bf16[2080,128]{1,0:T(8,128)(2,1)S(1)} %collective-permute-done.4.refs_2_), channel_id=1, source_target_pairs={{0,16},{16,32},{32,48},{48,64},{64,80},{80,96},{96,112},{112,0},{1... | collective-permute-start | bytes 1597448 | tf_op jit(solution)/shard_map/ppermute | solution.py:378
  56.1 11.2 %collective-permute-start.8 = (bf16[2080,128]{1,0:T(8,128)(2,1)S(1)}, bf16[2080,128]{1,0:T(8,128)(2,1)S(1)}, u32[]{:S(2)}, u32[]{:S(2)}) collective-permute-start(bf16[2080,128]{1,0:T(8,128)(2,1)S(1)} %collective-permute-done.7.refs_3_), channel_id=1, source_target_pairs={{0,112},{16,0},{32,16},{48,32},{64,48},{80,64},{96,80},{112,96},{1... | collective-permute-start | bytes 1597448 | tf_op jit(solution)/shard_map/ppermute | solution.py:379
  81.7 53.8 %collective-permute-start.11 = (f32[4,2,136,256]{3,2,1,0:T(8,128)S(1)}, f32[4,2,136,256]{3,2,1,0:T(8,128)S(1)}, u32[]{:S(2)}, u32[]{:S(2)}) collective-permute-start(f32[4,2,136,256]{3,2,1,0:T(8,128)S(1)} %ring.9), channel_id=1, source_target_pairs={{0,1},{1,0},{2,3},{3,2},{4,5},{5,4},{6,7},{7,6},{8,9},{9,8},{10,11... | collective-permute-start | bytes 3342344 | tf_op jit(solution)/shard_map/ppermute | solution.py:386
  136.3 5.5 %collective-permute-start.12 = (bf16[64,1024]{1,0:T(8,128)(2,1)S(1)}, bf16[64,1024]{1,0:T(8,128)(2,1)S(1)}, u32[]{:S(2)}, u32[]{:S(2)}) collective-permute-start(bf16[64,1024]{1,0:T(8,128)(2,1)S(1)} %get-tuple-element.38), channel_id=1, source_target_pairs={{0,8},{8,128},{128,136},{136,0},{1,9},{9,129},{129,137},{137,1},{2... | collective-permute-start | bytes 393224 | tf_op jit(solution)/shard_map/ppermute | solution.py:357
  137.9 7.7 %collective-permute-start.13 = (bf16[64,1024]{1,0:T(8,128)(2,1)S(1)}, bf16[64,1024]{1,0:T(8,128)(2,1)S(1)}, u32[]{:S(2)}, u32[]{:S(2)}) collective-permute-start(bf16[64,1024]{1,0:T(8,128)(2,1)S(1)} %get-tuple-element.39), channel_id=1, source_target_pairs={{0,128},{8,136},{128,0},{136,8},{1,129},{9,137},{129,1},{137,9},{2... | collective-permute-start | bytes 393224 | tf_op jit(solution)/shard_map/ppermute | solution.py:357
  139.2 7.3 %collective-permute-start.14 = (bf16[64,1024]{1,0:T(8,128)(2,1)S(1)}, bf16[64,1024]{1,0:T(8,128)(2,1)S(1)}, u32[]{:S(2)}, u32[]{:S(2)}) collective-permute-start(bf16[64,1024]{1,0:T(8,128)(2,1)S(1)} %get-tuple-element.40), channel_id=1, source_target_pairs={{0,136},{8,0},{128,8},{136,128},{1,137},{9,1},{129,9},{137,129},{2... | collective-permute-start | bytes 393224 | tf_op jit(solution)/shard_map/ppermute | solution.py:357

commit v5 on v4

--- a/solution.py
+++ b/solution.py
@@ -21,6 +21,7 @@
 VMEM = pl.BlockSpec(memory_space=pltpu.VMEM)
 SMEM = pl.BlockSpec(memory_space=pltpu.SMEM)
 ANY = pl.BlockSpec(memory_space=pl.ANY)
+HBM = pl.BlockSpec(memory_space=pltpu.HBM)
 
 
 def prep_kernel(kv_ref, out_ref):
@@ -41,14 +42,22 @@
         out_ref[base + 1024 : base + HALF, :] = bound
 
 
-def prep(kv):
+def prep_far_kernel(kv_hbm, out_ref, kv_ref, sem):
+    copy = pltpu.make_async_copy(kv_hbm, kv_ref, sem)
+    copy.start()
+    copy.wait()
+    prep_kernel(kv_ref, out_ref)
+
+
+def prep(kv, far=False):
     return pl.pallas_call(
-        prep_kernel,
+        prep_far_kernel if far else prep_kernel,
         out_shape=jax.ShapeDtypeStruct((2 * HALF, DH), jnp.bfloat16),
-        in_specs=[VMEM],
+        in_specs=[HBM if far else VMEM],
         out_specs=VMEM,
+        scratch_shapes=[pltpu.VMEM((16, 2 * STRIP, DH), jnp.bfloat16), pltpu.SemaphoreType.DMA] if far else [],
         name="prep",
-        compiler_params=pltpu.CompilerParams(vmem_limit_bytes=2 * 1024 * 1024),
+        compiler_params=pltpu.CompilerParams(vmem_limit_bytes=3 * 1024 * 1024),
         cost_estimate=pl.CostEstimate(flops=1000000, bytes_accessed=1000000, transcendentals=0),
     )(kv)
 
@@ -202,18 +211,25 @@
     both_ways(is_fast(st0, [get]), run)
 
 
-def step_kernel(n_chunks, first, n_rows, sc_ref, *refs):
-    q_refs, given, held = refs[:n_rows], refs[n_rows : n_rows + n_chunks], refs[-1]
-    refs = (q_refs, refs[-1 - n_rows : -1], sc_ref[0])
+def step_kernel(in_hbm, flags, n_rows, sc_ref, *refs):
+    n_chunks = len(in_hbm)
+    q_refs, given, held, sems = refs[:n_rows], refs[n_rows : n_rows + n_chunks], refs[-2], refs[-1]
+    refs = (q_refs, refs[-2 - n_rows : -2], sc_ref[0])
+    copies = [pltpu.make_async_copy(given[j], held.at[j], sems.at[j]) for j in range(n_chunks) if in_hbm[j]]
+    for copy in copies:
+        copy.start()
     for j in range(n_chunks):
-        held[j] = given[j][...]
+        if not in_hbm[j]:
+            held[j] = given[j][...]
+    for copy in copies:
+        copy.wait()
 
     def chunk(j):
         return lambda at, n: held[j, pl.ds(at, n), :]
 
     def run(fast):
         def each(j, carry):
-            before = sc_ref[first + 4 * j]
+            before = sc_ref[flags[0] + flags[1] * j]
             if fast:
 
                 @pl.when(before == 1)
@@ -267,15 +283,15 @@
     )(sc, q0, q1, chunk)
 
 
-def ring_step(sc, qs, state, chunks, first):
+def ring_step(sc, qs, state, chunks, flags, in_hbm):
     n, n_rows = len(chunks), len(qs)
     return pl.pallas_call(
-        functools.partial(step_kernel, n, first, n_rows),
+        functools.partial(step_kernel, in_hbm, flags, n_rows),
         out_shape=ST[:n_rows],
-        in_specs=[SMEM] + [VMEM] * (n + 2 * n_rows),
+        in_specs=[SMEM] + [VMEM] * n_rows + [HBM if h else VMEM for h in in_hbm] + [VMEM] * n_rows,
         out_specs=(VMEM,) * n_rows,
         input_output_aliases={1 + n_rows + n + i: i for i in range(n_rows)},
-        scratch_shapes=[pltpu.VMEM((n, 2 * HALF, DH), jnp.bfloat16)],
+        scratch_shapes=[pltpu.VMEM((n, 2 * HALF, DH), jnp.bfloat16), pltpu.SemaphoreType.DMA((n,))],
         name="ring",
         compiler_params=pltpu.CompilerParams(vmem_limit_bytes=8 * 1024 * 1024),
         cost_estimate=cost(2 * n * n_rows),
@@ -367,7 +383,7 @@
     raw = lax.ppermute(raw, "z", [(i, (i + nz // 2) % nz) for i in range(nz)])
     far = small(spread, sent, 1, False)(raw)
     far = lax.all_to_all(far, ("yh", "yl", "x"), split_axis=0, concat_axis=0, tiled=True)
-    far = prep(far)
+    far = prep(far, True)
     q_pieces = regroup(small(q_send_kernel, (piece,) * 4, 1)(sc, queries))
     q0 = small(join_kernel, jax.ShapeDtypeStruct((4, STRIP, 8 * DH), bf16), 4, False)(*q_pieces)
     q1 = lax.ppermute(q0, "c", swap)
@@ -379,12 +395,11 @@
         bwd.append(lax.ppermute(bwd[-1], "z", down))
 
     state = own_step(sc, q0, q1, chunk)
-    for k in range(1, 3):
-        state = ring_step(sc, (q0, q1), state, (fwd[k], bwd[k]), 2 + k)
-    state = ring_step(sc, (q0, q1), state, (far,), 6)
-    (theirs,) = ring_step(sc, (q1,), state[1:], (fwd[3], bwd[3]), 5)
+    state = ring_step(sc, (q0, q1), state, (fwd[1], bwd[1]), (3, 4), (True, True))
+    state = ring_step(sc, (q0, q1), state, (fwd[2], far, bwd[2]), (4, 2), (True, False, True))
+    (theirs,) = ring_step(sc, (q1,), state[1:], (fwd[3], bwd[3]), (5, 4), (False, False))
     other = lax.ppermute(theirs, "c", swap)
-    (ours,) = ring_step(sc, (q0,), state[:1], (fwd[3], bwd[3]), 5)
+    (ours,) = ring_step(sc, (q0,), state[:1], (fwd[3], bwd[3]), (5, 4), (False, False))
     pieces = small(merge_kernel, (piece,) * 4, 2)(sc, ours, other)
     out = jax.ShapeDtypeStruct((STRIP, H * DH), bf16)
     sems = [pltpu.SemaphoreType.DMA((4,))]

time: 151 us -> 160 us (1.060)
  starting transfers between devices: 62.1 us -> 72.3 us
    ppermute x1, starting transfers between devices: 39.5 us -> 49.7 us  [per_device(): other = lax.ppermute(theirs, 'c', swap)]
    pallas_call x7 -> x6, Pallas kernels: 47.2 us -> 46.8 us  [the longest x4 46.1 us: ring_step(): pl.pallas_call(functools.partial(step_kernel, in_hbm, flags, n_rows), out...]
  transfers between devices with their start and end apart: 16 -> 16, of which waited for: 6 -> 7; matrix products, arithmetic and copies ran while one was open for 0% -> 0% of each run, Pallas kernels for 26% -> 24%
where the time goes in v5:
time: 160 us; the launch traced here: 158 us
  starting transfers between devices  72.3 us (45%)
  Pallas kernels  56.6 us (35%)
  blocking collectives  16.1 us (10%)
  waiting for transfers between devices  12.3 us (8%)
    ppermute x1, starting transfers between devices, per_device(): other = lax.ppermute(theirs, 'c', swap)  49.7 us
    pallas_call x4, Pallas kernels, ring_step(): pl.pallas_call(functools.partial(step_kernel, in_hbm, flags, n_rows), out...  46.1 us
    all_to_all x1, blocking collectives, per_device(): lax.all_to_all(far, ('yh', 'yl', 'x'), split_axis=0, concat_axis=0, tiled...  16.1 us
    ppermute x6, starting transfers between devices, regroup(): lax.ppermute(pieces[d], ('yh', 'yl'), [(i, (i + d) % ny) for i in range(n...  8.21 us
    ppermute x6, waiting for transfers between devices, regroup(): lax.ppermute(pieces[d], ('yh', 'yl'), [(i, (i + d) % ny) for i in range(n...  8.01 us
    all_to_all x1, starting transfers between devices, per_device(): lax.all_to_all(kv, ('yh', 'yl', 'x'), split_axis=0, concat_axis=0, tiled=...  7.43 us
    pallas_call x1, Pallas kernels, own_step(): pl.pallas_call(own_kernel, out_shape=ST, in_specs=[SMEM, VMEM, VMEM, VMEM...  5.17 us
    ppermute x3, starting transfers between devices, per_device(): fwd.append(lax.ppermute(fwd[-1], 'z', up))  4.16 us
  transfers between devices with their start and end apart: 16, of which 7 were waited for; matrix products, arithmetic and copies ran while one was open for 0% of the time, Pallas kernels for 24%

profile of v5, /device:TPU:240, one launch (start us, length us, event | category | flops | bytes accessed | tf_op | source)
XLA Modules:
  0.0 157.7 jit_solution(7513883242353607760)
XLA Ops:
  0.0 0.0 copy-start
  0.0 1.8 %shard_map.39 = (bf16[16,128,128]{2,1,0:T(8,128)(2,1)}, bf16[128,512]{1,0:T(8,128)(2,1)}) custom-call(bf16[64,512]{1,0:T(8,128)(2,1)} %k_hbm.1, bf16[64,512]{1,0:T(8,128)(2,1)} %v_hbm.1), custom_call_target="tpu_custom_call" | custom-call | flops 1000000 | bytes 1000000 | tf_op jit(solution)/shard_map/pallas_call | solution.py:381
  1.8 0.0 copy-start.1
  1.8 7.4 %all-to-all-start = ((bf16[16,128,128]{2,1,0:T(8,128)(2,1)}), bf16[16,128,128]{2,1,0:T(8,128)(2,1)S(1)}, u32[]{:S(2)}, u32[]{:S(2)}) async-start(bf16[16,128,128]{2,1,0:T(8,128)(2,1)} %get-tuple-element.25), calls=%async_computation | async-start | bytes 1048576 | tf_op jit(solution)/shard_map/all_to_all | solution.py:382
  9.3 0.1 stack.79.sc_ref
  9.3 0.0 copy-done
  9.3 0.6 shard_map.37
  9.9 1.2 collective-permute-start
  11.2 0.9 collective-permute-start.1
  12.0 0.7 collective-permute-start.2
  12.8 0.0 copy-done.1
  12.8 1.4 collective-permute-start.10
  14.2 4.1 %all-to-all-done.kv_ref = bf16[16,128,128]{2,1,0:T(8,128)(2,1)S(1)} async-done(((bf16[16,128,128]{2,1,0:T(8,128)(2,1)}), bf16[16,128,128]{2,1,0:T(8,128)(2,1)S(1)}, u32[]{:S(2)}, u32[]{:S(2)}) %all-to-all-start) | async-done | bytes 524320 | tf_op jit(solution)/shard_map/all_to_all | solution.py:382
  18.3 0.3 prep.2.ch_ref
  18.6 0.1 collective-permute-start.3
  18.7 3.2 %collective-permute-done.b_ref = bf16[64,1024]{1,0:T(8,128)(2,1)S(1)} collective-permute-done((bf16[64,1024]{1,0:T(8,128)(2,1)S(1)}, bf16[64,1024]{1,0:T(8,128)(2,1)S(1)}, u32[]{:S(2)}, u32[]{:S(2)}) %collective-permute-start) | collective-permute-done | bytes 131104 | tf_op jit(solution)/shard_map/ppermute | solution.py:373
  21.9 1.0 collective-permute-start.6
  22.9 0.0 collective-permute-done.1.c_ref
  22.9 0.1 collective-permute-done.2.d_ref
  23.0 0.1 collective-permute-start.9
  23.1 0.0 collective-permute-done.10.raw_ref
  23.2 0.1 shard_map.40
  23.2 16.1 %all_to_all.10.kv_hbm = bf16[16,128,128]{2,1,0:T(8,128)(2,1)S(1)} all-to-all(bf16[16,128,128]{2,1,0:T(8,128)(2,1)S(1)} %shard_map.40), channel_id=1, replica_groups=mesh['yh'=2,'z'=8,'yl'=2,'x'=4,'c'=2] {'yh','yl','x'}, dimensions={0} | all-to-all | bytes 1048576 | tf_op jit(solution)/shard_map/all_to_all | solution.py:385
  39.4 0.4 prep.3.refs_3_
  39.7 0.0 collective-permute-done.3.refs_2_
  39.7 2.2 %collective-permute-start.4 = (bf16[2080,128]{1,0:T(8,128)(2,1)S(1)}, bf16[2080,128]{1,0:T(8,128)(2,1)S(1)}, u32[]{:S(2)}, u32[]{:S(2)}) collective-permute-start(bf16[2080,128]{1,0:T(8,128)(2,1)S(1)} %collective-permute-done.3.refs_2_), channel_id=1, source_target_pairs={{0,16},{16,32},{32,48},{48,64},{64,80},{80,96},{96,112},{112,0},{1... | collective-permute-start | bytes 1597448 | tf_op jit(solution)/shard_map/ppermute | solution.py:394
  41.9 0.0 collective-permute-done.6.refs_3_
  41.9 0.0 collective-permute-start.7
  41.9 0.0 collective-permute-done.9.q1.refs_1_.refs_0_
  41.9 5.2 %own.1 = (f32[4,2,136,256]{3,2,1,0:T(8,128)S(1)}, f32[4,2,136,256]{3,2,1,0:T(8,128)S(1)}) custom-call(s32[11]{0:T(128)S(1)} %stack.79.sc_ref, bf16[4,64,1024]{2,1,0:T(8,128)(2,1)S(1)} %shard_map.38.q0.refs_0_, bf16[4,64,1024]{2,1,0:T(8,128)(2,1)S(1)} %collective-permute-done.9.q1.refs_1_.refs_0_, bf16[2080,128]{1,0:T(8,128)(2,1)S(1)} %prep.2.ch_ref), custom_call_target="tpu_custom_call" | custom-call | flops 3221225472 | bytes 6000000 | tf_op jit(solution)/shard_map/own/pallas_call | solution.py:275
  47.1 7.2 %ring.4 = (f32[4,2,136,256]{3,2,1,0:T(8,128)S(1)}, f32[4,2,136,256]{3,2,1,0:T(8,128)S(1)}) custom-call(s32[11]{0:T(128)S(1)} %stack.79.sc_ref, bf16[4,64,1024]{2,1,0:T(8,128)(2,1)S(1)} %shard_map.38.q0.refs_0_, bf16[4,64,1024]{2,1,0:T(8,128)(2,1)S(1)} %collective-permute-done.9.q1.refs_1_.refs_0_, ...), custom_call_target="tpu_custom_call", output_to_operand_aliasing={{0}: (5, {}), {1}: (6, {})} | custom-call | flops 4294967296 | bytes 6000000 | tf_op jit(solution)/shard_map/ring/pallas_call | solution.py:288
  54.3 0.0 collective-permute-done.4.refs_2_
  54.3 1.9 %collective-permute-start.5 = (bf16[2080,128]{1,0:T(8,128)(2,1)S(1)}, bf16[2080,128]{1,0:T(8,128)(2,1)S(1)}, u32[]{:S(2)}, u32[]{:S(2)}) collective-permute-start(bf16[2080,128]{1,0:T(8,128)(2,1)S(1)} %collective-permute-done.4.refs_2_), channel_id=1, source_target_pairs={{0,16},{16,32},{32,48},{48,64},{64,80},{80,96},{96,112},{112,0},{1... | collective-permute-start | bytes 1597448 | tf_op jit(solution)/shard_map/ppermute | solution.py:394
  56.2 0.0 collective-permute-done.7.refs_4_
  56.2 0.2 collective-permute-start.8
  56.4 10.1 %ring.5 = (f32[4,2,136,256]{3,2,1,0:T(8,128)S(1)}, f32[4,2,136,256]{3,2,1,0:T(8,128)S(1)}) custom-call(s32[11]{0:T(128)S(1)} %stack.79.sc_ref, bf16[4,64,1024]{2,1,0:T(8,128)(2,1)S(1)} %shard_map.38.q0.refs_0_, bf16[4,64,1024]{2,1,0:T(8,128)(2,1)S(1)} %collective-permute-done.9.q1.refs_1_.refs_0_, ...), custom_call_target="tpu_custom_call", output_to_operand_aliasing={{0}: (6, {}), {1}: (7, {})} | custom-call | flops 6442450944 | bytes 6000000 | tf_op jit(solution)/shard_map/ring/pallas_call | solution.py:288
  66.5 0.0 collective-permute-done.5.refs_1_
  66.5 0.2 collective-permute-done.8.refs_2_
  66.7 14.3 %ring.7 = f32[4,2,136,256]{3,2,1,0:T(8,128)S(1)} custom-call(s32[11]{0:T(128)S(1)} %stack.79.sc_ref, bf16[4,64,1024]{2,1,0:T(8,128)(2,1)S(1)} %collective-permute-done.9.q1.refs_1_.refs_0_, bf16[2080,128]{1,0:T(8,128)(2,1)S(1)} %collective-permute-done.5.refs_1_, ...), custom_call_target="tpu_custom_call", output_to_operand_aliasing={{}: (4, {})} | custom-call | flops 2147483648 | bytes 6000000 | tf_op jit(solution)/shard_map/ring/pallas_call | solution.py:288
  81.0 49.7 %collective-permute-start.11 = (f32[4,2,136,256]{3,2,1,0:T(8,128)S(1)}, f32[4,2,136,256]{3,2,1,0:T(8,128)S(1)}, u32[]{:S(2)}, u32[]{:S(2)}) collective-permute-start(f32[4,2,136,256]{3,2,1,0:T(8,128)S(1)} %ring.7), channel_id=1, source_target_pairs={{0,1},{1,0},{2,3},{3,2},{4,5},{5,4},{6,7},{7,6},{8,9},{9,8},{10,11... | collective-permute-start | bytes 3342344 | tf_op jit(solution)/shard_map/ppermute | solution.py:401
  130.7 14.5 %ring.6.s_ref = f32[4,2,136,256]{3,2,1,0:T(8,128)S(1)} custom-call(s32[11]{0:T(128)S(1)} %stack.79.sc_ref, bf16[4,64,1024]{2,1,0:T(8,128)(2,1)S(1)} %shard_map.38.q0.refs_0_, bf16[2080,128]{1,0:T(8,128)(2,1)S(1)} %collective-permute-done.5.refs_1_, bf16[2080,128]{1,0:T(8,128)(2,1)S(1)} %collective-permute-done.8.refs_2_, ...), custom_call_target="tpu_custom_call", output_to_operand_aliasing={{}: (4, {})} | custom-call | flops 2147483648 | bytes 6000000 | tf_op jit(solution)/shard_map/ring/pallas_call | solution.py:288
  145.2 0.0 collective-permute-done.11.r_ref
  145.2 0.8 shard_map.41
  146.1 1.5 collective-permute-start.12
  147.6 1.3 collective-permute-start.13
  148.9 2.5 %collective-permute-start.14 = (bf16[64,1024]{1,0:T(8,128)(2,1)S(1)}, bf16[64,1024]{1,0:T(8,128)(2,1)S(1)}, u32[]{:S(2)}, u32[]{:S(2)}) collective-permute-start(bf16[64,1024]{1,0:T(8,128)(2,1)S(1)} %get-tuple-element.36), channel_id=1, source_target_pairs={{0,136},{8,0},{128,8},{136,128},{1,137},{9,1},{129,9},{137,129},{2... | collective-permute-start | bytes 393224 | tf_op jit(solution)/shard_map/ppermute | solution.py:373
  151.4 0.1 collective-permute-done.12.refs_1_
  151.5 3.7 %collective-permute-done.13.refs_2_ = bf16[64,1024]{1,0:T(8,128)(2,1)S(1)} collective-permute-done((bf16[64,1024]{1,0:T(8,128)(2,1)S(1)}, bf16[64,1024]{1,0:T(8,128)(2,1)S(1)}, u32[]{:S(2)}, u32[]{:S(2)}) %collective-permute-start.13) | collective-permute-done | bytes 131104 | tf_op jit(solution)/shard_map/ppermute | solution.py:373
  155.3 0.9 collective-permute-done.14.refs_3_
  156.2 1.4 shard_map.42
  (1 shorter events, 0.0 us)
Async XLA Ops:
  0.0 9.3 %copy-start = (bf16[64,4096]{1,0:T(8,128)(2,1)S(1)}, bf16[64,4096]{1,0:T(8,128)(2,1)}, u32[]{:S(2)}) copy-start(bf16[64,4096]{1,0:T(8,128)(2,1)} %q_ref.1) | copy-start | bytes 1572868
  1.8 11.0 %copy-start.1 = (bf16[128,512]{1,0:T(8,128)(2,1)S(1)}, bf16[128,512]{1,0:T(8,128)(2,1)}, u32[]{:S(2)}) copy-start(bf16[128,512]{1,0:T(8,128)(2,1)} %get-tuple-element.26) | copy-start | bytes 393220
  1.8 16.5 %all-to-all-start = ((bf16[16,128,128]{2,1,0:T(8,128)(2,1)}), bf16[16,128,128]{2,1,0:T(8,128)(2,1)S(1)}, u32[]{:S(2)}, u32[]{:S(2)}) async-start(bf16[16,128,128]{2,1,0:T(8,128)(2,1)} %get-tuple-element.25), calls=%async_computation | async-start | bytes 1048576 | tf_op jit(solution)/shard_map/all_to_all | solution.py:382
  9.9 11.9 %collective-permute-start = (bf16[64,1024]{1,0:T(8,128)(2,1)S(1)}, bf16[64,1024]{1,0:T(8,128)(2,1)S(1)}, u32[]{:S(2)}, u32[]{:S(2)}) collective-permute-start(bf16[64,1024]{1,0:T(8,128)(2,1)S(1)} %get-tuple-element.22), channel_id=1, source_target_pairs={{0,8},{8,128},{128,136},{136,0},{1,9},{9,129},{129,137},{137,1},{2... | collective-permute-start | bytes 393224 | tf_op jit(solution)/shard_map/ppermute | solution.py:373
  11.2 11.7 %collective-permute-start.1 = (bf16[64,1024]{1,0:T(8,128)(2,1)S(1)}, bf16[64,1024]{1,0:T(8,128)(2,1)S(1)}, u32[]{:S(2)}, u32[]{:S(2)}) collective-permute-start(bf16[64,1024]{1,0:T(8,128)(2,1)S(1)} %get-tuple-element.23), channel_id=1, source_target_pairs={{0,128},{8,136},{128,0},{136,8},{1,129},{9,137},{129,1},{137,9},{2... | collective-permute-start | bytes 393224 | tf_op jit(solution)/shard_map/ppermute | solution.py:373
  12.0 11.0 %collective-permute-start.2 = (bf16[64,1024]{1,0:T(8,128)(2,1)S(1)}, bf16[64,1024]{1,0:T(8,128)(2,1)S(1)}, u32[]{:S(2)}, u32[]{:S(2)}) collective-permute-start(bf16[64,1024]{1,0:T(8,128)(2,1)S(1)} %get-tuple-element.24), channel_id=1, source_target_pairs={{0,136},{8,0},{128,8},{136,128},{1,137},{9,1},{129,9},{137,129},{2... | collective-permute-start | bytes 393224 | tf_op jit(solution)/shard_map/ppermute | solution.py:373
  12.8 10.4 %collective-permute-start.10 = (bf16[128,512]{1,0:T(8,128)(2,1)S(1)}, bf16[128,512]{1,0:T(8,128)(2,1)S(1)}, u32[]{:S(2)}, u32[]{:S(2)}) collective-permute-start(bf16[128,512]{1,0:T(8,128)(2,1)S(1)} %copy-done.1), channel_id=1, source_target_pairs={{0,64},{16,80},{32,96},{48,112},{64,0},{80,16},{96,32},{112,48},{1... | collective-permute-start | bytes 393224 | tf_op jit(solution)/shard_map/ppermute | solution.py:383
  18.6 21.1 %collective-permute-start.3 = (bf16[2080,128]{1,0:T(8,128)(2,1)S(1)}, bf16[2080,128]{1,0:T(8,128)(2,1)S(1)}, u32[]{:S(2)}, u32[]{:S(2)}) collective-permute-start(bf16[2080,128]{1,0:T(8,128)(2,1)S(1)} %prep.2.ch_ref), channel_id=1, source_target_pairs={{0,16},{16,32},{32,48},{48,64},{64,80},{80,96},{96,112},{112,0},{1... | collective-permute-start | bytes 1597448 | tf_op jit(solution)/shard_map/ppermute | solution.py:394
  21.9 20.0 %collective-permute-start.6 = (bf16[2080,128]{1,0:T(8,128)(2,1)S(1)}, bf16[2080,128]{1,0:T(8,128)(2,1)S(1)}, u32[]{:S(2)}, u32[]{:S(2)}) collective-permute-start(bf16[2080,128]{1,0:T(8,128)(2,1)S(1)} %prep.2.ch_ref), channel_id=1, source_target_pairs={{0,112},{16,0},{32,16},{48,32},{64,48},{80,64},{96,80},{112,96},{1... | collective-permute-start | bytes 1597448 | tf_op jit(solution)/shard_map/ppermute | solution.py:395
  23.0 18.9 %collective-permute-start.9 = (bf16[4,64,1024]{2,1,0:T(8,128)(2,1)S(1)}, bf16[4,64,1024]{2,1,0:T(8,128)(2,1)S(1)}, u32[]{:S(2)}, u32[]{:S(2)}) collective-permute-start(bf16[4,64,1024]{2,1,0:T(8,128)(2,1)S(1)} %shard_map.38.q0.refs_0_), channel_id=1, source_target_pairs={{0,1},{1,0},{2,3},{3,2},{4,5},{5,4},{6,7},{7,6},{8,9},{9,8},{10,11... | collective-permute-start | bytes 1572872 | tf_op jit(solution)/shard_map/ppermute | solution.py:389
  39.7 14.6 %collective-permute-start.4 = (bf16[2080,128]{1,0:T(8,128)(2,1)S(1)}, bf16[2080,128]{1,0:T(8,128)(2,1)S(1)}, u32[]{:S(2)}, u32[]{:S(2)}) collective-permute-start(bf16[2080,128]{1,0:T(8,128)(2,1)S(1)} %collective-permute-done.3.refs_2_), channel_id=1, source_target_pairs={{0,16},{16,32},{32,48},{48,64},{64,80},{80,96},{96,112},{112,0},{1... | collective-permute-start | bytes 1597448 | tf_op jit(solution)/shard_map/ppermute | solution.py:394
  41.9 14.3 %collective-permute-start.7 = (bf16[2080,128]{1,0:T(8,128)(2,1)S(1)}, bf16[2080,128]{1,0:T(8,128)(2,1)S(1)}, u32[]{:S(2)}, u32[]{:S(2)}) collective-permute-start(bf16[2080,128]{1,0:T(8,128)(2,1)S(1)} %collective-permute-done.6.refs_3_), channel_id=1, source_target_pairs={{0,112},{16,0},{32,16},{48,32},{64,48},{80,64},{96,80},{112,96},{1... | collective-permute-start | bytes 1597448 | tf_op jit(solution)/shard_map/ppermute | solution.py:395
  54.3 12.2 %collective-permute-start.5 = (bf16[2080,128]{1,0:T(8,128)(2,1)S(1)}, bf16[2080,128]{1,0:T(8,128)(2,1)S(1)}, u32[]{:S(2)}, u32[]{:S(2)}) collective-permute-start(bf16[2080,128]{1,0:T(8,128)(2,1)S(1)} %collective-permute-done.4.refs_2_), channel_id=1, source_target_pairs={{0,16},{16,32},{32,48},{48,64},{64,80},{80,96},{96,112},{112,0},{1... | collective-permute-start | bytes 1597448 | tf_op jit(solution)/shard_map/ppermute | solution.py:394
  56.2 10.5 %collective-permute-start.8 = (bf16[2080,128]{1,0:T(8,128)(2,1)S(1)}, bf16[2080,128]{1,0:T(8,128)(2,1)S(1)}, u32[]{:S(2)}, u32[]{:S(2)}) collective-permute-start(bf16[2080,128]{1,0:T(8,128)(2,1)S(1)} %collective-permute-done.7.refs_4_), channel_id=1, source_target_pairs={{0,112},{16,0},{32,16},{48,32},{64,48},{80,64},{96,80},{112,96},{1... | collective-permute-start | bytes 1597448 | tf_op jit(solution)/shard_map/ppermute | solution.py:395
  81.0 64.2 %collective-permute-start.11 = (f32[4,2,136,256]{3,2,1,0:T(8,128)S(1)}, f32[4,2,136,256]{3,2,1,0:T(8,128)S(1)}, u32[]{:S(2)}, u32[]{:S(2)}) collective-permute-start(f32[4,2,136,256]{3,2,1,0:T(8,128)S(1)} %ring.7), channel_id=1, source_target_pairs={{0,1},{1,0},{2,3},{3,2},{4,5},{5,4},{6,7},{7,6},{8,9},{9,8},{10,11... | collective-permute-start | bytes 3342344 | tf_op jit(solution)/shard_map/ppermute | solution.py:401
  146.1 5.5 %collective-permute-start.12 = (bf16[64,1024]{1,0:T(8,128)(2,1)S(1)}, bf16[64,1024]{1,0:T(8,128)(2,1)S(1)}, u32[]{:S(2)}, u32[]{:S(2)}) collective-permute-start(bf16[64,1024]{1,0:T(8,128)(2,1)S(1)} %get-tuple-element.34), channel_id=1, source_target_pairs={{0,8},{8,128},{128,136},{136,0},{1,9},{9,129},{129,137},{137,1},{2... | collective-permute-start | bytes 393224 | tf_op jit(solution)/shard_map/ppermute | solution.py:373
  147.6 7.7 %collective-permute-start.13 = (bf16[64,1024]{1,0:T(8,128)(2,1)S(1)}, bf16[64,1024]{1,0:T(8,128)(2,1)S(1)}, u32[]{:S(2)}, u32[]{:S(2)}) collective-permute-start(bf16[64,1024]{1,0:T(8,128)(2,1)S(1)} %get-tuple-element.35), channel_id=1, source_target_pairs={{0,128},{8,136},{128,0},{136,8},{1,129},{9,137},{129,1},{137,9},{2... | collective-permute-start | bytes 393224 | tf_op jit(solution)/shard_map/ppermute | solution.py:373
  148.9 7.3 %collective-permute-start.14 = (bf16[64,1024]{1,0:T(8,128)(2,1)S(1)}, bf16[64,1024]{1,0:T(8,128)(2,1)S(1)}, u32[]{:S(2)}, u32[]{:S(2)}) collective-permute-start(bf16[64,1024]{1,0:T(8,128)(2,1)S(1)} %get-tuple-element.36), channel_id=1, source_target_pairs={{0,136},{8,0},{128,8},{136,128},{1,137},{9,1},{129,9},{137,129},{2... | collective-permute-start | bytes 393224 | tf_op jit(solution)/shard_map/ppermute | solution.py:373

commit v6 on v2

--- a/solution.py
+++ b/solution.py
@@ -312,10 +312,10 @@
     sc = jnp.stack([y, x, c, *flags, *wraps]).astype(jnp.int32)
 
     def regroup(pieces):
-        moved = []
-        for d in range(1, ny):
-            moved.append(lax.ppermute(pieces[d], ("yh", "yl"), [(i, (i + d) % ny) for i in range(ny)]))
-        return [pieces[0], *moved]
+        moved = {0: pieces[0]}
+        for d in (2, 3, 1):
+            moved[d] = lax.ppermute(pieces[d], ("yh", "yl"), [(i, (i + d) % ny) for i in range(ny)])
+        return [moved[d] for d in range(ny)]
 
     bf16 = jnp.bfloat16
     piece = jax.ShapeDtypeStruct((STRIP, 8 * DH), bf16)

time: 156 us -> 156 us (level)
  no operation moved by 1% of the time
where the time goes in v6:
time: 156 us; the launch traced here: 153 us
  starting transfers between devices  62.8 us (40%)
  Pallas kernels  57.4 us (37%)
  blocking collectives  16.4 us (11%)
  waiting for transfers between devices  16.1 us (10%)
    pallas_call x5, Pallas kernels, ring_step(): pl.pallas_call(functools.partial(step_kernel, parts, n_rows), out_shape=S...  47.3 us
    ppermute x1, starting transfers between devices, per_device(): other = lax.ppermute(theirs, 'c', swap)  27.3 us
    ppermute x1, starting transfers between devices, per_device(): far_h = lax.ppermute(bwd[3][HALF:], 'z', down)  17.9 us
    all_to_all x1, blocking collectives, per_device(): lax.all_to_all(kv, ('yh', 'yl', 'x'), split_axis=0, concat_axis=0, tiled=...  16.4 us
    ppermute x6, starting transfers between devices, regroup(): lax.ppermute(pieces[d], ('yh', 'yl'), [(i, (i + d) % ny) for i in range(n...  10.5 us
    ppermute x6, waiting for transfers between devices, regroup(): lax.ppermute(pieces[d], ('yh', 'yl'), [(i, (i + d) % ny) for i in range(n...  8.17 us
    ppermute x3, waiting for transfers between devices, per_device(): fwd.append(lax.ppermute(fwd[-1], 'z', up))  7.27 us
    pallas_call x1, Pallas kernels, own_step(): pl.pallas_call(own_kernel, out_shape=ST, in_specs=[SMEM, VMEM, VMEM, VMEM...  5.2 us
  transfers between devices with their start and end apart: 16, of which 9 were waited for; matrix products, arithmetic and copies ran while one was open for 0% of the time, Pallas kernels for 33%

profile of v6, /device:TPU:240, one launch (start us, length us, event | category | flops | bytes accessed | tf_op | source)
XLA Modules:
  0.0 153.1 jit_solution(14648207738075760949)
XLA Ops:
  0.0 1.7 %shard_map.39 = bf16[16,128,128]{2,1,0:T(8,128)(2,1)} custom-call(bf16[64,512]{1,0:T(8,128)(2,1)} %k_hbm.1, bf16[64,512]{1,0:T(8,128)(2,1)} %v_hbm.1), custom_call_target="tpu_custom_call" | custom-call | flops 1000000 | bytes 1000000 | tf_op jit(solution)/shard_map/pallas_call | solution.py:324
  1.8 0.0 copy-start
  1.8 16.4 %all_to_all.5.kv_ref = bf16[16,128,128]{2,1,0:T(8,128)(2,1)S(1)} all-to-all(bf16[16,128,128]{2,1,0:T(8,128)(2,1)} %shard_map.39), channel_id=1, replica_groups=mesh['yh'=2,'z'=8,'yl'=2,'x'=4,'c'=2] {'yh','yl','x'}, dimensions={0} | all-to-all | bytes 1048576 | tf_op jit(solution)/shard_map/all_to_all | solution.py:325
  18.1 0.3 prep.1.ch_ref
  18.4 0.1 collective-permute-start.3
  18.5 2.0 %collective-permute-start.7 = (bf16[2080,128]{1,0:T(8,128)(2,1)S(1)}, bf16[2080,128]{1,0:T(8,128)(2,1)S(1)}, u32[]{:S(2)}, u32[]{:S(2)}) collective-permute-start(bf16[2080,128]{1,0:T(8,128)(2,1)S(1)} %prep.1.ch_ref), channel_id=1, source_target_pairs={{0,112},{16,0},{32,16},{48,32},{64,48},{80,64},{96,80},{112,96},{1... | collective-permute-start | bytes 1597448 | tf_op jit(solution)/shard_map/ppermute | solution.py:334
  20.6 0.1 stack.79.sc_ref
  20.6 0.0 copy-done
  20.6 0.6 shard_map.37
  21.2 1.5 %collective-permute-start = (bf16[64,1024]{1,0:T(8,128)(2,1)S(1)}, bf16[64,1024]{1,0:T(8,128)(2,1)S(1)}, u32[]{:S(2)}, u32[]{:S(2)}) collective-permute-start(bf16[64,1024]{1,0:T(8,128)(2,1)S(1)} %get-tuple-element.22), channel_id=1, source_target_pairs={{0,8},{8,128},{128,136},{136,0},{1,9},{9,129},{129,137},{137,1},{2... | collective-permute-start | bytes 393224 | tf_op jit(solution)/shard_map/ppermute | solution.py:317
  22.8 1.3 collective-permute-start.1
  24.1 2.5 %collective-permute-start.2 = (bf16[64,1024]{1,0:T(8,128)(2,1)S(1)}, bf16[64,1024]{1,0:T(8,128)(2,1)S(1)}, u32[]{:S(2)}, u32[]{:S(2)}) collective-permute-start(bf16[64,1024]{1,0:T(8,128)(2,1)S(1)} %get-tuple-element.24), channel_id=1, source_target_pairs={{0,136},{8,0},{128,8},{136,128},{1,137},{9,1},{129,9},{137,129},{2... | collective-permute-start | bytes 393224 | tf_op jit(solution)/shard_map/ppermute | solution.py:317
  26.6 1.0 collective-permute-done.b_ref
  27.6 1.7 %collective-permute-done.1.c_ref = bf16[64,1024]{1,0:T(8,128)(2,1)S(1)} collective-permute-done((bf16[64,1024]{1,0:T(8,128)(2,1)S(1)}, bf16[64,1024]{1,0:T(8,128)(2,1)S(1)}, u32[]{:S(2)}, u32[]{:S(2)}) %collective-permute-start.1) | collective-permute-done | bytes 131104 | tf_op jit(solution)/shard_map/ppermute | solution.py:317
  29.2 0.5 collective-permute-done.2.d_ref
  29.8 0.1 collective-permute-start.11
  29.9 1.6 %collective-permute-done.3.refs_2_ = bf16[2080,128]{1,0:T(8,128)(2,1)S(1)} collective-permute-done((bf16[2080,128]{1,0:T(8,128)(2,1)S(1)}, bf16[2080,128]{1,0:T(8,128)(2,1)S(1)}, u32[]{:S(2)}, u32[]{:S(2)}) %collective-permute-start.3) | collective-permute-done | bytes 532512 | tf_op jit(solution)/shard_map/ppermute | solution.py:333
  31.6 1.5 collective-permute-start.4
  33.1 0.0 collective-permute-done.7.refs_3_
  33.1 0.5 collective-permute-start.8
  33.6 0.0 collective-permute-done.11.q1.refs_1_.refs_0_
  33.6 5.2 %own.1 = (f32[4,2,136,256]{3,2,1,0:T(8,128)S(1)}, f32[4,2,136,256]{3,2,1,0:T(8,128)S(1)}) custom-call(s32[11]{0:T(128)S(1)} %stack.79.sc_ref, bf16[4,64,1024]{2,1,0:T(8,128)(2,1)S(1)} %shard_map.38.q0.refs_0_, bf16[4,64,1024]{2,1,0:T(8,128)(2,1)S(1)} %collective-permute-done.11.q1.refs_1_.refs_0_, bf16[2080,128]{1,0:T(8,128)(2,1)S(1)} %prep.1.ch_ref), custom_call_target="tpu_custom_call" | custom-call | flops 3221225472 | bytes 6000000 | tf_op jit(solution)/shard_map/own/pallas_call | solution.py:225
  38.8 5.6 %collective-permute-done.4.refs_2_ = bf16[2080,128]{1,0:T(8,128)(2,1)S(1)} collective-permute-done((bf16[2080,128]{1,0:T(8,128)(2,1)S(1)}, bf16[2080,128]{1,0:T(8,128)(2,1)S(1)}, u32[]{:S(2)}, u32[]{:S(2)}) %collective-permute-start.4) | collective-permute-done | bytes 532512 | tf_op jit(solution)/shard_map/ppermute | solution.py:333
  44.4 2.8 %collective-permute-start.5 = (bf16[2080,128]{1,0:T(8,128)(2,1)S(1)}, bf16[2080,128]{1,0:T(8,128)(2,1)S(1)}, u32[]{:S(2)}, u32[]{:S(2)}) collective-permute-start(bf16[2080,128]{1,0:T(8,128)(2,1)S(1)} %collective-permute-done.4.refs_2_), channel_id=1, source_target_pairs={{0,16},{16,32},{32,48},{48,64},{64,80},{80,96},{96,112},{112,0},{1... | collective-permute-start | bytes 1597448 | tf_op jit(solution)/shard_map/ppermute | solution.py:333
  47.2 0.0 collective-permute-done.8.refs_3_
  47.2 0.0 collective-permute-start.9
  47.2 7.2 %ring.5 = (f32[4,2,136,256]{3,2,1,0:T(8,128)S(1)}, f32[4,2,136,256]{3,2,1,0:T(8,128)S(1)}) custom-call(s32[11]{0:T(128)S(1)} %stack.79.sc_ref, bf16[4,64,1024]{2,1,0:T(8,128)(2,1)S(1)} %shard_map.38.q0.refs_0_, bf16[4,64,1024]{2,1,0:T(8,128)(2,1)S(1)} %collective-permute-done.11.q1.refs_1_.refs_0_, ...), custom_call_target="tpu_custom_call", output_to_operand_aliasing={{0}: (5, {}), {1}: (6, {})} | custom-call | flops 4294967296 | bytes 6000000 | tf_op jit(solution)/shard_map/ring/pallas_call | solution.py:238
  54.4 7.1 %ring.6 = (f32[4,2,136,256]{3,2,1,0:T(8,128)S(1)}, f32[4,2,136,256]{3,2,1,0:T(8,128)S(1)}) custom-call(s32[11]{0:T(128)S(1)} %stack.79.sc_ref, bf16[4,64,1024]{2,1,0:T(8,128)(2,1)S(1)} %shard_map.38.q0.refs_0_, bf16[4,64,1024]{2,1,0:T(8,128)(2,1)S(1)} %collective-permute-done.11.q1.refs_1_.refs_0_, ...), custom_call_target="tpu_custom_call", output_to_operand_aliasing={{0}: (5, {}), {1}: (6, {})} | custom-call | flops 4294967296 | bytes 6000000 | tf_op jit(solution)/shard_map/ring/pallas_call | solution.py:238
  61.5 0.6 collective-permute-done.9.refs_3_
  62.1 17.9 %collective-permute-start.10 = (bf16[1040,128]{1,0:T(8,128)(2,1)S(1)}, bf16[1040,128]{1,0:T(8,128)(2,1)S(1)}, u32[]{:S(2)}, u32[]{:S(2)}) collective-permute-start(bf16[1040,128]{1,0:T(8,128)(2,1)S(1)} %slice.9), channel_id=1, source_target_pairs={{0,112},{16,0},{32,16},{48,32},{64,48},{80,64},{96,80},{112,96},{1... | collective-permute-start | bytes 798728 | tf_op jit(solution)/shard_map/ppermute | solution.py:336
  80.0 0.0 collective-permute-done.5.refs_2_
  80.1 0.1 collective-permute-start.6
  80.1 27.5 %ring.7 = (f32[4,2,136,256]{3,2,1,0:T(8,128)S(1)}, f32[4,2,136,256]{3,2,1,0:T(8,128)S(1)}) custom-call(s32[11]{0:T(128)S(1)} %stack.79.sc_ref, bf16[4,64,1024]{2,1,0:T(8,128)(2,1)S(1)} %shard_map.38.q0.refs_0_, bf16[4,64,1024]{2,1,0:T(8,128)(2,1)S(1)} %collective-permute-done.11.q1.refs_1_.refs_0_, ...), custom_call_target="tpu_custom_call", output_to_operand_aliasing={{0}: (5, {}), {1}: (6, {})} | custom-call | flops 4294967296 | bytes 6000000 | tf_op jit(solution)/shard_map/ring/pallas_call | solution.py:238
  107.6 0.0 collective-permute-done.10.refs_2_
  107.6 0.0 collective-permute-done.6.refs_1_
  107.6 2.9 %ring.9 = f32[4,2,136,256]{3,2,1,0:T(8,128)S(1)} custom-call(s32[11]{0:T(128)S(1)} %stack.79.sc_ref, bf16[4,64,1024]{2,1,0:T(8,128)(2,1)S(1)} %collective-permute-done.11.q1.refs_1_.refs_0_, bf16[1040,128]{1,0:T(8,128)(2,1)S(1)} %collective-permute-done.6.refs_1_, ...), custom_call_target="tpu_custom_call", output_to_operand_aliasing={{}: (4, {})} | custom-call | flops 2147483648 | bytes 6000000 | tf_op jit(solution)/shard_map/ring/pallas_call | solution.py:238
  110.6 27.3 %collective-permute-start.12 = (f32[4,2,136,256]{3,2,1,0:T(8,128)S(1)}, f32[4,2,136,256]{3,2,1,0:T(8,128)S(1)}, u32[]{:S(2)}, u32[]{:S(2)}) collective-permute-start(f32[4,2,136,256]{3,2,1,0:T(8,128)S(1)} %ring.9), channel_id=1, source_target_pairs={{0,1},{1,0},{2,3},{3,2},{4,5},{5,4},{6,7},{7,6},{8,9},{9,8},{10,11... | collective-permute-start | bytes 3342344 | tf_op jit(solution)/shard_map/ppermute | solution.py:344
  137.9 2.7 %ring.8.s_ref = f32[4,2,136,256]{3,2,1,0:T(8,128)S(1)} custom-call(s32[11]{0:T(128)S(1)} %stack.79.sc_ref, bf16[4,64,1024]{2,1,0:T(8,128)(2,1)S(1)} %shard_map.38.q0.refs_0_, bf16[1040,128]{1,0:T(8,128)(2,1)S(1)} %collective-permute-done.6.refs_1_, bf16[1040,128]{1,0:T(8,128)(2,1)S(1)} %collective-permute-done.10.refs_2_, ...), custom_call_target="tpu_custom_call", output_to_operand_aliasing={{}: (4, {})} | custom-call | flops 2147483648 | bytes 6000000 | tf_op jit(solution)/shard_map/ring/pallas_call | solution.py:238
  140.6 0.0 collective-permute-done.12.r_ref
  140.6 0.9 shard_map.40
  141.4 3.0 %collective-permute-start.13 = (bf16[64,1024]{1,0:T(8,128)(2,1)S(1)}, bf16[64,1024]{1,0:T(8,128)(2,1)S(1)}, u32[]{:S(2)}, u32[]{:S(2)}) collective-permute-start(bf16[64,1024]{1,0:T(8,128)(2,1)S(1)} %get-tuple-element.34), channel_id=1, source_target_pairs={{0,8},{8,128},{128,136},{136,0},{1,9},{9,129},{129,137},{137,1},{2... | collective-permute-start | bytes 393224 | tf_op jit(solution)/shard_map/ppermute | solution.py:317
  144.4 0.1 collective-permute-start.14
  144.5 2.1 %collective-permute-start.15 = (bf16[64,1024]{1,0:T(8,128)(2,1)S(1)}, bf16[64,1024]{1,0:T(8,128)(2,1)S(1)}, u32[]{:S(2)}, u32[]{:S(2)}) collective-permute-start(bf16[64,1024]{1,0:T(8,128)(2,1)S(1)} %get-tuple-element.36), channel_id=1, source_target_pairs={{0,136},{8,0},{128,8},{136,128},{1,137},{9,1},{129,9},{137,129},{2... | collective-permute-start | bytes 393224 | tf_op jit(solution)/shard_map/ppermute | solution.py:317
  146.6 1.8 %collective-permute-done.13.refs_1_ = bf16[64,1024]{1,0:T(8,128)(2,1)S(1)} collective-permute-done((bf16[64,1024]{1,0:T(8,128)(2,1)S(1)}, bf16[64,1024]{1,0:T(8,128)(2,1)S(1)}, u32[]{:S(2)}, u32[]{:S(2)}) %collective-permute-start.13) | collective-permute-done | bytes 131104 | tf_op jit(solution)/shard_map/ppermute | solution.py:317
  148.3 2.8 %collective-permute-done.14.refs_2_ = bf16[64,1024]{1,0:T(8,128)(2,1)S(1)} collective-permute-done((bf16[64,1024]{1,0:T(8,128)(2,1)S(1)}, bf16[64,1024]{1,0:T(8,128)(2,1)S(1)}, u32[]{:S(2)}, u32[]{:S(2)}) %collective-permute-start.14) | collective-permute-done | bytes 131104 | tf_op jit(solution)/shard_map/ppermute | solution.py:317
  151.1 0.5 collective-permute-done.15.refs_3_
  151.6 1.4 shard_map.41
  (3 shorter events, 0.1 us)
Async XLA Ops:
  1.8 18.9 %copy-start = (bf16[64,4096]{1,0:T(8,128)(2,1)S(1)}, bf16[64,4096]{1,0:T(8,128)(2,1)}, u32[]{:S(2)}) copy-start(bf16[64,4096]{1,0:T(8,128)(2,1)} %q_ref.1) | copy-start | bytes 1572868
  18.4 13.1 %collective-permute-start.3 = (bf16[2080,128]{1,0:T(8,128)(2,1)S(1)}, bf16[2080,128]{1,0:T(8,128)(2,1)S(1)}, u32[]{:S(2)}, u32[]{:S(2)}) collective-permute-start(bf16[2080,128]{1,0:T(8,128)(2,1)S(1)} %prep.1.ch_ref), channel_id=1, source_target_pairs={{0,16},{16,32},{32,48},{48,64},{64,80},{80,96},{96,112},{112,0},{1... | collective-permute-start | bytes 1597448 | tf_op jit(solution)/shard_map/ppermute | solution.py:333
  18.5 14.5 %collective-permute-start.7 = (bf16[2080,128]{1,0:T(8,128)(2,1)S(1)}, bf16[2080,128]{1,0:T(8,128)(2,1)S(1)}, u32[]{:S(2)}, u32[]{:S(2)}) collective-permute-start(bf16[2080,128]{1,0:T(8,128)(2,1)S(1)} %prep.1.ch_ref), channel_id=1, source_target_pairs={{0,112},{16,0},{32,16},{48,32},{64,48},{80,64},{96,80},{112,96},{1... | collective-permute-start | bytes 1597448 | tf_op jit(solution)/shard_map/ppermute | solution.py:334
  21.2 6.4 %collective-permute-start = (bf16[64,1024]{1,0:T(8,128)(2,1)S(1)}, bf16[64,1024]{1,0:T(8,128)(2,1)S(1)}, u32[]{:S(2)}, u32[]{:S(2)}) collective-permute-start(bf16[64,1024]{1,0:T(8,128)(2,1)S(1)} %get-tuple-element.22), channel_id=1, source_target_pairs={{0,8},{8,128},{128,136},{136,0},{1,9},{9,129},{129,137},{137,1},{2... | collective-permute-start | bytes 393224 | tf_op jit(solution)/shard_map/ppermute | solution.py:317
  22.8 6.5 %collective-permute-start.1 = (bf16[64,1024]{1,0:T(8,128)(2,1)S(1)}, bf16[64,1024]{1,0:T(8,128)(2,1)S(1)}, u32[]{:S(2)}, u32[]{:S(2)}) collective-permute-start(bf16[64,1024]{1,0:T(8,128)(2,1)S(1)} %get-tuple-element.23), channel_id=1, source_target_pairs={{0,128},{8,136},{128,0},{136,8},{1,129},{9,137},{129,1},{137,9},{2... | collective-permute-start | bytes 393224 | tf_op jit(solution)/shard_map/ppermute | solution.py:317
  24.1 5.7 %collective-permute-start.2 = (bf16[64,1024]{1,0:T(8,128)(2,1)S(1)}, bf16[64,1024]{1,0:T(8,128)(2,1)S(1)}, u32[]{:S(2)}, u32[]{:S(2)}) collective-permute-start(bf16[64,1024]{1,0:T(8,128)(2,1)S(1)} %get-tuple-element.24), channel_id=1, source_target_pairs={{0,136},{8,0},{128,8},{136,128},{1,137},{9,1},{129,9},{137,129},{2... | collective-permute-start | bytes 393224 | tf_op jit(solution)/shard_map/ppermute | solution.py:317
  29.8 3.8 %collective-permute-start.11 = (bf16[4,64,1024]{2,1,0:T(8,128)(2,1)S(1)}, bf16[4,64,1024]{2,1,0:T(8,128)(2,1)S(1)}, u32[]{:S(2)}, u32[]{:S(2)}) collective-permute-start(bf16[4,64,1024]{2,1,0:T(8,128)(2,1)S(1)} %shard_map.38.q0.refs_0_), channel_id=1, source_target_pairs={{0,1},{1,0},{2,3},{3,2},{4,5},{5,4},{6,7},{7,6},{8,9},{9,8},{10,11... | collective-permute-start | bytes 1572872 | tf_op jit(solution)/shard_map/ppermute | solution.py:328
  31.6 12.9 %collective-permute-start.4 = (bf16[2080,128]{1,0:T(8,128)(2,1)S(1)}, bf16[2080,128]{1,0:T(8,128)(2,1)S(1)}, u32[]{:S(2)}, u32[]{:S(2)}) collective-permute-start(bf16[2080,128]{1,0:T(8,128)(2,1)S(1)} %collective-permute-done.3.refs_2_), channel_id=1, source_target_pairs={{0,16},{16,32},{32,48},{48,64},{64,80},{80,96},{96,112},{112,0},{1... | collective-permute-start | bytes 1597448 | tf_op jit(solution)/shard_map/ppermute | solution.py:333
  33.1 14.2 %collective-permute-start.8 = (bf16[2080,128]{1,0:T(8,128)(2,1)S(1)}, bf16[2080,128]{1,0:T(8,128)(2,1)S(1)}, u32[]{:S(2)}, u32[]{:S(2)}) collective-permute-start(bf16[2080,128]{1,0:T(8,128)(2,1)S(1)} %collective-permute-done.7.refs_3_), channel_id=1, source_target_pairs={{0,112},{16,0},{32,16},{48,32},{64,48},{80,64},{96,80},{112,96},{1... | collective-permute-start | bytes 1597448 | tf_op jit(solution)/shard_map/ppermute | solution.py:334
  44.4 35.6 %collective-permute-start.5 = (bf16[2080,128]{1,0:T(8,128)(2,1)S(1)}, bf16[2080,128]{1,0:T(8,128)(2,1)S(1)}, u32[]{:S(2)}, u32[]{:S(2)}) collective-permute-start(bf16[2080,128]{1,0:T(8,128)(2,1)S(1)} %collective-permute-done.4.refs_2_), channel_id=1, source_target_pairs={{0,16},{16,32},{32,48},{48,64},{64,80},{80,96},{96,112},{112,0},{1... | collective-permute-start | bytes 1597448 | tf_op jit(solution)/shard_map/ppermute | solution.py:333
  47.2 14.9 %collective-permute-start.9 = (bf16[2080,128]{1,0:T(8,128)(2,1)S(1)}, bf16[2080,128]{1,0:T(8,128)(2,1)S(1)}, u32[]{:S(2)}, u32[]{:S(2)}) collective-permute-start(bf16[2080,128]{1,0:T(8,128)(2,1)S(1)} %collective-permute-done.8.refs_3_), channel_id=1, source_target_pairs={{0,112},{16,0},{32,16},{48,32},{64,48},{80,64},{96,80},{112,96},{1... | collective-permute-start | bytes 1597448 | tf_op jit(solution)/shard_map/ppermute | solution.py:334
  62.1 45.5 %collective-permute-start.10 = (bf16[1040,128]{1,0:T(8,128)(2,1)S(1)}, bf16[1040,128]{1,0:T(8,128)(2,1)S(1)}, u32[]{:S(2)}, u32[]{:S(2)}) collective-permute-start(bf16[1040,128]{1,0:T(8,128)(2,1)S(1)} %slice.9), channel_id=1, source_target_pairs={{0,112},{16,0},{32,16},{48,32},{64,48},{80,64},{96,80},{112,96},{1... | collective-permute-start | bytes 798728 | tf_op jit(solution)/shard_map/ppermute | solution.py:336
  80.1 27.6 %collective-permute-start.6 = (bf16[1040,128]{1,0:T(8,128)(2,1)S(1)}, bf16[1040,128]{1,0:T(8,128)(2,1)S(1)}, u32[]{:S(2)}, u32[]{:S(2)}) collective-permute-start(bf16[1040,128]{1,0:T(8,128)(2,1)S(1)} %slice.8), channel_id=1, source_target_pairs={{0,16},{16,32},{32,48},{48,64},{64,80},{80,96},{96,112},{112,0},{1... | collective-permute-start | bytes 798728 | tf_op jit(solution)/shard_map/ppermute | solution.py:335
  110.6 30.0 %collective-permute-start.12 = (f32[4,2,136,256]{3,2,1,0:T(8,128)S(1)}, f32[4,2,136,256]{3,2,1,0:T(8,128)S(1)}, u32[]{:S(2)}, u32[]{:S(2)}) collective-permute-start(f32[4,2,136,256]{3,2,1,0:T(8,128)S(1)} %ring.9), channel_id=1, source_target_pairs={{0,1},{1,0},{2,3},{3,2},{4,5},{5,4},{6,7},{7,6},{8,9},{9,8},{10,11... | collective-permute-start | bytes 3342344 | tf_op jit(solution)/shard_map/ppermute | solution.py:344
  141.4 6.9 %collective-permute-start.13 = (bf16[64,1024]{1,0:T(8,128)(2,1)S(1)}, bf16[64,1024]{1,0:T(8,128)(2,1)S(1)}, u32[]{:S(2)}, u32[]{:S(2)}) collective-permute-start(bf16[64,1024]{1,0:T(8,128)(2,1)S(1)} %get-tuple-element.34), channel_id=1, source_target_pairs={{0,8},{8,128},{128,136},{136,0},{1,9},{9,129},{129,137},{137,1},{2... | collective-permute-start | bytes 393224 | tf_op jit(solution)/shard_map/ppermute | solution.py:317
  144.4 6.7 %collective-permute-start.14 = (bf16[64,1024]{1,0:T(8,128)(2,1)S(1)}, bf16[64,1024]{1,0:T(8,128)(2,1)S(1)}, u32[]{:S(2)}, u32[]{:S(2)}) collective-permute-start(bf16[64,1024]{1,0:T(8,128)(2,1)S(1)} %get-tuple-element.35), channel_id=1, source_target_pairs={{0,128},{8,136},{128,0},{136,8},{1,129},{9,137},{129,1},{137,9},{2... | collective-permute-start | bytes 393224 | tf_op jit(solution)/shard_map/ppermute | solution.py:317
  144.5 7.1 %collective-permute-start.15 = (bf16[64,1024]{1,0:T(8,128)(2,1)S(1)}, bf16[64,1024]{1,0:T(8,128)(2,1)S(1)}, u32[]{:S(2)}, u32[]{:S(2)}) collective-permute-start(bf16[64,1024]{1,0:T(8,128)(2,1)S(1)} %get-tuple-element.36), channel_id=1, source_target_pairs={{0,136},{8,0},{128,8},{136,128},{1,137},{9,1},{129,9},{137,129},{2... | collective-permute-start | bytes 393224 | tf_op jit(solution)/shard_map/ppermute | solution.py:317
